TPU v7x, 8 devices: a whole 2x2x1 slice. The times are simulated.
8 devices in a mesh: depth: 2 (over z, y), col: 2 (over x), row: 2 (over core).
Axes of the slice: x: 2, y: 2, z: 1, core: 2. Of those that a mesh axis runs over, the one named last changes fastest.
Arguments:
- x: bfloat16 [96, 256, 4096], P(('depth', 'row'), None, 'col')
- ln_g: float32 [4096], P('col')
- ln_b: float32 [4096], P('col')
- w_qkv: bfloat16 [4096, 12288], P('row', 'col')
- b_qkv: float32 [96, 128], P('col')
- w_o: bfloat16 [4096, 4096], P('row', 'col')
- b_o: float32 [4096], P('col')
- d_y: bfloat16 [96, 256, 4096], P(('depth', 'row'), None, 'col')
Outputs:
- output 1: bfloat16 [96, 256, 4096], P(('depth', 'row'), None, 'col')
- output 2: bfloat16 [96, 256, 4096], P(('depth', 'row'), None, 'col')
- output 3: bfloat16 [4096, 12288], P('row', 'col')
- output 4: float32 [96, 128], P('col')
- output 5: bfloat16 [4096, 4096], P('row', 'col')
- output 6: float32 [4096], P('col')
- output 7: float32 [4096], P('col')
- output 8: float32 [4096], P('col')
All inputs are finite; a program needn't handle non-finite values.
Results may differ from a plain program's by a relative error of at most 0.0135278.
Values are sent between devices in bfloat16 or wider.
A program may use at most 1 GiB of HBM per device.

v0:
```python
import jax
import jax.numpy as jnp
from jax import lax
from jax.sharding import PartitionSpec as P

LN_EPS = 1e-5


def solution(mesh):
    num_cols = mesh.shape["col"]
    act_spec = P(("depth", "row"), None, "col")
    mat_spec = P("row", "col")
    vec_spec = P("col")
    bias_spec = P("col", None)
    data_axes = ("depth", "row")

    def local_block(x, ln_g, ln_b, w_qkv, b_qkv, w_o, b_o, d_y):
        num_seq, seq_len, col_width = x.shape
        hidden = col_width * num_cols
        head_dim = b_qkv.shape[1]
        heads_loc = b_qkv.shape[0] // 3
        att_scale = head_dim ** -0.5
        positions = jnp.arange(seq_len)
        causal = positions[:, None] >= positions[None, :]

        x_f = x.astype(jnp.float32)
        row_mean = lax.psum(jnp.sum(x_f, axis=-1, keepdims=True), "col") / hidden
        centred = x_f - row_mean
        row_var = lax.psum(jnp.sum(centred * centred, axis=-1, keepdims=True), "col") / hidden
        inv_std = lax.rsqrt(row_var + LN_EPS)
        x_hat = centred * inv_std
        x_norm = (x_hat * ln_g + ln_b).astype(jnp.bfloat16)

        xn_full = lax.all_gather(x_norm, "col", axis=2, tiled=True)
        wqkv_rows = lax.all_gather(w_qkv, "row", axis=0, tiled=True)
        qkv_vals = jnp.einsum("bsh,hn->bsn", xn_full, wqkv_rows, preferred_element_type=jnp.float32)
        qkv_vals = (qkv_vals + b_qkv.reshape(-1)).astype(jnp.bfloat16)
        qkv_vals = qkv_vals.reshape(num_seq, seq_len, 3, heads_loc, head_dim)
        q_rows = qkv_vals[:, :, 0]
        k_rows = qkv_vals[:, :, 1]
        v_rows = qkv_vals[:, :, 2]
        scores = jnp.einsum("bqnd,bknd->bnqk", q_rows, k_rows, preferred_element_type=jnp.float32) * att_scale
        scores = jnp.where(causal, scores, -1e30)
        prob_f = jax.nn.softmax(scores, axis=-1)
        prob_b = prob_f.astype(jnp.bfloat16)
        att_vals = jnp.einsum("bnqk,bknd->bqnd", prob_b, v_rows, preferred_element_type=jnp.float32)
        att_vals = att_vals.astype(jnp.bfloat16).reshape(num_seq, seq_len, col_width)
        att_full = lax.all_gather(att_vals, "col", axis=2, tiled=True)
        wo_rows = lax.all_gather(w_o, "row", axis=0, tiled=True)
        out_proj = jnp.einsum("bsh,hn->bsn", att_full, wo_rows, preferred_element_type=jnp.float32)
        y_out = (x_f + out_proj + b_o).astype(jnp.bfloat16)

        db_o = lax.psum(jnp.sum(d_y.astype(jnp.float32), axis=(0, 1)), data_axes)
        att_back = lax.all_gather(att_vals, "col", axis=2, tiled=True)
        wo_back = lax.all_gather(w_o, "row", axis=0, tiled=True)
        dwo_part = jnp.einsum("bsh,bsn->hn", att_back, d_y, preferred_element_type=jnp.float32)
        dw_o = lax.psum_scatter(dwo_part.astype(jnp.bfloat16), "row", scatter_dimension=0, tiled=True)
        dw_o = lax.psum(dw_o, "depth")
        datt_part = jnp.einsum("bsn,hn->bsh", d_y, wo_back, preferred_element_type=jnp.float32)
        d_att = lax.psum_scatter(datt_part.astype(jnp.bfloat16), "col", scatter_dimension=2, tiled=True)
        d_att = d_att.reshape(num_seq, seq_len, heads_loc, head_dim)

        d_v = jnp.einsum("bnqk,bqnd->bknd", prob_b, d_att, preferred_element_type=jnp.float32)
        d_prob = jnp.einsum("bqnd,bknd->bnqk", d_att, v_rows, preferred_element_type=jnp.float32)
        row_dot = jnp.sum(d_prob * prob_f, axis=-1, keepdims=True)
        d_scores = (prob_f * (d_prob - row_dot) * att_scale).astype(jnp.bfloat16)
        d_q = jnp.einsum("bnqk,bknd->bqnd", d_scores, k_rows, preferred_element_type=jnp.float32)
        d_k = jnp.einsum("bnqk,bqnd->bknd", d_scores, q_rows, preferred_element_type=jnp.float32)
        dqkv_f = jnp.stack([d_q, d_k, d_v], axis=2)
        db_qkv = lax.psum(jnp.sum(dqkv_f, axis=(0, 1)).reshape(3 * heads_loc, head_dim), data_axes)
        d_qkv = dqkv_f.astype(jnp.bfloat16).reshape(num_seq, seq_len, 3 * col_width)

        xn_back = lax.all_gather(x_norm, "col", axis=2, tiled=True)
        wqkv_back = lax.all_gather(w_qkv, "row", axis=0, tiled=True)
        dwqkv_part = jnp.einsum("bsh,bsn->hn", xn_back, d_qkv, preferred_element_type=jnp.float32)
        dw_qkv = lax.psum_scatter(dwqkv_part.astype(jnp.bfloat16), "row", scatter_dimension=0, tiled=True)
        dw_qkv = lax.psum(dw_qkv, "depth")
        dxn_part = jnp.einsum("bsn,hn->bsh", d_qkv, wqkv_back, preferred_element_type=jnp.float32)
        d_xn = lax.psum_scatter(dxn_part.astype(jnp.bfloat16), "col", scatter_dimension=2, tiled=True)
        d_xn = d_xn.astype(jnp.float32)

        dln_g = lax.psum(jnp.sum(d_xn * x_hat, axis=(0, 1)), data_axes)
        dln_b = lax.psum(jnp.sum(d_xn, axis=(0, 1)), data_axes)
        d_hat = d_xn * ln_g
        ln_stats = jnp.concatenate([jnp.sum(d_hat, axis=-1, keepdims=True), jnp.sum(d_hat * x_hat, axis=-1, keepdims=True)], axis=-1)
        ln_stats = lax.psum(ln_stats, "col") / hidden
        d_x = d_y.astype(jnp.float32) + inv_std * (d_hat - ln_stats[..., :1] - x_hat * ln_stats[..., 1:])
        return (y_out, d_x.astype(jnp.bfloat16), dw_qkv, db_qkv, dw_o, db_o, dln_g, dln_b)

    return jax.shard_map(local_block, mesh=mesh, in_specs=(act_spec, vec_spec, vec_spec, mat_spec, bias_spec, mat_spec, vec_spec, act_spec), out_specs=(act_spec, act_spec, mat_spec, bias_spec, mat_spec, vec_spec, vec_spec, vec_spec), check_vma=False)
```

profile of v0, /device:TPU:0, one launch (start us, length us, event | category | flops | bytes accessed | tf_op | source)
XLA Modules:
  0.0 5084.2 jit_solution(502323570644850918)
XLA Ops:
  7.2 0.0 copy-start.4
  7.2 0.0 all-gather.5.cloned.1.call-start
  7.2 9.8 convert_reduce_fusion.1
  17.0 10.3 psum.63
  27.3 11.2 fusion.19
  38.5 6.8 psum.64
  45.4 0.0 copy-start.2
  45.4 0.6 copy-done.2
  46.0 0.0 copy-done.7
  46.0 24.4 fusion.16
  70.4 0.0 all-gather.5.cloned.1.call-update
  70.4 0.0 all-gather.7.cloned.1.call-start
  70.4 0.7 all-gather.7.cloned.1.call-update
  71.1 0.0 all-gather.11.cloned.1.call-start
  71.2 0.7 all-gather.11.cloned.1.call-update
  71.9 0.2 all-gather.9.cloned.1.call-start
  72.1 0.7 iota_compare_fusion
  72.8 573.5 %all-gather.5.cloned.1.call-done = bf16[24,256,4096]{2,1,0:T(8,128)(2,1)} async-done(((bf16[24,256,2048]{2,1,0:T(8,128)(2,1)}), bf16[24,256,4096]{2,1,0:T(8,128)(2,1)}) %all-gather.5.cloned.1.call-update) | async-done | bytes 50331664 | tf_op jit(solution)/shard_map/all_gather | solution.py:34
  646.2 70.7 %all-gather.7.cloned.1.call-done = bf16[4096,6144]{1,0:T(8,128)(2,1)} async-done(((bf16[2048,6144]{1,0:T(8,128)(2,1)}), bf16[4096,6144]{1,0:T(8,128)(2,1)}) %all-gather.7.cloned.1.call-update) | async-done | bytes 50331664 | tf_op jit(solution)/shard_map/all_gather | solution.py:35
  716.9 327.3 %add_convert_fusion = bf16[24,256,6144]{2,1,0:T(8,128)(2,1)} fusion(f32[6144]{0:T(1024)S(1)} %bitcast.94, bf16[24,256,4096]{2,1,0:T(8,128)(2,1)} %all-gather.5.cloned.1.call-done, bf16[4096,6144]{1,0:T(8,128)(2,1)} %all-gather.7.cloned.1.call-done), kind=kOutput, calls=%fused_computation.3 | convolution fusion | flops 309313142784 | bytes 176185344 | tf_op jit(solution)/shard_map/bsh,hn->bsn/dot_general | solution.py:36
  1044.2 49.4 copy.82
  1093.6 49.8 fusion.73
  1143.4 32.0 copy.78
  1175.4 58.1 %fusion.50 = f32[24,16,256,256]{2,3,1,0:T(8,128)} fusion(bf16[24,256,1,16,128]{4,3,2,1,0:T(8,128)(2,1)} %get-tuple-element.20, bf16[24,256,1,16,128]{4,3,2,1,0:T(8,128)(2,1)} %get-tuple-element.18), kind=kOutput, calls=%fused_computation.60 | convolution fusion | flops 6442450944 | bytes 150994944 | tf_op jit(solution)/shard_map/bqnd,bknd->bnqk/dot_general | solution.py:42
  1233.5 96.2 %fusion.74 = (f32[24,16,256]{2,1,0:T(8,128)S(1)}, f32[24,16,256,256]{2,3,1,0:T(8,128)}) fusion(f32[24,16,256,256]{2,3,1,0:T(8,128)} %fusion.50, pred[256,256]{0,1:T(8,128)(4,1)S(1)} %copy-done.6), kind=kOutput, calls=%fused_computation.81 | output fusion | flops 150995200 | bytes 201785344 | tf_op jit(solution)/shard_map/sub | solution.py:44
  1329.6 48.4 fusion.62
  1378.1 32.3 copy.53
  1410.3 0.0 all-gather.9.cloned.1.call-update
  1410.4 0.0 reduce-scatter.8.cloned.1.call-start
  1410.4 0.0 all-gather.11.cloned.1.call-done
  1410.4 113.5 %convolution_convert_fusion = bf16[24,256,4096]{2,1,0:T(8,128)(2,1)} fusion(bf16[24,256,2048]{2,1,0:T(8,128)(2,1)} %param.15, bf16[4096,2048]{1,0:T(8,128)(2,1)} %all-gather.11.cloned.1.call-done), kind=kOutput, calls=%fused_computation.49 | convolution fusion | flops 103104380928 | bytes 92274688 | tf_op jit(solution)/shard_map/bsn,hn->bsh/dot_general | solution.py:59
  1524.0 0.0 reduce-scatter.8.cloned.1.call-update
  1524.0 0.0 reduce-scatter.12.cloned.1.call-start
  1524.0 462.0 %all-gather.9.cloned.1.call-done = bf16[24,256,4096]{2,1,0:T(8,128)(2,1)} async-done(((bf16[24,256,2048]{2,1,0:T(8,128)(2,1)}), bf16[24,256,4096]{2,1,0:T(8,128)(2,1)}) %all-gather.9.cloned.1.call-update) | async-done | bytes 50331664 | tf_op jit(solution)/shard_map/all_gather | solution.py:48
  1986.0 118.3 %bitcast_convert_fusion.1 = bf16[4096,2048]{1,0:T(8,128)(2,1)} fusion(bf16[24,256,4096]{2,1,0:T(8,128)(2,1)} %all-gather.9.cloned.1.call-done, bf16[24,256,2048]{2,1,0:T(8,128)(2,1)} %param.15), kind=kOutput, calls=%fused_computation.48 | convolution fusion | flops 103087603712 | bytes 92274688 | tf_op jit(solution)/shard_map/bsh,bsn->hn/dot_general | solution.py:56
  2104.3 0.0 reduce-scatter.12.cloned.1.call-update
  2104.3 0.0 reduce-scatter.14.cloned.1.call-start
  2104.4 429.9 %reduce-scatter.8.cloned.1.call-done = bf16[24,256,2048]{2,1,0:T(8,128)(2,1)} async-done(((bf16[24,256,4096]{2,1,0:T(8,128)(2,1)}), bf16[24,256,2048]{2,1,0:T(8,128)(2,1)}) %reduce-scatter.8.cloned.1.call-update) | async-done | bytes 25165840 | tf_op jit(solution)/shard_map/reduce_scatter | solution.py:60
  2534.3 32.7 copy.81
  2567.0 50.7 fusion.43
  2617.7 145.3 %fusion.54 = f32[24,256,1,16,128]{1,4,3,0,2:T(8,128)} fusion(f32[24,16,256,256]{2,3,1,0:T(8,128)} %fusion.43, bf16[24,256,1,16,128]{4,3,2,1,0:T(8,128)(2,1)} %get-tuple-element.18, f32[24,16,256,256]{2,3,1,0:T(8,128)} %get-tuple-element.26, f32[24,16,256]{2,1,0:T(8,128)S(1)} %copy-done.11), kind=kOutput, calls=%fused_computation.62 | convolution fusion | flops 6618710016 | bytes 277217280 | tf_op jit(solution)/shard_map/bnqk,bknd->bqnd/dot_general | solution.py:67
  2763.0 145.1 %fusion.57 = f32[24,256,1,16,128]{1,4,3,0,2:T(8,128)} fusion(f32[24,16,256,256]{2,3,1,0:T(8,128)} %fusion.43, bf16[24,256,1,16,128]{4,3,2,1,0:T(8,128)(2,1)} %get-tuple-element.20, f32[24,16,256,256]{2,3,1,0:T(8,128)} %get-tuple-element.26, f32[24,16,256]{2,1,0:T(8,128)S(1)} %copy-done.11), kind=kOutput, calls=%fused_computation.63 | convolution fusion | flops 6618710016 | bytes 277217280 | tf_op jit(solution)/shard_map/bnqk,bqnd->bknd/dot_general | solution.py:68
  2908.2 57.6 %fusion.51 = f32[24,256,1,16,128]{1,4,3,0,2:T(8,128)} fusion(bf16[24,256,16,128]{1,3,2,0:T(8,128)(2,1)} %bitcast.87, f32[24,16,256,256]{2,3,1,0:T(8,128)} %get-tuple-element.26, f32[24,16,256]{2,1,0:T(8,128)S(1)} %copy-done.11), kind=kOutput, calls=%fused_computation.61 | convolution fusion | flops 6492782592 | bytes 176553984 | tf_op jit(solution)/shard_map/bnqk,bqnd->bknd/dot_general | solution.py:63
  2965.7 71.8 %fusion.3 = bf16[24,256,3,16,128]{1,4,3,0,2:T(8,128)(2,1)} fusion(f32[24,256,1,16,128]{1,4,3,0,2:T(8,128)} %fusion.51, f32[24,256,1,16,128]{1,4,3,0,2:T(8,128)} %fusion.57, f32[24,256,1,16,128]{1,4,3,0,2:T(8,128)} %fusion.54), kind=kLoop, calls=%fused_computation.5 | loop fusion | flops 75497472 | bytes 226492416 | tf_op jit(solution)/shard_map/convert_element_type | solution.py:71
  3037.5 49.2 copy.62
  3086.7 341.8 %bitcast_convert_fusion = bf16[4096,6144]{1,0:T(8,128)(2,1)} fusion(bf16[24,256,4096]{2,1,0:T(8,128)(2,1)} %all-gather.5.cloned.1.call-done, bf16[24,256,6144]{1,2,0:T(8,128)(2,1)} %bitcast.18), kind=kOutput, calls=%fused_computation.6 | convolution fusion | flops 309262811136 | bytes 176160768 | tf_op jit(solution)/shard_map/bsh,bsn->hn/dot_general | solution.py:75
  3428.5 0.0 reduce-scatter.14.cloned.1.call-update
  3428.5 0.0 reduce-scatter.10.cloned.1.call-start
  3428.6 337.9 %fusion.40 = bf16[24,256,4096]{2,1,0:T(8,128)(2,1)} fusion(bf16[24,256,6144]{1,2,0:T(8,128)(2,1)} %bitcast.18, bf16[4096,6144]{1,0:T(8,128)(2,1)} %all-gather.7.cloned.1.call-done), kind=kOutput, calls=%fused_computation.50 | convolution fusion | flops 309262811136 | bytes 176160768 | tf_op jit(solution)/shard_map/bsn,hn->bsh/dot_general | solution.py:78
  3766.5 0.0 reduce-scatter.10.cloned.1.call-update
  3766.5 0.0 all-reduce.5.cloned.1.call-start
  3766.5 0.0 reduce-scatter.12.cloned.1.call-done
  3766.6 0.0 reduce-scatter.14.cloned.1.call-done
  3766.6 0.6 all-reduce.5.cloned.1.call-update
  3767.2 115.6 %fusion.23 = bf16[24,256,2048]{2,1,0:T(8,128)(2,1)} fusion(bf16[24,256,2048]{2,1,0:T(8,128)(2,1)} %param.8, f32[2048]{0:T(1024)S(1)} %copy-done.9, bf16[24,256,4096]{2,1,0:T(8,128)(2,1)} %all-gather.9.cloned.1.call-done, bf16[4096,2048]{1,0:T(8,128)(2,1)} %all-gather.11.cloned.1.call-done), kind=kOutput, calls=%fused_computation.36 | convolution fusion | flops 103129546752 | bytes 117448704 | tf_op jit(solution)/shard_map/bsh,hn->bsn/dot_general | solution.py:50
  3882.8 45.5 fusion.2
  3928.3 384.5 %reduce-scatter.10.cloned.1.call-done = bf16[24,256,2048]{2,1,0:T(8,128)(2,1)} async-done(((bf16[24,256,4096]{2,1,0:T(8,128)(2,1)}), bf16[24,256,2048]{2,1,0:T(8,128)(2,1)}) %reduce-scatter.10.cloned.1.call-update) | async-done | bytes 25165840 | tf_op jit(solution)/shard_map/reduce_scatter | solution.py:79
  4312.8 27.5 fusion.24
  4340.4 7.5 psum.65
  4347.9 34.3 convert_reduce_fusion.2
  4382.1 12.9 all-reduce.1
  4395.0 653.0 %all-reduce.5.cloned.1.call-done = (bf16[2048,6144]{1,0:T(8,128)(2,1)}, bf16[2048,2048]{1,0:T(8,128)(2,1)}) async-done(((bf16[2048,6144]{1,0:T(8,128)(2,1)}, bf16[2048,2048]{1,0:T(8,128)(2,1)}), (bf16[2048,6144]{1,0:T(8,128)(2,1)}, bf16[2048,2048]{1,0:T(8,128)(2,1)})) %all-reduce.5.cloned.1.call-update) | async-done | bytes 33554448 | tf_op jit(solution)/shard_map/psum | solution.py:77
  5048.0 21.0 copy.95
  5069.0 8.4 copy.96
  (25 shorter events, 0.1 us)
Async XLA Ops:
  7.2 38.8 copy-start.7
  7.2 38.8 copy-start.4
  7.2 639.0 %all-gather.5.cloned.1.call-start = ((), (), s32[]{:S(2)}) async-start(), calls=%async_computation.4 | async-start | bytes 75497472 | tf_op jit(solution)/shard_map/all_gather | solution.py:34
  27.3 43.1 copy-start
  45.4 0.6 copy-start.2
  46.0 670.9 %copy-start.8 = (f32[48,128]{1,0:T(8,128)S(1)}, f32[48,128]{1,0:T(8,128)}, u32[]{:S(2)}) copy-start(f32[48,128]{1,0:T(8,128)} %param.12) | copy-start | bytes 73732
  70.4 646.5 %all-gather.7.cloned.1.call-start = ((), (), s32[]{:S(2)}) async-start(), calls=%async_computation.5 | async-start | bytes 75497472 | tf_op jit(solution)/shard_map/all_gather | solution.py:35
  71.1 1339.3 %all-gather.11.cloned.1.call-start = ((), (), s32[]{:S(2)}) async-start(), calls=%async_computation.7 | async-start | bytes 25165824 | tf_op jit(solution)/shard_map/all_gather | solution.py:49
  71.9 1914.2 %all-gather.9.cloned.1.call-start = ((), (), s32[]{:S(2)}) async-start(), calls=%async_computation.6 | async-start | bytes 75497472 | tf_op jit(solution)/shard_map/all_gather | solution.py:48
  1175.4 58.1 %copy-start.6 = (pred[256,256]{0,1:T(8,128)(4,1)S(1)}, pred[256,256]{0,1:T(8,128)(4,1)}, u32[]{:S(2)}) copy-start(pred[256,256]{0,1:T(8,128)(4,1)} %iota_compare_fusion) | copy-start | bytes 196612
  1329.6 48.4 copy-start.10
  1410.4 1123.9 %reduce-scatter.8.cloned.1.call-start = ((), (), s32[]{:S(2)}) async-start(), calls=%async_computation.8 | async-start | bytes 75497472 | tf_op jit(solution)/shard_map/reduce_scatter | solution.py:60
  1524.0 2242.6 %reduce-scatter.12.cloned.1.call-start = ((), (), s32[]{:S(2)}) async-start(), calls=%async_computation.10 | async-start | bytes 25165824 | tf_op jit(solution)/shard_map/reduce_scatter | solution.py:57
  2104.3 1662.3 %reduce-scatter.14.cloned.1.call-start = ((), (), s32[]{:S(2)}) async-start(), calls=%async_computation.11 | async-start | bytes 75497472
  2567.0 50.7 copy-start.11
  3428.5 884.3 %reduce-scatter.10.cloned.1.call-start = ((), (), s32[]{:S(2)}) async-start(), calls=%async_computation.9 | async-start | bytes 75497472 | tf_op jit(solution)/shard_map/reduce_scatter | solution.py:79
  3766.5 0.8 copy-start.9
  3766.5 1281.5 %all-reduce.5.cloned.1.call-start = ((), (), s32[]{:S(2)}) async-start(), calls=%async_computation.12 | async-start | bytes 67108864 | tf_op jit(solution)/shard_map/psum | solution.py:77
  3882.8 430.0 %copy-start.1 = (f32[24,256]{1,0:T(8,128)S(1)}, f32[24,256]{1,0:T(8,128)}, u32[]{:S(2)}) copy-start(f32[24,256]{1,0:T(8,128)} %copy-done) | copy-start | bytes 73732
  3882.8 430.0 %copy-start.3 = (f32[24,256]{1,0:T(8,128)S(1)}, f32[24,256]{1,0:T(8,128)}, u32[]{:S(2)}) copy-start(f32[24,256]{1,0:T(8,128)} %copy-done.2) | copy-start | bytes 73732
  3882.8 430.0 %copy-start.5 = (f32[2048]{0:T(1024)S(1)}, f32[2048]{0:T(1024)}, u32[]{:S(2)}) copy-start(f32[2048]{0:T(1024)} %param.9) | copy-start | bytes 24580
Sparse Core Ops, SparseCore 0:
  70.5 575.6 all-gather.4
  647.7 69.1 all-gather.6
  718.4 28.9 all-gather.10
  1410.5 575.4 all-gather.8
  1988.1 546.1 reduce-scatter.7
  2536.4 21.8 reduce-scatter.11
  3428.6 49.1 reduce-scatter.13
  3766.6 546.1 reduce-scatter.9
  4315.4 732.5 all-reduce.4
where the time goes:
time: 5090 us; the launch traced here: 5080 us
  waiting for transfers between devices  2580 us (51%)
  matrix products  1860 us (37%)
  other arithmetic  321 us (6%)
  local copies, waits for them, and re-layouts  276 us (5%)
    psum x1, waiting for transfers between devices, local_block(): dw_qkv = lax.psum(dw_qkv, 'depth')  653 us
    all_gather x1, waiting for transfers between devices, local_block(): xn_full = lax.all_gather(x_norm, 'col', axis=2, tiled=True)  573 us
    all_gather x1, waiting for transfers between devices, local_block(): att_full = lax.all_gather(att_vals, 'col', axis=2, tiled=True)  462 us
    reduce_scatter x1, waiting for transfers between devices, local_block(): lax.psum_scatter(datt_part.astype(jnp.bfloat16), 'col', scatter_dimension...  430 us
    reduce_scatter x1, waiting for transfers between devices, local_block(): lax.psum_scatter(dxn_part.astype(jnp.bfloat16), 'col', scatter_dimension=...  385 us
    dot_general x1, matrix products, local_block(): jnp.einsum('bsh,bsn->hn', xn_back, d_qkv, preferred_element_type=jnp.floa...  342 us
    dot_general x1, matrix products, local_block(): jnp.einsum('bsn,hn->bsh', d_qkv, wqkv_back, preferred_element_type=jnp.fl...  338 us
    dot_general x1, matrix products, local_block(): jnp.einsum('bsh,hn->bsn', xn_full, wqkv_rows, preferred_element_type=jnp....  327 us
  transfers between devices with their start and end apart: 9, of which 6 were waited for; matrix products, arithmetic and copies ran while one was open for 47% of the time, Pallas kernels for 0%

commit v1 on v0

v1 whole, which is shorter than its diff:
```python
import functools

import jax
import jax.numpy as jnp
from jax import lax
from jax.experimental import pallas as pl
from jax.experimental.pallas import tpu as pltpu
from jax.sharding import PartitionSpec as P


LN_EPS = 1e-5
SWAP = [(0, 1), (1, 0)]
F32 = jnp.float32
BF16 = jnp.bfloat16
LOG2E = 1.4426950408889634


def nt_dot(lhs, rhs):
    return lax.dot_general(lhs, rhs, (((1,), (1,)), ((), ())), preferred_element_type=F32)


def tn_dot(lhs, rhs):
    return lax.dot_general(lhs, rhs, (((0,), (0,)), ((), ())), preferred_element_type=F32)


def nn_dot(lhs, rhs):
    return lax.dot_general(lhs, rhs, (((1,), (0,)), ((), ())), preferred_element_type=F32)


def row_sum(val):
    return jnp.sum(val, -1, keepdims=True)


def group_rows(i, unroll, step):
    return [pl.ds(pl.multiple_of((i * unroll + u) * step, step), step) for u in range(unroll)]


def ln_fwd_body(col_ref, own_ref, recv_ref, g_ref, b_ref, *rest):
    xn_ref = rest[-1]
    width = own_ref.shape[1]
    inv_n = 1.0 / (2 * width)
    col = col_ref[0]
    own_cols = pl.ds(pl.multiple_of(col * width, width), width)
    far_cols = pl.ds(pl.multiple_of((1 - col) * width, width), width)
    step, unroll = 16, 4

    @pl.loop(0, own_ref.shape[0] // (step * unroll))
    def _(i):
        groups = group_rows(i, unroll, step)
        means = [row_sum(own_ref[r, :].astype(F32) + recv_ref[r, :].astype(F32)) * inv_n for r in groups]
        invs = []
        for r, mean in zip(groups, means):
            own = own_ref[r, :].astype(F32) - mean
            far = recv_ref[r, :].astype(F32) - mean
            invs.append(lax.rsqrt(row_sum(own * own + far * far) * inv_n + LN_EPS))
        for r, mean, inv in zip(groups, means, invs):
            for src, cols in ((own_ref, own_cols), (recv_ref, far_cols)):
                hat = (src[r, :].astype(F32) - mean) * inv
                xn_ref[r, cols] = (hat * g_ref[:, cols] + b_ref[:, cols]).astype(BF16)


def ln_fwd(col, x_loc, x_recv, g_full, b_full, row0, total, prev):
    rows, width = x_recv.shape
    blk = 256
    nall = total // blk
    off = row0 // blk
    in_specs = [
        pl.BlockSpec((blk, width), lambda i, c: (i + off + c[0] * nall, 0)),
        pl.BlockSpec((blk, width), lambda i, c: (i, 0)),
        pl.BlockSpec((1, 2 * width), lambda i, c: (0, 0)),
        pl.BlockSpec((1, 2 * width), lambda i, c: (0, 0)),
    ]
    args = [col, x_loc, x_recv, g_full, b_full]
    aliases = {}
    if prev is not None:
        in_specs.append(pl.BlockSpec(memory_space=pl.ANY))
        args.append(prev)
        aliases = {5: 0}
    return pl.pallas_call(
        ln_fwd_body,
        out_shape=jax.ShapeDtypeStruct((total, 2 * width), BF16),
        grid_spec=pltpu.PrefetchScalarGridSpec(
            num_scalar_prefetch=1,
            grid=(rows // blk,),
            in_specs=in_specs,
            out_specs=pl.BlockSpec((blk, 2 * width), lambda i, c: (i + off, 0)),
        ),
        input_output_aliases=aliases,
        cost_estimate=pl.CostEstimate(flops=20 * rows * 2 * width, bytes_accessed=8 * rows * width, transcendentals=0),
        name="ln_fwd",
    )(*args)


def ln_bwd_body(col_ref, dxn_ref, own_ref, recv_ref, dy_own_ref, dy_recv_ref, g_ref, *rest):
    dx_own_ref, dx_send_ref, dg_ref, db_ref = rest[-4:]
    width = own_ref.shape[1]
    inv_n = 1.0 / (2 * width)
    col = col_ref[0]
    own_cols = pl.ds(pl.multiple_of(col * width, width), width)
    far_cols = pl.ds(pl.multiple_of((1 - col) * width, width), width)
    step, unroll = 16, 8

    @pl.when(pl.program_id(0) == 0)
    def _():
        dg_ref[...] = jnp.zeros_like(dg_ref)
        db_ref[...] = jnp.zeros_like(db_ref)

    def fold(val):
        return jnp.sum(val.reshape(val.shape[0] // 8, 8, val.shape[1]), axis=0)

    @pl.loop(0, own_ref.shape[0] // (step * unroll))
    def _(i):
        groups = group_rows(i, unroll, step)
        stats = []
        for r in groups:
            mean = row_sum(own_ref[r, :].astype(F32) + recv_ref[r, :].astype(F32)) * inv_n
            m1 = row_sum(dxn_ref[r, own_cols] * g_ref[:, own_cols] + dxn_ref[r, far_cols] * g_ref[:, far_cols]) * inv_n
            stats.append((mean, m1))
        full = []
        for r, (mean, m1) in zip(groups, stats):
            own = own_ref[r, :].astype(F32) - mean
            far = recv_ref[r, :].astype(F32) - mean
            var = row_sum(own * own + far * far) * inv_n
            m2 = row_sum(dxn_ref[r, own_cols] * g_ref[:, own_cols] * own + dxn_ref[r, far_cols] * g_ref[:, far_cols] * far) * inv_n
            inv = lax.rsqrt(var + LN_EPS)
            full.append((mean, inv, m1, m2 * inv))
        for src, dy, dx, cols in ((own_ref, dy_own_ref, dx_own_ref, own_cols), (recv_ref, dy_recv_ref, dx_send_ref, far_cols)):
            sum_g = sum_b = None
            for r, (mean, inv, m1, m2) in zip(groups, full):
                hat = (src[r, :].astype(F32) - mean) * inv
                d = dxn_ref[r, cols]
                add_g, add_b = fold(d * hat), fold(d)
                sum_g = add_g if sum_g is None else sum_g + add_g
                sum_b = add_b if sum_b is None else sum_b + add_b
                dx[r, :] = (dy[r, :].astype(F32) + inv * (d * g_ref[:, cols] - m1 - hat * m2)).astype(BF16)
            dg_ref[:, cols] += sum_g
            db_ref[:, cols] += sum_b


def ln_bwd(col, dxn, x_loc, x_recv, dy_loc, dy_recv, g_full, row0, total, dx_prev):
    rows, width = dxn.shape[0], dy_recv.shape[1]
    blk = 128
    nall = total // blk
    nblk = rows // blk
    off = row0 // blk
    own_spec = pl.BlockSpec((blk, width), lambda i, c: (i + off + c[0] * nall, 0))
    recv_spec = pl.BlockSpec((blk, width), lambda i, c: (i + off, 0))
    npiece = x_recv[0].shape[0] // blk
    x_specs = [pl.BlockSpec((blk, width), lambda i, c, p=p: (jnp.clip(i + off - p * npiece, 0, npiece - 1), 0)) for p in range(2)]
    in_specs = [
        pl.BlockSpec((blk, 2 * width), lambda i, c: (i, 0)),
        own_spec,
        *x_specs,
        own_spec,
        recv_spec,
        pl.BlockSpec((1, 2 * width), lambda i, c: (0, 0)),
    ]
    args = [col, dxn, x_loc, *x_recv, dy_loc, dy_recv, g_full]
    aliases = {}
    if dx_prev is not None:
        in_specs.append(pl.BlockSpec(memory_space=pl.ANY))
        args.append(dx_prev)
        aliases = {8: 0}

    def body(col_ref, dxn_ref, own_ref, x0_ref, x1_ref, *rest):
        late = pl.program_id(0) + off >= npiece

        @pl.when(jnp.logical_not(late))
        def _():
            ln_bwd_body(col_ref, dxn_ref, own_ref, x0_ref, *rest)

        @pl.when(late)
        def _():
            ln_bwd_body(col_ref, dxn_ref, own_ref, x1_ref, *rest)

    return pl.pallas_call(
        body,
        out_shape=(
            jax.ShapeDtypeStruct((2 * total, width), BF16),
            jax.ShapeDtypeStruct((rows, width), BF16),
            jax.ShapeDtypeStruct((8, 2 * width), F32),
            jax.ShapeDtypeStruct((8, 2 * width), F32),
        ),
        grid_spec=pltpu.PrefetchScalarGridSpec(
            num_scalar_prefetch=1,
            grid=(nblk,),
            in_specs=in_specs,
            out_specs=(
                own_spec,
                pl.BlockSpec((blk, width), lambda i, c: (i, 0)),
                pl.BlockSpec((8, 2 * width), lambda i, c: (0, 0)),
                pl.BlockSpec((8, 2 * width), lambda i, c: (0, 0)),
            ),
        ),
        input_output_aliases=aliases,
        cost_estimate=pl.CostEstimate(flops=40 * rows * 2 * width, bytes_accessed=20 * rows * width, transcendentals=0),
        name="ln_bwd",
    )(*args)


def attn_fwd_body(heads, scale, grp_ref, q_ref, k_ref, v_ref, *rest):
    out_ref = rest[-1]
    half = q_ref.shape[0] // 2
    causal = lax.broadcasted_iota(jnp.int32, (half, half), 0) >= lax.broadcasted_iota(jnp.int32, (half, half), 1)
    unroll = 8
    coef = scale * LOG2E

    @pl.loop(0, heads // unroll)
    def _(i):
        scores = []
        for j in range(unroll):
            cols = pl.ds(pl.multiple_of((i * unroll + j) * 128, 128), 128)
            k = k_ref[:, cols]
            scores.append((cols, nt_dot(q_ref[:half, cols], k[:half]), nt_dot(q_ref[half:, cols], k)))
        probs = []
        for cols, s0, s1 in scores:
            sa = jnp.where(causal, s0, -1e30)
            ea = jnp.exp2((sa - jnp.max(sa, -1, keepdims=True)) * coef)
            pa = (ea * (1.0 / row_sum(ea))).astype(BF16)
            sb, sc = s1[:, :half], jnp.where(causal, s1[:, half:], -1e30)
            top = jnp.max(jnp.maximum(sb, sc), -1, keepdims=True)
            eb, ec = jnp.exp2((sb - top) * coef), jnp.exp2((sc - top) * coef)
            inv = 1.0 / row_sum(eb + ec)
            probs.append((cols, pa, jnp.concatenate([(eb * inv).astype(BF16), (ec * inv).astype(BF16)], axis=1)))
        for cols, p0, p1 in probs:
            v = v_ref[:, cols]
            out_ref[:half, cols] = nn_dot(p0, v[:half]).astype(BF16)
            out_ref[half:, cols] = nn_dot(p1, v).astype(BF16)


def attn_fwd(grp, qkv, groups, width, seq, row0, total, prev):
    rows = qkv.shape[0]
    heads = width // 128
    off = row0 // seq
    in_specs = [pl.BlockSpec((seq, width), lambda g, i, c, j=j: (i, 3 * g + j)) for j in range(3)]
    args = [grp, qkv, qkv, qkv]
    aliases = {}
    if prev is not None:
        in_specs.append(pl.BlockSpec(memory_space=pl.ANY))
        args.append(prev)
        aliases = {4: 0}
    nheads = rows // seq * heads * groups
    return pl.pallas_call(
        functools.partial(attn_fwd_body, heads, 128 ** -0.5),
        out_shape=jax.ShapeDtypeStruct((total, 4096), BF16),
        grid_spec=pltpu.PrefetchScalarGridSpec(
            num_scalar_prefetch=1,
            grid=(groups, rows // seq),
            in_specs=in_specs,
            out_specs=pl.BlockSpec((seq, width), lambda g, i, c: (i + off, c[0] + g)),
        ),
        input_output_aliases=aliases,
        cost_estimate=pl.CostEstimate(flops=nheads * seq * seq * 128 * 8, bytes_accessed=8 * rows * width * groups, transcendentals=nheads * seq * seq),
        name="attn_fwd",
    )(*args)


def attn_bwd_body(heads, scale, grp_ref, q_ref, k_ref, v_ref, d_ref, *rest):
    dq_ref, sum_ref = rest[-2:]
    seq, width = q_ref.shape
    half = seq // 2
    causal = lax.broadcasted_iota(jnp.int32, (half, half), 1) >= lax.broadcasted_iota(jnp.int32, (half, half), 0)
    unroll = 8
    coef = scale * LOG2E

    @pl.when(pl.program_id(0) == 0)
    def _():
        sum_ref[...] = jnp.zeros_like(sum_ref)

    def col_sum(val):
        return jnp.sum(val, 0, keepdims=True)

    def emit(top, bottom, start):
        cols = pl.ds(pl.multiple_of(start, 128), 128)
        dq_ref[:half, cols] = top.astype(BF16)
        dq_ref[half:, cols] = bottom.astype(BF16)
        sum_ref[:, cols] += jnp.sum((top + bottom).reshape(half // 8, 8, 128), axis=0)

    @pl.loop(0, heads // unroll)
    def _(i):
        first = []
        for j in range(unroll):
            h = (i * unroll + j) * 128
            cols = pl.ds(pl.multiple_of(h, 128), 128)
            q, k, v, d = q_ref[:, cols], k_ref[:, cols], v_ref[:, cols], d_ref[:, cols]
            first.append((h, cols, nt_dot(k[:half], q), nt_dot(k[half:], q[half:]), nt_dot(v[:half], d), nt_dot(v[half:], d[half:])))
        second = []
        for h, cols, s0, s1, dp0, dpc in first:
            sa = jnp.where(causal, s0[:, :half], -1e30)
            ea = jnp.exp2((sa - jnp.max(sa, 0, keepdims=True)) * coef)
            pa = ea * (1.0 / col_sum(ea))
            dpa, dpb = dp0[:, :half], dp0[:, half:]
            dsa = (pa * (dpa - col_sum(dpa * pa)) * scale).astype(BF16)
            sb, sc = s0[:, half:], jnp.where(causal, s1, -1e30)
            top = jnp.max(jnp.maximum(sb, sc), 0, keepdims=True)
            eb, ec = jnp.exp2((sb - top) * coef), jnp.exp2((sc - top) * coef)
            inv = 1.0 / col_sum(eb + ec)
            pb, pc = eb * inv, ec * inv
            dot = col_sum(dpb * pb + dpc * pc)
            dsb = (pb * (dpb - dot) * scale).astype(BF16)
            dsc = (pc * (dpc - dot) * scale).astype(BF16)
            p0 = jnp.concatenate([pa.astype(BF16), pb.astype(BF16)], axis=1)
            second.append((h, cols, p0, pc.astype(BF16), dsa, dsb, dsc))
        for h, cols, p0, p1, dsa, dsb, dsc in second:
            q, k, d = q_ref[:, cols], k_ref[:, cols], d_ref[:, cols]
            emit(nn_dot(p0, d), nn_dot(p1, d[half:]), h + 2 * width)
            emit(nn_dot(jnp.concatenate([dsa, dsb], axis=1), q), nn_dot(dsc, q[half:]), h + width)
            emit(tn_dot(dsa, k[:half]), tn_dot(jnp.concatenate([dsb, dsc], axis=0), k), h)


def attn_bwd(grp, qkv, d_att, group, out_groups, width, seq, row0, total, prev):
    rows = qkv.shape[0]
    heads = width // 128
    off = row0 // seq
    in_specs = [pl.BlockSpec((seq, width), lambda i, c, j=j: (i, 3 * group + j)) for j in range(3)]
    in_specs.append(pl.BlockSpec((seq, width), lambda i, c: (i + off, c[0])))
    args = [grp, qkv, qkv, qkv, d_att]
    aliases = {}
    if prev is not None:
        in_specs.append(pl.BlockSpec(memory_space=pl.ANY))
        args.append(prev)
        aliases = {5: 0}
    nheads = rows // seq * heads
    return pl.pallas_call(
        functools.partial(attn_bwd_body, heads, 128 ** -0.5),
        out_shape=(
            jax.ShapeDtypeStruct((total, 3 * width * out_groups), BF16),
            jax.ShapeDtypeStruct((8, 3 * width), F32),
        ),
        grid_spec=pltpu.PrefetchScalarGridSpec(
            num_scalar_prefetch=1,
            grid=(rows // seq,),
            in_specs=in_specs,
            out_specs=(
                pl.BlockSpec((seq, 3 * width), lambda i, c: (i + off, group)),
                pl.BlockSpec((8, 3 * width), lambda i, c: (0, 0)),
            ),
        ),
        input_output_aliases=aliases,
        cost_estimate=pl.CostEstimate(flops=nheads * seq * seq * 128 * 20, bytes_accessed=14 * rows * width, transcendentals=nheads * seq * seq),
        name="attn_bwd",
    )(*args)


def assemble_body(pos_ref, own_ref, recv_ref, out_ref):
    half = pl.num_programs(0) // 2
    mine = (pl.program_id(0) // half) == pos_ref[0]

    @pl.when(mine)
    def _():
        out_ref[...] = own_ref[...]

    @pl.when(jnp.logical_not(mine))
    def _():
        out_ref[...] = recv_ref[...]


def assemble(pos, own, recv, blk):
    rows, width = own.shape
    half = rows // blk

    def own_map(i, p):
        return (jnp.clip(i - p[0] * half, 0, half - 1), 0)

    def recv_map(i, p):
        return (jnp.clip(i - (1 - p[0]) * half, 0, half - 1), 0)

    return pl.pallas_call(
        assemble_body,
        out_shape=jax.ShapeDtypeStruct((2 * rows, width), own.dtype),
        grid_spec=pltpu.PrefetchScalarGridSpec(
            num_scalar_prefetch=1,
            grid=(2 * half,),
            in_specs=[pl.BlockSpec((blk, width), own_map), pl.BlockSpec((blk, width), recv_map)],
            out_specs=pl.BlockSpec((blk, width), lambda i, p: (i, 0)),
        ),
        cost_estimate=pl.CostEstimate(flops=rows * width, bytes_accessed=8 * rows * width, transcendentals=0),
        name="assemble",
    )(pos, own, recv)


def regroup_body(src_ref, out_ref):
    wide = src_ref.shape[1] // 6
    for j in range(2):
        for t in range(3):
            out_ref[:, (3 * j + t) * wide:(3 * j + t + 1) * wide] = src_ref[:, (2 * t + j) * wide:(2 * t + j + 1) * wide]


def regroup(val):
    rows, width = val.shape
    spec = pl.BlockSpec((256, width), lambda i: (i, 0))
    return pl.pallas_call(
        regroup_body,
        out_shape=jax.ShapeDtypeStruct(val.shape, val.dtype),
        grid=(rows // 256,),
        in_specs=[spec],
        out_specs=spec,
        cost_estimate=pl.CostEstimate(flops=rows * width, bytes_accessed=4 * rows * width, transcendentals=0),
        name="regroup",
    )(val)


def join_body(pos_ref, own_ref, recv_ref, half_ref, rest_ref, out_ref):
    wide = own_ref.shape[1] // 3
    steps = pl.num_programs(0) // 2
    mine = (pl.program_id(0) // steps) == pos_ref[0]

    def cols(t, j):
        return pl.ds((2 * t + j) * wide, wide)

    for src, flag in ((own_ref, mine), (recv_ref, jnp.logical_not(mine))):
        @pl.when(flag)
        def _(src=src):
            for t in range(3):
                out_ref[:, cols(t, 0)] = src[:, t * wide:(t + 1) * wide]

    for t in range(3):
        part = pl.ds(t * wide, wide)
        out_ref[:, cols(t, 1)] = (half_ref[:, part].astype(F32) + rest_ref[:, part].astype(F32)).astype(BF16)


def join(pos, own, recv, half, rest):
    rows, width = own.shape
    blk = 128
    steps = rows // blk
    own_spec = pl.BlockSpec((blk, width), lambda i, p: (jnp.clip(i - p[0] * steps, 0, steps - 1), 0))
    recv_spec = pl.BlockSpec((blk, width), lambda i, p: (jnp.clip(i - (1 - p[0]) * steps, 0, steps - 1), 0))
    full_spec = pl.BlockSpec((blk, width), lambda i, p: (i, 0))
    return pl.pallas_call(
        join_body,
        out_shape=jax.ShapeDtypeStruct((2 * rows, 2 * width), BF16),
        grid_spec=pltpu.PrefetchScalarGridSpec(
            num_scalar_prefetch=1,
            grid=(2 * steps,),
            in_specs=[own_spec, recv_spec, full_spec, full_spec],
            out_specs=pl.BlockSpec((blk, 2 * width), lambda i, p: (i, 0)),
        ),
        cost_estimate=pl.CostEstimate(flops=rows * width, bytes_accessed=20 * rows * width, transcendentals=0),
        name="join",
    )(pos, own, recv, half, rest)


def solution(mesh):
    act_spec = P(("depth", "row"), None, "col")
    mat_spec = P("row", "col")
    vec_spec = P("col")
    bias_spec = P("col", None)

    def swap(val, axis):
        return lax.ppermute(val, axis, SWAP)

    def tie(val, *deps):
        return lax.optimization_barrier((val,) + deps)[0]

    def gather(val, axes):
        return lax.all_gather(val, axes, axis=0, tiled=True)

    def scatter(val, axes):
        return lax.psum_scatter(val, axes, scatter_dimension=0, tiled=True)

    def block(x, ln_g, ln_b, w_qkv, b_qkv, w_o, b_o, d_y):
        num_seq, seq, width = x.shape
        half = num_seq // 2 * seq
        tokens = num_seq * seq
        piece = w_qkv.shape[0] // 2
        hw = width // 2
        col = lax.axis_index("col")
        dep = lax.axis_index("depth")
        other = 1 - col

        def grp_s(val):
            return jnp.reshape(val, (1,)).astype(jnp.int32)

        x2 = x.reshape(tokens, width)
        dy2 = d_y.reshape(tokens, width)
        col_arr, oth_arr, dep_arr = grp_s(col), grp_s(other), grp_s(dep)
        own_grp = [grp_s(col * 2 + j) for j in range(2)]
        oth_grp = [grp_s(other * 2 + j) for j in range(2)]

        def group_cols(val, j):
            return [val[:, t * width + j * hw:t * width + (j + 1) * hw] for t in range(3)]

        def slab(j):
            part = lax.dynamic_slice_in_dim(w_qkv, dep * piece, piece, 0)
            return jnp.concatenate(group_cols(part, j), axis=1)

        def send(val, axis="col"):
            return swap(val, axis)

        nb = hw // 128
        bias = jnp.concatenate([b_qkv[(2 * t + j) * nb:(2 * t + j + 1) * nb] for j in range(2) for t in range(3)], axis=0)
        vecs = jnp.concatenate([ln_g.reshape(-1, 128), ln_b.reshape(-1, 128), b_o.reshape(-1, 128), bias], axis=0)
        vecs_r = send(vecs)
        rows2 = half // 2
        x_out = [lax.dynamic_slice_in_dim(x2, other * half, rows2, 0)]
        slab_a = tie(slab(0), x_out[0])
        x_out.append(lax.dynamic_slice_in_dim(tie(x2, slab_a), other * half + rows2, rows2, 0))
        slab_b = tie(slab(1), x_out[1])
        wo_out = lax.dynamic_slice_in_dim(tie(w_o, slab_b), dep * piece, piece, 0)
        dy_out = lax.dynamic_slice_in_dim(tie(dy2, wo_out), other * half, half, 0)
        x_recv = [send(x_out[0])]
        wa_in = send(slab_a)
        x_recv.append(send(x_out[1]))
        wb_in = send(slab_b)
        wo_in = send(wo_out)
        dy_recv = send(dy_out)
        w_perm = regroup(tie(w_qkv, dy_out))
        wo_own = gather(w_o, "row")
        w_own = gather(w_perm, "row")

        nv = width // 128
        first = col == 0

        def both(lo, hi):
            a = vecs[lo:hi].reshape(1, -1)
            b = vecs_r[lo:hi].reshape(1, -1)
            return jnp.concatenate([jnp.where(first, a, b), jnp.where(first, b, a)], axis=1)

        g_full = both(0, nv)
        b_full = both(nv, 2 * nv)
        bo_oth = vecs_r[2 * nv:3 * nv].reshape(-1)
        bq_own = bias.reshape(-1)
        bq_oth = vecs_r[3 * nv:].reshape(2, 3 * hw)
        db_o = jnp.sum(dy2.astype(F32), axis=0)
        wq_oth = [None, None]
        qkv_oth = [None, None]
        dqkv_oth = [None, None]
        sum_oth = [None, None]

        def held(*vals):
            return lax.optimization_barrier(vals)

        def project(j):
            return (nn_dot(xn, wq_oth[j]) + bq_oth[j]).astype(BF16)

        def weight_grad(lhs, rhs):
            return tn_dot(lhs, rhs).astype(BF16)

        dy_own = lax.dynamic_slice_in_dim(tie(dy2, dy_out), col * half, half, 0)
        datt_part = nt_dot(tie(dy_own, w_perm), wo_own)

        xn = ln_fwd(col_arr, tie(x2, datt_part), x_recv[0], g_full, b_full, 0, half, None)
        qkv_own = [(nn_dot(xn[:rows2], w_own) + bq_own).astype(BF16)]
        wa_in, xn, qkv_own[0] = held(wa_in, xn, qkv_own[0])
        wq_oth[0] = gather(wa_in, ("row", "depth"))
        xn = ln_fwd(col_arr, x2, x_recv[1], g_full, b_full, rows2, half, xn)
        qkv_own.append((nn_dot(xn[rows2:], w_own) + bq_own).astype(BF16))
        att = None
        for i in range(2):
            att = attn_fwd(own_grp[0], qkv_own[i] if i else tie(qkv_own[0], qkv_own[1]), 2, hw, seq, i * rows2, half, att)
        wb_in, xn, att = held(wb_in, xn, att)
        wq_oth[1] = gather(wb_in, ("row", "depth"))
        qkv_oth[0] = project(0)
        att = attn_fwd(oth_grp[0], qkv_oth[0], 1, hw, seq, 0, half, att)
        wo_in, att, xn = held(wo_in, att, xn)
        wo_oth = gather(wo_in, ("row", "depth"))
        qkv_oth[1] = project(1)
        att = attn_fwd(oth_grp[1], qkv_oth[1], 1, hw, seq, 0, half, att)
        x_all = jnp.concatenate(x_recv, axis=0)
        y_send = (x_all.astype(F32) + nn_dot(att, wo_oth) + bo_oth).astype(BF16)
        y_recv = send(y_send)
        x_own = lax.dynamic_slice_in_dim(tie(x2, y_send), col * half, half, 0)
        y_own = (x_own.astype(F32) + nn_dot(att, wo_own) + b_o).astype(BF16)

        def back_far(j, gate):
            dqkv_oth[j], sum_oth[j] = attn_bwd(oth_grp[j], tie(qkv_oth[j], gate), d_att, 0, 1, hw, seq, 0, half, None)

        def back_own(j, gate, prev):
            total = 0.0
            for i in range(2):
                prev, part = attn_bwd(own_grp[j], tie(qkv_own[i], gate), d_att, j, 2, hw, seq, i * rows2, half, prev)
                total = total + part
            return prev, total

        wide = 3 * hw
        sum_own = [None, None]
        d_att = (nt_dot(tie(dy_recv, y_own), wo_oth) + datt_part).astype(BF16)
        dwo_far = weight_grad(tie(att, d_att), dy_recv)
        red_of = scatter(dwo_far, "row")
        back_far(0, dwo_far)
        dw_a = weight_grad(xn, dqkv_oth[0])
        red_a = scatter(dw_a, ("row", "depth"))
        red_of, dw_a = held(red_of, dw_a)
        far_o = send(red_of)
        dwo_near = weight_grad(tie(att, dw_a), dy_own)
        red_on = scatter(dwo_near, "row")
        back_far(1, dwo_near)
        dw_b = weight_grad(xn, dqkv_oth[1])
        red_b = scatter(dw_b, "row")
        far_o, red_on, red_a, dw_b = held(far_o, red_on, red_a, dw_b)
        far_a = send(red_a)
        half_o = (red_on.astype(F32) + far_o.astype(F32)).astype(BF16)
        half_r = send(half_o, "depth")
        dqkv_own, sum_own[0] = back_own(0, half_o, None)
        dw_oa = weight_grad(xn, dqkv_own[:, :wide])
        red_oa = scatter(dw_oa, ("row", "depth"))
        red_b, dw_oa = held(red_b, dw_oa)
        far_b = send(red_b)
        dqkv_own, sum_own[1] = back_own(1, dw_oa, dqkv_own)
        dw_ob = weight_grad(xn, dqkv_own[:, wide:])
        red_ob = scatter(dw_ob, "row")

        parts = (half // 3,) * 3
        dx, gate = None, dw_ob
        dx_recv, sums_n = [], []
        for part in range(len(parts)):
            lo, rows = part * parts[0], parts[part]
            dxn = nt_dot(tie(dqkv_own, gate)[lo:lo + rows], w_own)
            if part == 0:
                far_a, red_oa, dxn = held(far_a, red_oa, dxn)
                half_a = (red_oa.astype(F32) + far_a.astype(F32)).astype(BF16)
                rest_a = send(half_a, "depth")
                dxn = tie(dxn, half_a)
            dxn = nt_dot(dqkv_oth[0][lo:lo + rows], wq_oth[0]) + dxn
            if part == 0:
                far_b, red_ob, dxn = held(far_b, red_ob, dxn)
                half_b = (red_ob.astype(F32) + far_b.astype(F32)).astype(BF16)
                rest_b = send(half_b, "depth")
                dxn = tie(dxn, half_b)
            dxn = nt_dot(dqkv_oth[1][lo:lo + rows], wq_oth[1]) + dxn
            dx, dx_send, dg8, db8 = ln_bwd(col_arr, dxn, x2, x_recv, dy2, dy_recv, g_full, lo, half, dx)
            sums_n.append((dg8, db8))
            dx_recv.append(send(dx_send))
            gate = dx_send
        y = assemble(col_arr, y_own, tie(y_recv, gate), 256)
        dw_o = (tie(half_o, y).astype(F32) + half_r.astype(F32)).astype(BF16)
        dw_qkv = join(dep_arr, half_a, tie(rest_a, dw_o), half_b, rest_b)
        dg8 = sum(pair[0] for pair in sums_n)
        db8 = sum(pair[1] for pair in sums_n)

        def natural(pair):
            vals = [jnp.sum(s, axis=0).reshape(3, hw) for s in pair]
            return jnp.concatenate([vals[j][t] for t in range(3) for j in range(2)])

        dg = jnp.sum(dg8, axis=0)
        dbn = jnp.sum(db8, axis=0)
        far = jnp.concatenate([natural(sum_oth), lax.dynamic_slice_in_dim(dg, other * width, width), lax.dynamic_slice_in_dim(dbn, other * width, width)])
        near = jnp.concatenate([natural(sum_own), lax.dynamic_slice_in_dim(dg, col * width, width), lax.dynamic_slice_in_dim(dbn, col * width, width)])
        total = near.reshape(-1, 128) + send(far.reshape(-1, 128))
        total, db_o = lax.psum((total, db_o), ("depth", "row"))
        for part in range(len(parts)):
            dx = lax.dynamic_update_slice(dx, tie(dx_recv[part], dw_o if part < 2 else dw_qkv), (other * half + part * parts[0], 0))
        nq = 3 * nv
        return (
            y.reshape(x.shape),
            dx.reshape(x.shape),
            dw_qkv,
            total[:nq],
            dw_o,
            db_o,
            total[nq:nq + nv].reshape(-1),
            total[nq + nv:].reshape(-1),
        )

    return jax.shard_map(
        block,
        mesh=mesh,
        in_specs=(act_spec, vec_spec, vec_spec, mat_spec, bias_spec, mat_spec, vec_spec, act_spec),
        out_specs=(act_spec, act_spec, mat_spec, bias_spec, mat_spec, vec_spec, vec_spec, vec_spec),
        check_vma=False,
    )
```

time: 5090 us -> 3200 us (0.63)
  waiting for transfers between devices: 2580 us -> 1160 us
  matrix products: 1860 us -> 1490 us
  Pallas kernels: 0 us -> 358 us
  other arithmetic: 321 us -> 67.1 us
  local copies, waits for them, and re-layouts: 276 us -> 74.8 us
    ppermute x0 -> x18, waiting for transfers between devices: none -> 1120 us  [swap(): return lax.ppermute(val, axis, SWAP)]
    all_gather x4 -> x5, waiting for transfers between devices: 1110 us -> 39.3 us  [gather(): return lax.all_gather(val, axes, axis=0, tiled=True)]
    reduce_scatter x3 -> x4, waiting for transfers between devices: 814 us -> 0.02 us  [scatter(): return lax.psum_scatter(val, axes, scatter_dimension=0, tiled=True)]
    psum x1 -> x0, waiting for transfers between devices: 653 us -> none  [local_block(): dw_qkv = lax.psum(dw_qkv, 'depth')]
    dot_general x12 -> x23, matrix products: 1860 us -> 1490 us  [the longest x11 526 us: nt_dot(): lax.dot_general(lhs, rhs, (((1,), (1,)), ((), ())), preferred_element_typ...]
    pallas_call x0 -> x18, Pallas kernels: none -> 358 us  [the longest x6 120 us: attn_bwd(): pl.pallas_call(functools.partial(attn_bwd_body, heads, 128 ** (-0.5)), ou...]
    reduce_sum x5 -> x7, other arithmetic: 128 us -> 11.8 us  [the longest x1 9.74 us: block(): db_o = jnp.sum(dy2.astype(F32), axis=0)]
    unnamed x28 -> x68, local copies, waits for them, and re-layouts: 112 us -> 4.86 us
  transfers between devices with their start and end apart: 9 -> 29, of which waited for: 6 -> 7; matrix products, arithmetic and copies ran while one was open for 47% -> 47% of each run, Pallas kernels for 0% -> 11%
where the time goes in v1:
time: 3200 us; the launch traced here: 3190 us
  matrix products  1490 us (47%)
  waiting for transfers between devices  1160 us (36%)
  Pallas kernels  358 us (11%)
  local copies, waits for them, and re-layouts  74.8 us (2%)
  other arithmetic  67.1 us (2%)
    ppermute x18, waiting for transfers between devices, swap(): return lax.ppermute(val, axis, SWAP)  1120 us
    dot_general x11, matrix products, nt_dot(): lax.dot_general(lhs, rhs, (((1,), (1,)), ((), ())), preferred_element_typ...  526 us
    dot_general x6, matrix products, nn_dot(): lax.dot_general(lhs, rhs, (((1,), (0,)), ((), ())), preferred_element_typ...  486 us
    dot_general x6, matrix products, tn_dot(): lax.dot_general(lhs, rhs, (((0,), (0,)), ((), ())), preferred_element_typ...  477 us
    pallas_call x6, Pallas kernels, attn_bwd(): pl.pallas_call(functools.partial(attn_bwd_body, heads, 128 ** (-0.5)), ou...  120 us
    pallas_call x4, Pallas kernels, attn_fwd(): pl.pallas_call(functools.partial(attn_fwd_body, heads, 128 ** (-0.5)), ou...  69.7 us
    pallas_call x3, Pallas kernels, ln_bwd(): pl.pallas_call(body, out_shape=(jax.ShapeDtypeStruct((2 * total, width),...  68.2 us
  transfers between devices with their start and end apart: 29, of which 7 were waited for; matrix products, arithmetic and copies ran while one was open for 47% of the time, Pallas kernels for 11%

profile of v1, /device:TPU:0, one launch (start us, length us, event | category | flops | bytes accessed | tf_op | source)
XLA Modules:
  0.0 3191.0 jit_solution(9981314001933511066)
XLA Ops:
  8.0 5.4 constant_dynamic-slice_fusion
  13.4 8.9 constant_dynamic-slice_fusion.5
  22.3 6.7 pad_maximum_fusion
  29.0 8.4 constant_dynamic-slice_fusion.4
  37.4 4.8 constant_dynamic-slice_fusion.3
  42.2 10.7 constant_dynamic-slice_fusion.2
  52.9 18.3 regroup.1
  77.1 13.7 constant_dynamic-slice_fusion.1
  90.8 255.3 %collective-permute-done.4 = f32[96,128]{1,0:T(8,128)S(1)} collective-permute-done((f32[96,128]{1,0:T(8,128)S(1)}, f32[96,128]{1,0:T(8,128)S(1)}, u32[]{:S(2)}, u32[]{:S(2)}) %collective-permute-start.4) | collective-permute-done | bytes 49184 | tf_op jit(solution)/shard_map/ppermute | solution.py:450
  347.3 61.1 %fusion.22 = f32[3072,4096]{1,0:T(8,128)} fusion(bf16[3072,2048]{1,0:T(8,128)(2,1)} %constant_dynamic-slice_fusion.1, bf16[4096,2048]{1,0:T(8,128)(2,1)} %all-gather.6.cloned.1.call-done), kind=kOutput, calls=%fused_computation.100 | convolution fusion | flops 51539607552 | bytes 79691776 | tf_op jit(solution)/shard_map/dot_general | solution.py:19
  408.4 15.3 ln_fwd.2.rest_0_
  423.7 88.9 %add_convert_fusion.4.q_ref.k_ref.v_ref = bf16[1536,6144]{1,0:T(8,128)(2,1)} fusion(bf16[4096,6144]{1,0:T(8,128)(2,1)} %all-gather.8.cloned.1.call-done, f32[6144]{0:T(1024)S(1)} %bitcast.106, bf16[3072,4096]{1,0:T(8,128)(2,1)} %ln_fwd.2.rest_0_), kind=kOutput, calls=%fused_computation.5 | convolution fusion | flops 77328285696 | bytes 81813504 | tf_op jit(solution)/shard_map/dot_general | solution.py:27
  514.7 136.7 %collective-permute-done.1.recv_ref.x1_ref = bf16[1536,2048]{1,0:T(8,128)(2,1)} collective-permute-done((bf16[1536,2048]{1,0:T(8,128)(2,1)}, bf16[1536,2048]{1,0:T(8,128)(2,1)}, u32[]{:S(2)}, u32[]{:S(2)}) %collective-permute-start.1) | collective-permute-done | bytes 6291488 | tf_op jit(solution)/shard_map/ppermute | solution.py:450
  651.4 15.5 ln_fwd.3
  666.9 88.4 %add_convert_fusion.3.q_ref.k_ref.v_ref = bf16[1536,6144]{1,0:T(8,128)(2,1)} fusion(bf16[4096,6144]{1,0:T(8,128)(2,1)} %all-gather.8.cloned.1.call-done, f32[6144]{0:T(1024)S(1)} %bitcast.107, bf16[3072,4096]{1,0:T(8,128)(2,1)} %ln_fwd.3), kind=kOutput, calls=%fused_computation.4 | convolution fusion | flops 77328285696 | bytes 81813504 | tf_op jit(solution)/shard_map/dot_general | solution.py:27
  755.4 17.4 attn_fwd.4.rest_0_
  772.8 17.4 attn_fwd.5.rest_0_
  792.6 92.8 %add_convert_fusion.2.q_ref.k_ref.v_ref = bf16[3072,3072]{1,0:T(8,128)(2,1)} fusion(f32[3072]{0:T(1024)S(1)} %get-tuple-element.172, bf16[3072,4096]{1,0:T(8,128)(2,1)} %ln_fwd.3, bf16[4096,3072]{1,0:T(8,128)(2,1)} %all-gather.10.cloned.1.call-done), kind=kOutput, calls=%fused_computation.3 | convolution fusion | flops 77328285696 | bytes 69218304 | tf_op jit(solution)/shard_map/dot_general | solution.py:27
  885.4 17.5 attn_fwd.6.rest_0_
  904.3 39.3 %all-gather.12.cloned.1.call-done = bf16[4096,3072]{1,0:T(8,128)(2,1)} async-done(((bf16[1024,3072]{1,0:T(8,128)(2,1)}), bf16[4096,3072]{1,0:T(8,128)(2,1)}) %all-gather.12.cloned.1.call-update) | async-done | bytes 25165840 | tf_op jit(solution)/shard_map/all_gather | solution.py:456
  943.6 90.2 %add_convert_fusion.1.q_ref.k_ref.v_ref = bf16[3072,3072]{1,0:T(8,128)(2,1)} fusion(f32[3072]{0:T(1024)S(1)} %copy-done.15, bf16[3072,4096]{1,0:T(8,128)(2,1)} %ln_fwd.3, bf16[4096,3072]{1,0:T(8,128)(2,1)} %all-gather.12.cloned.1.call-done), kind=kOutput, calls=%fused_computation.2 | convolution fusion | flops 77328285696 | bytes 69218304 | tf_op jit(solution)/shard_map/dot_general | solution.py:27
  1033.8 17.4 attn_fwd.7
  1051.2 63.9 %add_convert_fusion.7 = bf16[3072,2048]{1,0:T(8,128)(2,1)} fusion(bf16[1536,2048]{1,0:T(8,128)(2,1)} %collective-permute-done.1.recv_ref.x1_ref, bf16[1536,2048]{1,0:T(8,128)(2,1)} %collective-permute-done.recv_ref.x0_ref, f32[2048]{0:T(1024)S(1)} %copy-done.18, bf16[3072,4096]{1,0:T(8,128)(2,1)} %attn_fwd.7, ...), kind=kOutput, calls=%fused_computation.8 | convolution fusion | flops 51583647744 | bytes 67117056 | tf_op jit(solution)/shard_map/dot_general | solution.py:27
  1115.1 62.3 %add_convert_fusion.6.own_ref = bf16[3072,2048]{1,0:T(8,128)(2,1)} fusion(bf16[3072,4096]{1,0:T(8,128)(2,1)} %attn_fwd.7, bf16[4096,2048]{1,0:T(8,128)(2,1)} %all-gather.6.cloned.1.call-done, f32[2048]{0:T(1024)S(1)} %copy-done.17, bf16[6144,2048]{1,0:T(8,128)(2,1)} %bitcast.91, s32[]{:T(128)S(6)} %select_n.75), kind=kOutput, calls=%fused_computation.7 | convolution fusion | flops 51564773376 | bytes 67117056 | tf_op jit(solution)/shard_map/dot_general | solution.py:27
  1177.4 63.3 %add_convert_fusion.d_ref = bf16[3072,4096]{1,0:T(8,128)(2,1)} fusion(f32[3072,4096]{1,0:T(8,128)} %fusion.22, bf16[3072,2048]{1,0:T(8,128)(2,1)} %collective-permute-done.7.rest_1_, bf16[4096,2048]{1,0:T(8,128)(2,1)} %all-gather.14.cloned.1.call-done), kind=kOutput, calls=%fused_computation.1 | convolution fusion | flops 51564773376 | bytes 104857600 | tf_op jit(solution)/shard_map/dot_general | solution.py:19
  1240.7 61.3 %convolution_convert_fusion.4 = bf16[4096,2048]{1,0:T(8,128)(2,1)} fusion(bf16[3072,4096]{1,0:T(8,128)(2,1)} %attn_fwd.7, bf16[3072,2048]{1,0:T(8,128)(2,1)} %collective-permute-done.7.rest_1_), kind=kOutput, calls=%fused_computation.19 | convolution fusion | flops 51547996160 | bytes 54525952 | tf_op jit(solution)/shard_map/dot_general | solution.py:23
  1302.1 62.9 %convolution_convert_fusion.5 = bf16[4096,2048]{1,0:T(8,128)(2,1)} fusion(bf16[3072,4096]{1,0:T(8,128)(2,1)} %attn_fwd.7, bf16[3072,2048]{1,0:T(8,128)(2,1)} %constant_dynamic-slice_fusion.1), kind=kOutput, calls=%fused_computation.20 | convolution fusion | flops 51547996160 | bytes 54525952 | tf_op jit(solution)/shard_map/dot_general | solution.py:23
  1365.1 28.6 attn_bwd.7
  1393.7 88.0 %convolution_convert_fusion.2 = bf16[4096,3072]{1,0:T(8,128)(2,1)} fusion(bf16[3072,4096]{1,0:T(8,128)(2,1)} %ln_fwd.3, bf16[3072,3072]{1,0:T(8,128)(2,1)} %get-tuple-element.108), kind=kOutput, calls=%fused_computation.11 | convolution fusion | flops 77321994240 | bytes 69206016 | tf_op jit(solution)/shard_map/dot_general | solution.py:23
  1481.8 30.2 attn_bwd.6
  1512.0 88.2 %convolution_convert_fusion.3 = bf16[4096,3072]{1,0:T(8,128)(2,1)} fusion(bf16[3072,4096]{1,0:T(8,128)(2,1)} %ln_fwd.3, bf16[3072,3072]{1,0:T(8,128)(2,1)} %get-tuple-element.105), kind=kOutput, calls=%fused_computation.12 | convolution fusion | flops 77321994240 | bytes 69206016 | tf_op jit(solution)/shard_map/dot_general | solution.py:23
  1600.7 181.7 %collective-permute-done.8 = bf16[2048,2048]{1,0:T(8,128)(2,1)} collective-permute-done((bf16[2048,2048]{1,0:T(8,128)(2,1)}, bf16[2048,2048]{1,0:T(8,128)(2,1)}, u32[]{:S(2)}, u32[]{:S(2)}) %collective-permute-start.8) | collective-permute-done | bytes 8388640 | tf_op jit(solution)/shard_map/ppermute | solution.py:450
  1782.5 10.6 add_convert_fusion.9
  1793.1 14.4 attn_bwd.8
  1807.5 14.4 attn_bwd.9
  1821.8 88.0 %convolution_convert_fusion.1 = bf16[4096,3072]{1,0:T(8,128)(2,1)} fusion(bf16[3072,4096]{1,0:T(8,128)(2,1)} %ln_fwd.3, bf16[3072,6144]{1,0:T(8,128)(2,1)} %get-tuple-element.115.rest_0_), kind=kOutput, calls=%fused_computation.10 | convolution fusion | flops 77321994240 | bytes 69206016 | tf_op jit(solution)/shard_map/dot_general | solution.py:23
  1909.9 16.1 attn_bwd.10
  1926.1 15.8 attn_bwd.11
  1941.9 88.2 %convolution_convert_fusion = bf16[4096,3072]{1,0:T(8,128)(2,1)} fusion(bf16[3072,4096]{1,0:T(8,128)(2,1)} %ln_fwd.3, bf16[3072,6144]{1,0:T(8,128)(2,1)} %get-tuple-element.136), kind=kOutput, calls=%fused_computation.9 | convolution fusion | flops 77321994240 | bytes 69206016 | tf_op jit(solution)/shard_map/dot_general | solution.py:23
  2031.3 33.7 %fusion.12 = f32[1024,4096]{1,0:T(8,128)} fusion(bf16[4096,3072]{1,0:T(8,128)(2,1)} %all-gather.10.cloned.1.call-done, bf16[3072,3072]{1,0:T(8,128)(2,1)} %get-tuple-element.108), kind=kOutput, calls=%fused_computation.36 | convolution fusion | flops 25769803776 | bytes 48234496 | tf_op jit(solution)/shard_map/dot_general | solution.py:19
  2065.0 34.6 %fusion.15 = f32[1024,4096]{1,0:T(8,128)} fusion(bf16[4096,3072]{1,0:T(8,128)(2,1)} %all-gather.10.cloned.1.call-done, bf16[3072,3072]{1,0:T(8,128)(2,1)} %get-tuple-element.108), kind=kOutput, calls=%fused_computation.39 | convolution fusion | flops 25769803776 | bytes 48234496 | tf_op jit(solution)/shard_map/dot_general | solution.py:19
  2102.1 66.4 %fusion.8 = f32[1024,4096]{1,0:T(8,128)} fusion(bf16[4096,6144]{1,0:T(8,128)(2,1)} %all-gather.8.cloned.1.call-done, bf16[3072,6144]{1,0:T(8,128)(2,1)} %get-tuple-element.136), kind=kOutput, calls=%fused_computation.28 | convolution fusion | flops 51539607552 | bytes 79691776 | tf_op jit(solution)/shard_map/dot_general | solution.py:19
  2172.1 266.4 %collective-permute-done.10 = bf16[1024,3072]{1,0:T(8,128)(2,1)} collective-permute-done((bf16[1024,3072]{1,0:T(8,128)(2,1)}, bf16[1024,3072]{1,0:T(8,128)(2,1)}, u32[]{:S(2)}, u32[]{:S(2)}) %collective-permute-start.10) | collective-permute-done | bytes 6291488 | tf_op jit(solution)/shard_map/ppermute | solution.py:450
  2438.5 10.1 add_convert_fusion.10.own_ref
  2448.6 35.1 %convolution_add_fusion = f32[1024,4096]{1,0:T(8,128)} fusion(f32[1024,4096]{1,0:T(8,128)} %fusion.8, bf16[4096,3072]{1,0:T(8,128)(2,1)} %all-gather.10.cloned.1.call-done, bf16[3072,3072]{1,0:T(8,128)(2,1)} %get-tuple-element.108), kind=kOutput, calls=%fused_computation.30 | convolution fusion | flops 25773998080 | bytes 65011712 | tf_op jit(solution)/shard_map/dot_general | solution.py:19
  2483.8 221.9 %collective-permute-done.9 = bf16[2048,3072]{1,0:T(8,128)(2,1)} collective-permute-done((bf16[2048,3072]{1,0:T(8,128)(2,1)}, bf16[2048,3072]{1,0:T(8,128)(2,1)}, u32[]{:S(2)}, u32[]{:S(2)}) %collective-permute-start.9) | collective-permute-done | bytes 12582944 | tf_op jit(solution)/shard_map/ppermute | solution.py:450
  2705.7 15.5 add_convert_fusion.5.half_ref
  2722.1 34.6 %convolution_add_fusion.1.dxn_ref = f32[1024,4096]{1,0:T(8,128)} fusion(f32[1024,4096]{1,0:T(8,128)} %convolution_add_fusion, bf16[4096,3072]{1,0:T(8,128)(2,1)} %all-gather.12.cloned.1.call-done, bf16[3072,3072]{1,0:T(8,128)(2,1)} %get-tuple-element.105), kind=kOutput, calls=%fused_computation.31 | convolution fusion | flops 25773998080 | bytes 65011712 | tf_op jit(solution)/shard_map/dot_general | solution.py:19
  2756.7 22.7 ln_bwd.3
  2779.4 61.2 %fusion.6 = f32[1024,4096]{1,0:T(8,128)} fusion(bf16[4096,6144]{1,0:T(8,128)(2,1)} %all-gather.8.cloned.1.call-done, bf16[3072,6144]{1,0:T(8,128)(2,1)} %get-tuple-element.136), kind=kOutput, calls=%fused_computation.25 | convolution fusion | flops 51539607552 | bytes 79691776 | tf_op jit(solution)/shard_map/dot_general | solution.py:19
  2840.6 37.4 %add_add_fusion.1.dxn_ref = f32[1024,4096]{1,0:T(8,128)} fusion(f32[1024,4096]{1,0:T(8,128)} %fusion.12, f32[1024,4096]{1,0:T(8,128)} %fusion.6, bf16[4096,3072]{1,0:T(8,128)(2,1)} %all-gather.12.cloned.1.call-done, bf16[3072,3072]{1,0:T(8,128)(2,1)} %get-tuple-element.105), kind=kOutput, calls=%fused_computation.17 | convolution fusion | flops 25778192384 | bytes 81788928 | tf_op jit(solution)/shard_map/dot_general | solution.py:19
  2878.0 22.6 ln_bwd.4
  2902.3 61.6 %fusion.4 = f32[1024,4096]{1,0:T(8,128)} fusion(bf16[4096,6144]{1,0:T(8,128)(2,1)} %all-gather.8.cloned.1.call-done, bf16[3072,6144]{1,0:T(8,128)(2,1)} %get-tuple-element.136), kind=kOutput, calls=%fused_computation.23 | convolution fusion | flops 51539607552 | bytes 79691776 | tf_op jit(solution)/shard_map/dot_general | solution.py:19
  2964.3 37.1 %add_add_fusion.dxn_ref = f32[1024,4096]{1,0:T(8,128)} fusion(f32[1024,4096]{1,0:T(8,128)} %fusion.15, f32[1024,4096]{1,0:T(8,128)} %fusion.4, bf16[4096,3072]{1,0:T(8,128)(2,1)} %all-gather.12.cloned.1.call-done, bf16[3072,3072]{1,0:T(8,128)(2,1)} %get-tuple-element.105), kind=kOutput, calls=%fused_computation.16 | convolution fusion | flops 25778192384 | bytes 81788928 | tf_op jit(solution)/shard_map/dot_general | solution.py:19
  3001.4 22.9 ln_bwd.5
  3029.2 53.2 %collective-permute-done.17 = f32[80,128]{1,0:T(8,128)S(1)} collective-permute-done((f32[80,128]{1,0:T(8,128)S(1)}, f32[80,128]{1,0:T(8,128)S(1)}, u32[]{:S(2)}, u32[]{:S(2)}) %collective-permute-start.17) | collective-permute-done | bytes 40992 | tf_op jit(solution)/shard_map/ppermute | solution.py:450
  3084.0 9.7 convert_reduce_fusion
  3093.8 26.4 assemble.1
  3120.2 10.4 add_convert_fusion.8
  3131.4 12.0 all-reduce.2
  3144.6 4.8 constant_dynamic-update-slice_fusion.19
  3149.4 4.8 constant_dynamic-update-slice_fusion.18
  3154.2 25.3 join.1
  3179.5 4.8 constant_dynamic-update-slice_fusion.17
  (147 shorter events, 33.0 us)
Async XLA Ops:
  7.2 340.2 %all-gather.6.cloned.1.call-start = ((), (), s32[]{:S(2)}) async-start(), calls=%async_computation.6 | async-start | bytes 25165824 | tf_op jit(solution)/shard_map/all_gather | solution.py:456
  7.9 415.8 %all-gather.8.cloned.1.call-start = ((), (), s32[]{:S(2)}) async-start(), calls=%async_computation.7 | async-start | bytes 75497472 | tf_op jit(solution)/shard_map/all_gather | solution.py:456
  71.2 3.2 copy-start.10
  71.2 3.2 copy-start.13
  71.2 3.2 copy-start.14
  71.2 3.2 copy-start.16
  71.2 721.3 %all-gather.10.cloned.1.call-start = ((), (), s32[]{:S(2)}) async-start(), calls=%async_computation.8 | async-start | bytes 31457280 | tf_op jit(solution)/shard_map/all_gather | solution.py:456
  71.3 337.1 %collective-permute-start = (bf16[1536,2048]{1,0:T(8,128)(2,1)}, bf16[1536,2048]{1,0:T(8,128)(2,1)}, u32[]{:S(2)}, u32[]{:S(2)}) collective-permute-start(bf16[1536,2048]{1,0:T(8,128)(2,1)} %constant_dynamic-slice_fusion.5), channel_id=1, source_target_pairs={{0,2},{2,0},{1,3},{3,1},{4,6},{6,4},{5,7},{7,5}} | collective-permute-start | bytes 18874376 | tf_op jit(solution)/shard_map/ppermute | solution.py:450
  74.4 438.3 %collective-permute-start.5 = (bf16[1024,3072]{1,0:T(8,128)(2,1)}, bf16[1024,3072]{1,0:T(8,128)(2,1)}, u32[]{:S(2)}, u32[]{:S(2)}) collective-permute-start(bf16[1024,3072]{1,0:T(8,128)(2,1)} %get-tuple-element.83), channel_id=1, source_target_pairs={{0,2},{2,0},{1,3},{3,1},{4,6},{6,4},{5,7},{7,5}} | collective-permute-start | bytes 18874376 | tf_op jit(solution)/shard_map/ppermute | solution.py:450
  74.5 0.6 copy-start.19
  75.1 271.0 %collective-permute-start.4 = (f32[96,128]{1,0:T(8,128)S(1)}, f32[96,128]{1,0:T(8,128)S(1)}, u32[]{:S(2)}, u32[]{:S(2)}) collective-permute-start(f32[96,128]{1,0:T(8,128)S(1)} %constant_dynamic-update-slice_fusion), channel_id=1, source_target_pairs={{0,2},{2,0},{1,3},{3,1},{4,6},{6,4},{5,7},{7,5}} | collective-permute-start | bytes 147464 | tf_op jit(solution)/shard_map/ppermute | solution.py:450
  346.1 62.3 %copy-start.11 = (f32[96,128]{1,0:T(8,128)}, f32[96,128]{1,0:T(8,128)S(1)}, u32[]{:S(2)}) copy-start(f32[96,128]{1,0:T(8,128)S(1)} %collective-permute-done.4) | copy-start | bytes 147460
  408.4 15.3 copy-start.20
  512.6 430.9 %all-gather.12.cloned.1.call-start = ((), (), s32[]{:S(2)}) async-start(), calls=%async_computation.9 | async-start | bytes 31457280 | tf_op jit(solution)/shard_map/all_gather | solution.py:456
  512.7 138.7 %collective-permute-start.1 = (bf16[1536,2048]{1,0:T(8,128)(2,1)}, bf16[1536,2048]{1,0:T(8,128)(2,1)}, u32[]{:S(2)}, u32[]{:S(2)}) collective-permute-start(bf16[1536,2048]{1,0:T(8,128)(2,1)} %constant_dynamic-slice_fusion.4), channel_id=1, source_target_pairs={{0,2},{2,0},{1,3},{3,1},{4,6},{6,4},{5,7},{7,5}} | collective-permute-start | bytes 18874376 | tf_op jit(solution)/shard_map/ppermute | solution.py:450
  514.4 275.8 %collective-permute-start.3 = (bf16[1024,3072]{1,0:T(8,128)(2,1)}, bf16[1024,3072]{1,0:T(8,128)(2,1)}, u32[]{:S(2)}, u32[]{:S(2)}) collective-permute-start(bf16[1024,3072]{1,0:T(8,128)(2,1)} %get-tuple-element.85), channel_id=1, source_target_pairs={{0,2},{2,0},{1,3},{3,1},{4,6},{6,4},{5,7},{7,5}} | collective-permute-start | bytes 18874376 | tf_op jit(solution)/shard_map/ppermute | solution.py:450
  772.8 19.2 copy-start.12
  790.2 260.9 %all-gather.14.cloned.1.call-start = ((), (), s32[]{:S(2)}) async-start(), calls=%async_computation.10 | async-start | bytes 20971520 | tf_op jit(solution)/shard_map/all_gather | solution.py:456
  790.3 112.6 %collective-permute-start.2 = (bf16[1024,2048]{1,0:T(8,128)(2,1)}, bf16[1024,2048]{1,0:T(8,128)(2,1)}, u32[]{:S(2)}, u32[]{:S(2)}) collective-permute-start(bf16[1024,2048]{1,0:T(8,128)(2,1)} %constant_dynamic-slice_fusion.3), channel_id=1, source_target_pairs={{0,2},{2,0},{1,3},{3,1},{4,6},{6,4},{5,7},{7,5}} | collective-permute-start | bytes 12582920 | tf_op jit(solution)/shard_map/ppermute | solution.py:450
  885.4 58.2 %copy-start.15 = (f32[3072]{0:T(1024)S(1)}, f32[3072]{0:T(1024)}, u32[]{:S(2)}) copy-start(f32[3072]{0:T(1024)} %get-tuple-element.173) | copy-start | bytes 36868
  902.9 697.4 %reduce-scatter.13.cloned.1.call-start = ((), (), s32[]{:S(2)}) async-start(), calls=%async_computation.11 | async-start | bytes 25165824 | tf_op jit(solution)/shard_map/reduce_scatter | solution.py:459
  902.9 274.5 %collective-permute-start.7 = (bf16[3072,2048]{1,0:T(8,128)(2,1)}, bf16[3072,2048]{1,0:T(8,128)(2,1)}, u32[]{:S(2)}, u32[]{:S(2)}) collective-permute-start(bf16[3072,2048]{1,0:T(8,128)(2,1)} %constant_dynamic-slice_fusion.2), channel_id=1, source_target_pairs={{0,2},{2,0},{1,3},{3,1},{4,6},{6,4},{5,7},{7,5}} | collective-permute-start | bytes 37748744 | tf_op jit(solution)/shard_map/ppermute | solution.py:450
  1033.8 17.4 copy-start.18
  1051.2 63.9 %copy-start.17 = (f32[2048]{0:T(1024)S(1)}, f32[2048]{0:T(1024)}, u32[]{:S(2)}) copy-start(f32[2048]{0:T(1024)} %param.14) | copy-start | bytes 24580
  1302.1 298.6 %reduce-scatter.15.cloned.1.call-start = ((), (), s32[]{:S(2)}) async-start(), calls=%async_computation.12 | async-start | bytes 25165824 | tf_op jit(solution)/shard_map/reduce_scatter | solution.py:459
  1365.0 417.4 %reduce-scatter.17.cloned.1.call-start = ((), (), s32[]{:S(2)}) async-start(), calls=%async_computation.13 | async-start | bytes 31457280 | tf_op jit(solution)/shard_map/reduce_scatter | solution.py:459
  1481.7 428.2 %reduce-scatter.21.cloned.1.call-start = ((), (), s32[]{:S(2)}) async-start(), calls=%async_computation.15 | async-start | bytes 37748736
  1600.2 838.3 %reduce-scatter.19.cloned.1.call-start = ((), (), s32[]{:S(2)}) async-start(), calls=%async_computation.14 | async-start | bytes 31457280 | tf_op jit(solution)/shard_map/reduce_scatter | solution.py:459
  1600.3 182.2 %collective-permute-start.8 = (bf16[2048,2048]{1,0:T(8,128)(2,1)}, bf16[2048,2048]{1,0:T(8,128)(2,1)}, u32[]{:S(2)}, u32[]{:S(2)}) collective-permute-start(bf16[2048,2048]{1,0:T(8,128)(2,1)} %reduce-scatter.13.cloned.1.call-done), channel_id=1, source_target_pairs={{0,2},{2,0},{1,3},{3,1},{4,6},{6,4},{5,7},{7,5}} | collective-permute-start | bytes 25165832 | tf_op jit(solution)/shard_map/ppermute | solution.py:450
  1909.8 795.8 %reduce-scatter.23.cloned.1.call-start = ((), (), s32[]{:S(2)}) async-start(), calls=%async_computation.16 | async-start | bytes 37748736
  2030.1 1.0 copy-start.6
  2030.1 1.1 copy-start.4
  2030.1 933.8 %collective-permute-start.6 = (bf16[3072,2048]{1,0:T(8,128)(2,1)}, bf16[3072,2048]{1,0:T(8,128)(2,1)}, u32[]{:S(2)}, u32[]{:S(2)}) collective-permute-start(bf16[3072,2048]{1,0:T(8,128)(2,1)} %add_convert_fusion.7), channel_id=1, source_target_pairs={{0,2},{2,0},{1,3},{3,1},{4,6},{6,4},{5,7},{7,5}} | collective-permute-start | bytes 37748744 | tf_op jit(solution)/shard_map/ppermute | solution.py:450
  2031.3 33.7 %copy-start.21 = (f32[10240]{0:T(1024)}, f32[10240]{0:T(1024)S(1)}, u32[]{:S(2)}) copy-start(f32[10240]{0:T(1024)S(1)} %slice_dynamic-update-slice_fusion) | copy-start | bytes 122884
  2099.7 68.8 %copy-start.8 = (f32[8,3072]{1,0:T(8,128)S(1)}, f32[8,3072]{1,0:T(8,128)}, u32[]{:S(2)}) copy-start(f32[8,3072]{1,0:T(8,128)} %get-tuple-element.148) | copy-start | bytes 294916
  2099.7 68.8 %copy-start.9 = (f32[8,3072]{1,0:T(8,128)S(1)}, f32[8,3072]{1,0:T(8,128)}, u32[]{:S(2)}) copy-start(f32[8,3072]{1,0:T(8,128)} %get-tuple-element.149) | copy-start | bytes 294916
  2099.7 68.8 %copy-start.5 = (f32[8,3072]{1,0:T(8,128)S(1)}, f32[8,3072]{1,0:T(8,128)}, u32[]{:S(2)}) copy-start(f32[8,3072]{1,0:T(8,128)} %get-tuple-element.146) | copy-start | bytes 294916
  2099.7 68.8 %copy-start.7 = (f32[8,3072]{1,0:T(8,128)S(1)}, f32[8,3072]{1,0:T(8,128)}, u32[]{:S(2)}) copy-start(f32[8,3072]{1,0:T(8,128)} %get-tuple-element.147) | copy-start | bytes 294916
  2099.7 927.8 %collective-permute-start.12 = (bf16[2048,2048]{1,0:T(8,128)(2,1)}, bf16[2048,2048]{1,0:T(8,128)(2,1)}, u32[]{:S(2)}, u32[]{:S(2)}) collective-permute-start(bf16[2048,2048]{1,0:T(8,128)(2,1)} %add_convert_fusion.9), channel_id=1, source_target_pairs={{0,4},{4,0},{1,5},{5,1},{2,6},{6,2},{3,7},{7,3}} | collective-permute-start | bytes 25165832 | tf_op jit(solution)/shard_map/ppermute | solution.py:450
  2100.0 338.5 %collective-permute-start.10 = (bf16[1024,3072]{1,0:T(8,128)(2,1)}, bf16[1024,3072]{1,0:T(8,128)(2,1)}, u32[]{:S(2)}, u32[]{:S(2)}) collective-permute-start(bf16[1024,3072]{1,0:T(8,128)(2,1)} %reduce-scatter.17.cloned.1.call-done), channel_id=1, source_target_pairs={{0,2},{2,0},{1,3},{3,1},{4,6},{6,4},{5,7},{7,5}} | collective-permute-start | bytes 18874376 | tf_op jit(solution)/shard_map/ppermute | solution.py:450
  2100.7 605.0 %collective-permute-start.9 = (bf16[2048,3072]{1,0:T(8,128)(2,1)}, bf16[2048,3072]{1,0:T(8,128)(2,1)}, u32[]{:S(2)}, u32[]{:S(2)}) collective-permute-start(bf16[2048,3072]{1,0:T(8,128)(2,1)} %reduce-scatter.21.cloned.1.call-done), channel_id=1, source_target_pairs={{0,2},{2,0},{1,3},{3,1},{4,6},{6,4},{5,7},{7,5}} | collective-permute-start | bytes 37748744 | tf_op jit(solution)/shard_map/ppermute | solution.py:450
  2448.6 705.6 %collective-permute-start.15 = (bf16[1024,3072]{1,0:T(8,128)(2,1)}, bf16[1024,3072]{1,0:T(8,128)(2,1)}, u32[]{:S(2)}, u32[]{:S(2)}) collective-permute-start(bf16[1024,3072]{1,0:T(8,128)(2,1)} %add_convert_fusion.10.own_ref), channel_id=1, source_target_pairs={{0,4},{4,0},{1,5},{5,1},{2,6},{6,2},{3,7},{7,3}} | collective-permute-start | bytes 18874376 | tf_op jit(solution)/shard_map/ppermute | solution.py:450
  2721.1 433.1 %collective-permute-start.16 = (bf16[2048,3072]{1,0:T(8,128)(2,1)}, bf16[2048,3072]{1,0:T(8,128)(2,1)}, u32[]{:S(2)}, u32[]{:S(2)}) collective-permute-start(bf16[2048,3072]{1,0:T(8,128)(2,1)} %add_convert_fusion.5.half_ref), channel_id=1, source_target_pairs={{0,4},{4,0},{1,5},{5,1},{2,6},{6,2},{3,7},{7,3}} | collective-permute-start | bytes 37748744 | tf_op jit(solution)/shard_map/ppermute | solution.py:450
  2900.6 244.0 %collective-permute-start.13 = (bf16[1024,2048]{1,0:T(8,128)(2,1)}, bf16[1024,2048]{1,0:T(8,128)(2,1)}, u32[]{:S(2)}, u32[]{:S(2)}) collective-permute-start(bf16[1024,2048]{1,0:T(8,128)(2,1)} %get-tuple-element.135), channel_id=1, source_target_pairs={{0,2},{2,0},{1,3},{3,1},{4,6},{6,4},{5,7},{7,5}} | collective-permute-start | bytes 12582920 | tf_op jit(solution)/shard_map/ppermute | solution.py:450
  2963.9 180.7 %collective-permute-start.11 = (bf16[1024,2048]{1,0:T(8,128)(2,1)}, bf16[1024,2048]{1,0:T(8,128)(2,1)}, u32[]{:S(2)}, u32[]{:S(2)}) collective-permute-start(bf16[1024,2048]{1,0:T(8,128)(2,1)} %get-tuple-element.132), channel_id=1, source_target_pairs={{0,2},{2,0},{1,3},{3,1},{4,6},{6,4},{5,7},{7,5}} | collective-permute-start | bytes 12582920 | tf_op jit(solution)/shard_map/ppermute | solution.py:450
  3001.4 22.9 copy-start.2
  3001.4 22.9 copy-start.3
  3001.4 23.9 copy-start.22
  3001.4 24.5 copy-start
  3001.4 24.5 copy-start.1
  3027.5 54.9 %collective-permute-start.17 = (f32[80,128]{1,0:T(8,128)S(1)}, f32[80,128]{1,0:T(8,128)S(1)}, u32[]{:S(2)}, u32[]{:S(2)}) collective-permute-start(f32[80,128]{1,0:T(8,128)S(1)} %bitcast.108), channel_id=1, source_target_pairs={{0,2},{2,0},{1,3},{3,1},{4,6},{6,4},{5,7},{7,5}} | collective-permute-start | bytes 122888 | tf_op jit(solution)/shard_map/ppermute | solution.py:450
  3082.4 97.1 %collective-permute-start.14 = (bf16[1024,2048]{1,0:T(8,128)(2,1)}, bf16[1024,2048]{1,0:T(8,128)(2,1)}, u32[]{:S(2)}, u32[]{:S(2)}) collective-permute-start(bf16[1024,2048]{1,0:T(8,128)(2,1)} %get-tuple-element.138), channel_id=1, source_target_pairs={{0,2},{2,0},{1,3},{3,1},{4,6},{6,4},{5,7},{7,5}} | collective-permute-start | bytes 12582920 | tf_op jit(solution)/shard_map/ppermute | solution.py:450
Sparse Core Ops, SparseCore 0:
  9.5 30.0 all-gather.5
  71.4 72.6 all-gather.7
  512.8 153.1 all-gather.9
  790.3 153.1 all-gather.11
  944.9 103.1 all-gather.13
  1302.2 21.9 reduce-scatter.12
  1365.2 21.3 reduce-scatter.14
  1481.8 175.3 reduce-scatter.16
  1659.5 32.6 reduce-scatter.20
  1910.0 175.8 reduce-scatter.18
  2088.7 32.6 reduce-scatter.22

commit v2 on v1

--- a/solution.py
+++ b/solution.py
@@ -36,7 +36,7 @@
 
 
 def ln_fwd_body(col_ref, own_ref, recv_ref, g_ref, b_ref, *rest):
-    xn_ref = rest[-1]
+    xn_ref, stat_ref = rest[-2:]
     width = own_ref.shape[1]
     inv_n = 1.0 / (2 * width)
     col = col_ref[0]
@@ -54,6 +54,8 @@
             far = recv_ref[r, :].astype(F32) - mean
             invs.append(lax.rsqrt(row_sum(own * own + far * far) * inv_n + LN_EPS))
         for r, mean, inv in zip(groups, means, invs):
+            stat_ref[r, :128] = jnp.broadcast_to(mean, (step, 128))
+            stat_ref[r, 128:] = jnp.broadcast_to(inv, (step, 128))
             for src, cols in ((own_ref, own_cols), (recv_ref, far_cols)):
                 hat = (src[r, :].astype(F32) - mean) * inv
                 xn_ref[r, cols] = (hat * g_ref[:, cols] + b_ref[:, cols]).astype(BF16)
@@ -73,17 +75,17 @@
     args = [col, x_loc, x_recv, g_full, b_full]
     aliases = {}
     if prev is not None:
-        in_specs.append(pl.BlockSpec(memory_space=pl.ANY))
-        args.append(prev)
-        aliases = {5: 0}
+        in_specs.extend([pl.BlockSpec(memory_space=pl.ANY)] * 2)
+        args.extend(prev)
+        aliases = {5: 0, 6: 1}
     return pl.pallas_call(
         ln_fwd_body,
-        out_shape=jax.ShapeDtypeStruct((total, 2 * width), BF16),
+        out_shape=(jax.ShapeDtypeStruct((total, 2 * width), BF16), jax.ShapeDtypeStruct((total, 256), F32)),
         grid_spec=pltpu.PrefetchScalarGridSpec(
             num_scalar_prefetch=1,
             grid=(rows // blk,),
             in_specs=in_specs,
-            out_specs=pl.BlockSpec((blk, 2 * width), lambda i, c: (i + off, 0)),
+            out_specs=(pl.BlockSpec((blk, 2 * width), lambda i, c: (i + off, 0)), pl.BlockSpec((blk, 256), lambda i, c: (i + off, 0))),
         ),
         input_output_aliases=aliases,
         cost_estimate=pl.CostEstimate(flops=20 * rows * 2 * width, bytes_accessed=8 * rows * width, transcendentals=0),
@@ -91,90 +93,138 @@
     )(*args)
 
 
-def ln_bwd_body(col_ref, dxn_ref, own_ref, recv_ref, dy_own_ref, dy_recv_ref, g_ref, *rest):
-    dx_own_ref, dx_send_ref, dg_ref, db_ref = rest[-4:]
-    width = own_ref.shape[1]
-    inv_n = 1.0 / (2 * width)
-    col = col_ref[0]
-    own_cols = pl.ds(pl.multiple_of(col * width, width), width)
-    far_cols = pl.ds(pl.multiple_of((1 - col) * width, width), width)
-    step, unroll = 16, 8
-
-    @pl.when(pl.program_id(0) == 0)
-    def _():
-        dg_ref[...] = jnp.zeros_like(dg_ref)
-        db_ref[...] = jnp.zeros_like(db_ref)
+def ln_bwd_rows(dxn_ref, sides, stat_ref, g_ref, dg_ref, db_ref):
+    rows = dxn_ref.shape[0]
+    inv_n = 1.0 / dxn_ref.shape[1]
+    step, unroll = 16, 4
 
     def fold(val):
         return jnp.sum(val.reshape(val.shape[0] // 8, 8, val.shape[1]), axis=0)
 
-    @pl.loop(0, own_ref.shape[0] // (step * unroll))
+    @pl.loop(0, rows // (step * unroll))
     def _(i):
         groups = group_rows(i, unroll, step)
-        stats = []
+        full = []
         for r in groups:
-            mean = row_sum(own_ref[r, :].astype(F32) + recv_ref[r, :].astype(F32)) * inv_n
-            m1 = row_sum(dxn_ref[r, own_cols] * g_ref[:, own_cols] + dxn_ref[r, far_cols] * g_ref[:, far_cols]) * inv_n
-            stats.append((mean, m1))
-        full = []
-        for r, (mean, m1) in zip(groups, stats):
-            own = own_ref[r, :].astype(F32) - mean
-            far = recv_ref[r, :].astype(F32) - mean
-            var = row_sum(own * own + far * far) * inv_n
-            m2 = row_sum(dxn_ref[r, own_cols] * g_ref[:, own_cols] * own + dxn_ref[r, far_cols] * g_ref[:, far_cols] * far) * inv_n
-            inv = lax.rsqrt(var + LN_EPS)
-            full.append((mean, inv, m1, m2 * inv))
-        for src, dy, dx, cols in ((own_ref, dy_own_ref, dx_own_ref, own_cols), (recv_ref, dy_recv_ref, dx_send_ref, far_cols)):
+            mean, inv = stat_ref[r, 0:1], stat_ref[r, 128:129]
+            m1, m2 = 0.0, 0.0
+            for x_ref, _, _, cols in sides:
+                part = dxn_ref[r, cols] * g_ref[:, cols]
+                m1 = m1 + part
+                m2 = m2 + part * (x_ref[r, :].astype(F32) - mean)
+            full.append((mean, inv, row_sum(m1) * inv_n, row_sum(m2) * inv_n * inv))
+        for x_ref, dy_ref, dx_ref, cols in sides:
             sum_g = sum_b = None
             for r, (mean, inv, m1, m2) in zip(groups, full):
-                hat = (src[r, :].astype(F32) - mean) * inv
+                hat = (x_ref[r, :].astype(F32) - mean) * inv
                 d = dxn_ref[r, cols]
                 add_g, add_b = fold(d * hat), fold(d)
                 sum_g = add_g if sum_g is None else sum_g + add_g
                 sum_b = add_b if sum_b is None else sum_b + add_b
-                dx[r, :] = (dy[r, :].astype(F32) + inv * (d * g_ref[:, cols] - m1 - hat * m2)).astype(BF16)
+                dx_ref[r, :] = (dy_ref[r, :].astype(F32) + inv * (d * g_ref[:, cols] - m1 - hat * m2)).astype(BF16)
             dg_ref[:, cols] += sum_g
             db_ref[:, cols] += sum_b
 
 
-def ln_bwd(col, dxn, x_loc, x_recv, dy_loc, dy_recv, g_full, row0, total, dx_prev):
-    rows, width = dxn.shape[0], dy_recv.shape[1]
-    blk = 128
+def dx_body(row0, half, col_ref, d_own, d_a, d_b, w_own, w_a, w_b, x_ref, x0_ref, x1_ref, dy_ref, dyr_ref, stat_ref, g_ref, *rest):
+    dx_ref, send_ref, dg_ref, db_ref, acc, w_buf, d_buf, ln_buf, sems, ln_sems = rest[-10:]
+    m, steps = pl.program_id(0), pl.num_programs(0)
+    blk, wide = d_buf.shape[1:]
+    width = x_ref.shape[1]
+    col = col_ref[0]
+    sources, count = [], 0
+    for d, w in ((d_own, w_own), (d_a, w_a), (d_b, w_b)):
+        chunks = d.shape[1] // wide
+        sources.append((d, w, count, chunks))
+        count += chunks
+
+    def copies(d, w, block, chunk, slot):
+        rows = pl.ds(pl.multiple_of(row0 + block * blk, blk), blk)
+        cols = pl.ds(pl.multiple_of(chunk * wide, wide), wide)
+        return (
+            pltpu.make_async_copy(w.at[:, cols], w_buf.at[slot], sems.at[0, slot]),
+            pltpu.make_async_copy(d.at[rows, cols], d_buf.at[slot], sems.at[1, slot]),
+        )
+
+    def fetch(block, chunk, slot):
+        for d, w, lo, chunks in sources:
+            @pl.when((chunk >= lo) & (chunk < lo + chunks))
+            def _():
+                for copy in copies(d, w, block, chunk - lo, slot):
+                    copy.start()
+
+    @pl.when(m == 0)
+    def _():
+        dg_ref[...] = jnp.zeros_like(dg_ref)
+        db_ref[...] = jnp.zeros_like(db_ref)
+        fetch(0, 0, 0)
+
+    row = row0 + m * blk
+    own_rows = pl.ds(pl.multiple_of(col * half + row, blk), blk)
+    far_rows = pl.ds(pl.multiple_of(row, blk), blk)
+    pair = half // 2
+    x0_rows = pl.ds(pl.multiple_of(jnp.minimum(row, pair - blk), blk), blk)
+    x1_rows = pl.ds(pl.multiple_of(jnp.maximum(row - pair, 0), blk), blk)
+
+    def ln_copy(i, src):
+        return pltpu.make_async_copy(src, ln_buf.at[i], ln_sems.at[i])
+
+    ln_copy(0, x_ref.at[own_rows]).start()
+    ln_copy(2, dy_ref.at[own_rows]).start()
+    ln_copy(3, dyr_ref.at[far_rows]).start()
+
+    @pl.when(row < pair)
+    def _():
+        ln_copy(1, x0_ref.at[x0_rows]).start()
+
+    @pl.when(row >= pair)
+    def _():
+        ln_copy(1, x1_ref.at[x1_rows]).start()
+
+    acc[...] = jnp.zeros_like(acc)
+
+    @pl.loop(0, count)
+    def _(k):
+        slot = lax.rem(m * count + k, 2)
+
+        @pl.when(k + 1 < count)
+        def _():
+            fetch(m, k + 1, 1 - slot)
+
+        @pl.when((k + 1 == count) & (m + 1 < steps))
+        def _():
+            fetch(m + 1, 0, 1 - slot)
+
+        for copy in copies(d_a, w_a, 0, 0, slot):
+            copy.wait()
+        acc[...] += nt_dot(d_buf[slot], w_buf[slot])
+
+    for i in range(4):
+        ln_copy(i, dyr_ref.at[far_rows]).wait()
+    own_cols = pl.ds(pl.multiple_of(col * width, width), width)
+    far_cols = pl.ds(pl.multiple_of((1 - col) * width, width), width)
+    sides = ((ln_buf.at[0], ln_buf.at[2], dx_ref, own_cols), (ln_buf.at[1], ln_buf.at[3], send_ref, far_cols))
+    ln_bwd_rows(acc, sides, stat_ref, g_ref, dg_ref, db_ref)
+
+
+def dx_part(col, dqkv, weights, x_loc, x_recv, dy_loc, dy_recv, stats, g_full, row0, rows, dx_prev):
+    total, width = dy_recv.shape
+    blk, wide = 512, 1024
+    off = row0 // blk
     nall = total // blk
-    nblk = rows // blk
-    off = row0 // blk
     own_spec = pl.BlockSpec((blk, width), lambda i, c: (i + off + c[0] * nall, 0))
-    recv_spec = pl.BlockSpec((blk, width), lambda i, c: (i + off, 0))
-    npiece = x_recv[0].shape[0] // blk
-    x_specs = [pl.BlockSpec((blk, width), lambda i, c, p=p: (jnp.clip(i + off - p * npiece, 0, npiece - 1), 0)) for p in range(2)]
-    in_specs = [
-        pl.BlockSpec((blk, 2 * width), lambda i, c: (i, 0)),
-        own_spec,
-        *x_specs,
-        own_spec,
-        recv_spec,
-        pl.BlockSpec((1, 2 * width), lambda i, c: (0, 0)),
-    ]
-    args = [col, dxn, x_loc, *x_recv, dy_loc, dy_recv, g_full]
+    sums_spec = pl.BlockSpec((8, 2 * width), lambda i, c: (0, 0))
+    any_spec = pl.BlockSpec(memory_space=pl.ANY)
+    in_specs = [any_spec] * 11 + [pl.BlockSpec((blk, 256), lambda i, c: (i + off, 0)), pl.BlockSpec((1, 2 * width), lambda i, c: (0, 0))]
+    args = [col, *dqkv, *weights, x_loc, *x_recv, dy_loc, dy_recv, stats, g_full]
     aliases = {}
     if dx_prev is not None:
-        in_specs.append(pl.BlockSpec(memory_space=pl.ANY))
+        in_specs.append(any_spec)
         args.append(dx_prev)
-        aliases = {8: 0}
-
-    def body(col_ref, dxn_ref, own_ref, x0_ref, x1_ref, *rest):
-        late = pl.program_id(0) + off >= npiece
-
-        @pl.when(jnp.logical_not(late))
-        def _():
-            ln_bwd_body(col_ref, dxn_ref, own_ref, x0_ref, *rest)
-
-        @pl.when(late)
-        def _():
-            ln_bwd_body(col_ref, dxn_ref, own_ref, x1_ref, *rest)
-
+        aliases = {14: 0}
+    depth = sum(d.shape[1] for d in dqkv)
     return pl.pallas_call(
-        body,
+        functools.partial(dx_body, row0, total),
         out_shape=(
             jax.ShapeDtypeStruct((2 * total, width), BF16),
             jax.ShapeDtypeStruct((rows, width), BF16),
@@ -183,18 +233,22 @@
         ),
         grid_spec=pltpu.PrefetchScalarGridSpec(
             num_scalar_prefetch=1,
-            grid=(nblk,),
+            grid=(rows // blk,),
             in_specs=in_specs,
-            out_specs=(
-                own_spec,
-                pl.BlockSpec((blk, width), lambda i, c: (i, 0)),
-                pl.BlockSpec((8, 2 * width), lambda i, c: (0, 0)),
-                pl.BlockSpec((8, 2 * width), lambda i, c: (0, 0)),
-            ),
+            out_specs=(own_spec, pl.BlockSpec((blk, width), lambda i, c: (i, 0)), sums_spec, sums_spec),
+            scratch_shapes=[
+                pltpu.VMEM((blk, 2 * width), F32),
+                pltpu.VMEM((2, 2 * width, wide), BF16),
+                pltpu.VMEM((2, blk, wide), BF16),
+                pltpu.VMEM((4, blk, width), BF16),
+                pltpu.SemaphoreType.DMA((2, 2)),
+                pltpu.SemaphoreType.DMA((4,)),
+            ],
         ),
         input_output_aliases=aliases,
-        cost_estimate=pl.CostEstimate(flops=40 * rows * 2 * width, bytes_accessed=20 * rows * width, transcendentals=0),
-        name="ln_bwd",
+        compiler_params=pltpu.CompilerParams(vmem_limit_bytes=60 * 1024 * 1024),
+        cost_estimate=pl.CostEstimate(flops=4 * rows * width * depth, bytes_accessed=(rows // blk) * 4 * width * depth, transcendentals=0),
+        name="dx_part",
     )(*args)
 
 
@@ -342,41 +396,34 @@
     )(*args)
 
 
-def assemble_body(pos_ref, own_ref, recv_ref, out_ref):
-    half = pl.num_programs(0) // 2
-    mine = (pl.program_id(0) // half) == pos_ref[0]
-
-    @pl.when(mine)
-    def _():
-        out_ref[...] = own_ref[...]
-
-    @pl.when(jnp.logical_not(mine))
-    def _():
-        out_ref[...] = recv_ref[...]
-
-
-def assemble(pos, own, recv, blk):
-    rows, width = own.shape
-    half = rows // blk
-
-    def own_map(i, p):
-        return (jnp.clip(i - p[0] * half, 0, half - 1), 0)
-
-    def recv_map(i, p):
-        return (jnp.clip(i - (1 - p[0]) * half, 0, half - 1), 0)
-
+def out_body(col_ref, att_ref, w_ref, x_ref, b_ref, out_ref):
+    out_ref[...] = (x_ref[...].astype(F32) + nn_dot(att_ref[...], w_ref[...]) + b_ref[...]).astype(BF16)
+
+
+def out_rows(col, att, w_o, x_loc, bias):
+    tokens, full = att.shape
+    width = w_o.shape[1]
+    blk, wide = 1024, 1024
+    nblk = tokens // blk
+    place = pl.BlockSpec((blk, wide), lambda n, m, c: (m + c[0] * nblk, n))
     return pl.pallas_call(
-        assemble_body,
-        out_shape=jax.ShapeDtypeStruct((2 * rows, width), own.dtype),
+        out_body,
+        out_shape=jax.ShapeDtypeStruct((2 * tokens, width), BF16),
         grid_spec=pltpu.PrefetchScalarGridSpec(
             num_scalar_prefetch=1,
-            grid=(2 * half,),
-            in_specs=[pl.BlockSpec((blk, width), own_map), pl.BlockSpec((blk, width), recv_map)],
-            out_specs=pl.BlockSpec((blk, width), lambda i, p: (i, 0)),
+            grid=(width // wide, nblk),
+            in_specs=[
+                pl.BlockSpec((blk, full), lambda n, m, c: (m, 0)),
+                pl.BlockSpec((full, wide), lambda n, m, c: (0, n)),
+                place,
+                pl.BlockSpec((1, wide), lambda n, m, c: (0, n)),
+            ],
+            out_specs=place,
         ),
-        cost_estimate=pl.CostEstimate(flops=rows * width, bytes_accessed=8 * rows * width, transcendentals=0),
-        name="assemble",
-    )(pos, own, recv)
+        compiler_params=pltpu.CompilerParams(vmem_limit_bytes=56 * 1024 * 1024),
+        cost_estimate=pl.CostEstimate(flops=2 * tokens * full * width, bytes_accessed=4 * tokens * full, transcendentals=0),
+        name="out_rows",
+    )(col, att, w_o, x_loc, bias)
 
 
 def regroup_body(src_ref, out_ref):
@@ -400,10 +447,10 @@
     )(val)
 
 
-def join_body(pos_ref, own_ref, recv_ref, half_ref, rest_ref, out_ref):
+def join_body(side, pos_ref, own_ref, recv_ref, half_ref, rest_ref, *rest):
+    out_ref = rest[-1]
     wide = own_ref.shape[1] // 3
-    steps = pl.num_programs(0) // 2
-    mine = (pl.program_id(0) // steps) == pos_ref[0]
+    mine = pos_ref[0] == side
 
     def cols(t, j):
         return pl.ds((2 * t + j) * wide, wide)
@@ -419,25 +466,33 @@
         out_ref[:, cols(t, 1)] = (half_ref[:, part].astype(F32) + rest_ref[:, part].astype(F32)).astype(BF16)
 
 
-def join(pos, own, recv, half, rest):
+def join(side, pos, own, recv, half, rest, prev):
     rows, width = own.shape
     blk = 128
     steps = rows // blk
-    own_spec = pl.BlockSpec((blk, width), lambda i, p: (jnp.clip(i - p[0] * steps, 0, steps - 1), 0))
-    recv_spec = pl.BlockSpec((blk, width), lambda i, p: (jnp.clip(i - (1 - p[0]) * steps, 0, steps - 1), 0))
+    own_spec = pl.BlockSpec((blk, width), lambda i, p: (jnp.where(p[0] == side, i, 0), 0))
+    recv_spec = pl.BlockSpec((blk, width), lambda i, p: (jnp.where(p[0] == side, 0, i), 0))
     full_spec = pl.BlockSpec((blk, width), lambda i, p: (i, 0))
+    in_specs = [own_spec, recv_spec, full_spec, full_spec]
+    args = [pos, own, recv, half, rest]
+    aliases = {}
+    if prev is not None:
+        in_specs.append(pl.BlockSpec(memory_space=pl.ANY))
+        args.append(prev)
+        aliases = {5: 0}
     return pl.pallas_call(
-        join_body,
+        functools.partial(join_body, side),
         out_shape=jax.ShapeDtypeStruct((2 * rows, 2 * width), BF16),
         grid_spec=pltpu.PrefetchScalarGridSpec(
             num_scalar_prefetch=1,
-            grid=(2 * steps,),
-            in_specs=[own_spec, recv_spec, full_spec, full_spec],
-            out_specs=pl.BlockSpec((blk, 2 * width), lambda i, p: (i, 0)),
+            grid=(steps,),
+            in_specs=in_specs,
+            out_specs=pl.BlockSpec((blk, 2 * width), lambda i, p: (i + side * steps, 0)),
         ),
-        cost_estimate=pl.CostEstimate(flops=rows * width, bytes_accessed=20 * rows * width, transcendentals=0),
+        input_output_aliases=aliases,
+        cost_estimate=pl.CostEstimate(flops=rows * width, bytes_accessed=10 * rows * width, transcendentals=0),
         name="join",
-    )(pos, own, recv, half, rest)
+    )(*args)
 
 
 def solution(mesh):
@@ -490,9 +545,10 @@
         nb = hw // 128
         bias = jnp.concatenate([b_qkv[(2 * t + j) * nb:(2 * t + j + 1) * nb] for j in range(2) for t in range(3)], axis=0)
         vecs = jnp.concatenate([ln_g.reshape(-1, 128), ln_b.reshape(-1, 128), b_o.reshape(-1, 128), bias], axis=0)
-        vecs_r = send(vecs)
         rows2 = half // 2
         x_out = [lax.dynamic_slice_in_dim(x2, other * half, rows2, 0)]
+        vecs = tie(vecs, x_out[0])
+        vecs_r = send(vecs)
         slab_a = tie(slab(0), x_out[0])
         x_out.append(lax.dynamic_slice_in_dim(tie(x2, slab_a), other * half + rows2, rows2, 0))
         slab_b = tie(slab(1), x_out[1])
@@ -511,6 +567,26 @@
         nv = width // 128
         first = col == 0
 
+        db_o = jnp.sum(dy2.astype(F32), axis=0)
+        wq_oth = [None, None]
+        qkv_oth = [None, None]
+        dqkv_oth = [None, None]
+        sum_oth = [None, None]
+
+        def held(*vals):
+            return lax.optimization_barrier(vals)
+
+        def project(j):
+            return (nn_dot(xn, wq_oth[j]) + bq_oth[j]).astype(BF16)
+
+        def weight_grad(lhs, rhs):
+            return tn_dot(lhs, rhs).astype(BF16)
+
+        dy_own = lax.dynamic_slice_in_dim(tie(dy2, dy_out), col * half, half, 0)
+        datt_part = nt_dot(tie(dy_own, w_perm), wo_own)
+
+        vecs_r = tie(vecs_r, datt_part)
+
         def both(lo, hi):
             a = vecs[lo:hi].reshape(1, -1)
             b = vecs_r[lo:hi].reshape(1, -1)
@@ -521,29 +597,12 @@
         bo_oth = vecs_r[2 * nv:3 * nv].reshape(-1)
         bq_own = bias.reshape(-1)
         bq_oth = vecs_r[3 * nv:].reshape(2, 3 * hw)
-        db_o = jnp.sum(dy2.astype(F32), axis=0)
-        wq_oth = [None, None]
-        qkv_oth = [None, None]
-        dqkv_oth = [None, None]
-        sum_oth = [None, None]
-
-        def held(*vals):
-            return lax.optimization_barrier(vals)
-
-        def project(j):
-            return (nn_dot(xn, wq_oth[j]) + bq_oth[j]).astype(BF16)
-
-        def weight_grad(lhs, rhs):
-            return tn_dot(lhs, rhs).astype(BF16)
-
-        dy_own = lax.dynamic_slice_in_dim(tie(dy2, dy_out), col * half, half, 0)
-        datt_part = nt_dot(tie(dy_own, w_perm), wo_own)
-
-        xn = ln_fwd(col_arr, tie(x2, datt_part), x_recv[0], g_full, b_full, 0, half, None)
+
+        xn, stats = ln_fwd(col_arr, tie(x2, datt_part, db_o), x_recv[0], g_full, b_full, 0, half, None)
         qkv_own = [(nn_dot(xn[:rows2], w_own) + bq_own).astype(BF16)]
         wa_in, xn, qkv_own[0] = held(wa_in, xn, qkv_own[0])
         wq_oth[0] = gather(wa_in, ("row", "depth"))
-        xn = ln_fwd(col_arr, x2, x_recv[1], g_full, b_full, rows2, half, xn)
+        xn, stats = ln_fwd(col_arr, x2, x_recv[1], g_full, b_full, rows2, half, (xn, stats))
         qkv_own.append((nn_dot(xn[rows2:], w_own) + bq_own).astype(BF16))
         att = None
         for i in range(2):
@@ -559,8 +618,7 @@
         x_all = jnp.concatenate(x_recv, axis=0)
         y_send = (x_all.astype(F32) + nn_dot(att, wo_oth) + bo_oth).astype(BF16)
         y_recv = send(y_send)
-        x_own = lax.dynamic_slice_in_dim(tie(x2, y_send), col * half, half, 0)
-        y_own = (x_own.astype(F32) + nn_dot(att, wo_own) + b_o).astype(BF16)
+        y = out_rows(col_arr, tie(att, y_send), wo_own, x2, b_o.reshape(1, -1))
 
         def back_far(j, gate):
             dqkv_oth[j], sum_oth[j] = attn_bwd(oth_grp[j], tie(qkv_oth[j], gate), d_att, 0, 1, hw, seq, 0, half, None)
@@ -574,7 +632,7 @@
 
         wide = 3 * hw
         sum_own = [None, None]
-        d_att = (nt_dot(tie(dy_recv, y_own), wo_oth) + datt_part).astype(BF16)
+        d_att = (nt_dot(tie(dy_recv, y), wo_oth) + datt_part).astype(BF16)
         dwo_far = weight_grad(tie(att, d_att), dy_recv)
         red_of = scatter(dwo_far, "row")
         back_far(0, dwo_far)
@@ -600,46 +658,60 @@
         dw_ob = weight_grad(xn, dqkv_own[:, wide:])
         red_ob = scatter(dw_ob, "row")
 
-        parts = (half // 3,) * 3
-        dx, gate = None, dw_ob
+        unit = half // 6
+        parts = (unit, unit, 2 * unit, unit, unit)
+        dx, gate, lo = None, dw_ob, 0
         dx_recv, sums_n = [], []
-        for part in range(len(parts)):
-            lo, rows = part * parts[0], parts[part]
-            dxn = nt_dot(tie(dqkv_own, gate)[lo:lo + rows], w_own)
-            if part == 0:
-                far_a, red_oa, dxn = held(far_a, red_oa, dxn)
-                half_a = (red_oa.astype(F32) + far_a.astype(F32)).astype(BF16)
-                rest_a = send(half_a, "depth")
-                dxn = tie(dxn, half_a)
-            dxn = nt_dot(dqkv_oth[0][lo:lo + rows], wq_oth[0]) + dxn
-            if part == 0:
-                far_b, red_ob, dxn = held(far_b, red_ob, dxn)
-                half_b = (red_ob.astype(F32) + far_b.astype(F32)).astype(BF16)
-                rest_b = send(half_b, "depth")
-                dxn = tie(dxn, half_b)
-            dxn = nt_dot(dqkv_oth[1][lo:lo + rows], wq_oth[1]) + dxn
-            dx, dx_send, dg8, db8 = ln_bwd(col_arr, dxn, x2, x_recv, dy2, dy_recv, g_full, lo, half, dx)
+        grads = [dqkv_own, *dqkv_oth]
+        for part, rows in enumerate(parts):
+            grads[1] = tie(grads[1], gate)
+            dx, dx_send, dg8, db8 = dx_part(col_arr, grads, (w_own, *wq_oth), x2, x_recv, dy2, dy_recv, stats, g_full, lo, rows, dx)
+            lo += rows
             sums_n.append((dg8, db8))
             dx_recv.append(send(dx_send))
             gate = dx_send
-        y = assemble(col_arr, y_own, tie(y_recv, gate), 256)
-        dw_o = (tie(half_o, y).astype(F32) + half_r.astype(F32)).astype(BF16)
-        dw_qkv = join(dep_arr, half_a, tie(rest_a, dw_o), half_b, rest_b)
-        dg8 = sum(pair[0] for pair in sums_n)
-        db8 = sum(pair[1] for pair in sums_n)
+            if part == 0:
+                far_a, red_oa, gate = held(far_a, red_oa, gate)
+                half_a = (red_oa.astype(F32) + far_a.astype(F32)).astype(BF16)
+                rest_a = send(half_a, "depth")
+                gate = half_a
+            if part == 1:
+                far_b, red_ob, gate = held(far_b, red_ob, gate)
+                half_b, rest_b = [], []
+                for i in range(2):
+                    part_rows = slice(i * piece, (i + 1) * piece)
+                    half_b.append((tie(red_ob, gate)[part_rows].astype(F32) + far_b[part_rows].astype(F32)).astype(BF16))
+                    rest_b.append(send(half_b[i], "depth"))
+                    gate = half_b[i]
 
         def natural(pair):
             vals = [jnp.sum(s, axis=0).reshape(3, hw) for s in pair]
             return jnp.concatenate([vals[j][t] for t in range(3) for j in range(2)])
 
-        dg = jnp.sum(dg8, axis=0)
-        dbn = jnp.sum(db8, axis=0)
+        dg = jnp.sum(sum(pair[0] for pair in sums_n), axis=0)
+        dbn = jnp.sum(sum(pair[1] for pair in sums_n), axis=0)
         far = jnp.concatenate([natural(sum_oth), lax.dynamic_slice_in_dim(dg, other * width, width), lax.dynamic_slice_in_dim(dbn, other * width, width)])
         near = jnp.concatenate([natural(sum_own), lax.dynamic_slice_in_dim(dg, col * width, width), lax.dynamic_slice_in_dim(dbn, col * width, width)])
-        total = near.reshape(-1, 128) + send(far.reshape(-1, 128))
-        total, db_o = lax.psum((total, db_o), ("depth", "row"))
-        for part in range(len(parts)):
-            dx = lax.dynamic_update_slice(dx, tie(dx_recv[part], dw_o if part < 2 else dw_qkv), (other * half + part * parts[0], 0))
+        near = near.reshape(-1, 128)
+        far = send(far.reshape(-1, 128))
+        y = lax.dynamic_update_slice(y, tie(y_recv, gate), (other * half, 0))
+        far, y = held(far, y)
+        total = jnp.concatenate([near + far, db_o.reshape(-1, 128)], axis=0)
+        row_in = send(total, "row")
+        dw_o = (tie(half_o, y, total).astype(F32) + half_r.astype(F32)).astype(BF16)
+        row_in, dw_o = held(row_in, dw_o)
+        total = total + row_in
+        dep_in = send(total, "depth")
+        place, lo = dw_o, 0
+        for part, rows in enumerate(parts):
+            if part == 3:
+                dw_qkv = join(0, dep_arr, half_a, tie(rest_a, dx), half_b[0], rest_b[0], None)
+                dw_qkv = join(1, dep_arr, half_a, rest_a, half_b[1], rest_b[1], dw_qkv)
+                place = dw_qkv
+            dx = lax.dynamic_update_slice(dx, tie(dx_recv[part], place), (other * half + lo, 0))
+            lo += rows
+        total = total + tie(dep_in, dx)
+        db_o = total[-nv:]
         nq = 3 * nv
         return (
             y.reshape(x.shape),
@@ -647,9 +719,9 @@
             dw_qkv,
             total[:nq],
             dw_o,
-            db_o,
+            db_o.reshape(-1),
             total[nq:nq + nv].reshape(-1),
-            total[nq + nv:].reshape(-1),
+            total[nq + nv:nq + 2 * nv].reshape(-1),
         )
 
     return jax.shard_map(

time: 3200 us -> 3470 us (1.084)
  matrix products: 1490 us -> 1030 us
  Pallas kernels: 358 us -> 741 us
  waiting for transfers between devices: 1160 us -> 1480 us
    dot_general x11 -> x2, matrix products: 526 us -> 128 us  [nt_dot(): lax.dot_general(lhs, rhs, (((1,), (1,)), ((), ())), preferred_element_typ...]
    pallas_call x7 -> x10, Pallas kernels: 151 us -> 534 us  [the longest x5 416 us: dx_part(): pl.pallas_call(functools.partial(dx_body, row0, total), out_shape=(jax.Sh...]
    ppermute x18 -> x23, waiting for transfers between devices: 1120 us -> 1440 us  [swap(): return lax.ppermute(val, axis, SWAP)]
    dot_general x6 -> x5, matrix products: 486 us -> 425 us  [nn_dot(): lax.dot_general(lhs, rhs, (((1,), (0,)), ((), ())), preferred_element_typ...]
  transfers between devices with their start and end apart: 29 -> 34, of which waited for: 7 -> 11; matrix products, arithmetic and copies ran while one was open for 47% -> 31% of each run, Pallas kernels for 11% -> 21%
where the time goes in v2:
time: 3470 us; the launch traced here: 3460 us
  waiting for transfers between devices  1480 us (43%)
  matrix products  1030 us (30%)
  Pallas kernels  741 us (21%)
  local copies, waits for them, and re-layouts  92.6 us (3%)
  other arithmetic  77.9 us (2%)
    ppermute x23, waiting for transfers between devices, swap(): return lax.ppermute(val, axis, SWAP)  1440 us
    dot_general x6, matrix products, tn_dot(): lax.dot_general(lhs, rhs, (((0,), (0,)), ((), ())), preferred_element_typ...  477 us
    dot_general x5, matrix products, nn_dot(): lax.dot_general(lhs, rhs, (((1,), (0,)), ((), ())), preferred_element_typ...  425 us
    pallas_call x5, Pallas kernels, dx_part(): pl.pallas_call(functools.partial(dx_body, row0, total), out_shape=(jax.Sh...  416 us
    dot_general x2, matrix products, nt_dot(): lax.dot_general(lhs, rhs, (((1,), (1,)), ((), ())), preferred_element_typ...  128 us
    pallas_call x6, Pallas kernels, attn_bwd(): pl.pallas_call(functools.partial(attn_bwd_body, heads, 128 ** (-0.5)), ou...  119 us
    pallas_call x4, Pallas kernels, attn_fwd(): pl.pallas_call(functools.partial(attn_fwd_body, heads, 128 ** (-0.5)), ou...  69.7 us
  transfers between devices with their start and end apart: 34, of which 11 were waited for; matrix products, arithmetic and copies ran while one was open for 31% of the time, Pallas kernels for 21%

profile of v2, /device:TPU:0, one launch (start us, length us, event | category | flops | bytes accessed | tf_op | source)
XLA Modules:
  0.0 3457.7 jit_solution(9941907985160110118)
XLA Ops:
  8.0 5.4 constant_dynamic-slice_fusion
  13.4 8.9 constant_dynamic-slice_fusion.5
  22.3 6.7 pad_maximum_fusion
  29.0 8.4 constant_dynamic-slice_fusion.4
  37.4 4.7 constant_dynamic-slice_fusion.3
  42.1 10.7 constant_dynamic-slice_fusion.2
  52.8 18.3 regroup.1
  71.2 3.1 collective-permute-start.3
  79.7 2.0 collective-permute-start.2
  81.7 14.1 constant_dynamic-slice_fusion.1
  95.8 16.8 convert_reduce_fusion
  112.6 64.7 %fusion.5 = f32[3072,4096]{1,0:T(8,128)} fusion(bf16[3072,2048]{1,0:T(8,128)(2,1)} %constant_dynamic-slice_fusion.1, bf16[4096,2048]{1,0:T(8,128)(2,1)} %all-gather.6.cloned.1.call-done.w_ref), kind=kOutput, calls=%fused_computation.86 | convolution fusion | flops 51539607552 | bytes 79691776 | tf_op jit(solution)/shard_map/dot_general | solution.py:19
  177.3 168.8 %collective-permute-done.2 = f32[96,128]{1,0:T(8,128)} collective-permute-done((f32[96,128]{1,0:T(8,128)}, f32[96,128]{1,0:T(8,128)}, u32[]{:S(2)}, u32[]{:S(2)}) %collective-permute-start.2) | collective-permute-done | bytes 49184 | tf_op jit(solution)/shard_map/ppermute | solution.py:505
  348.7 15.5 ln_fwd.2
  364.2 88.8 %add_convert_fusion.4.q_ref.k_ref.v_ref = bf16[1536,6144]{1,0:T(8,128)(2,1)} fusion(bf16[4096,6144]{1,0:T(8,128)(2,1)} %all-gather.8.cloned.1.call-done.w_own, f32[6144]{0:T(1024)S(1)} %bitcast.90, bf16[3072,4096]{1,0:T(8,128)(2,1)} %get-tuple-element.115.rest_0_), kind=kOutput, calls=%fused_computation.5 | convolution fusion | flops 77328285696 | bytes 81813504 | tf_op jit(solution)/shard_map/dot_general | solution.py:27
  455.1 136.7 %collective-permute-done.1.recv_ref.x1_ref = bf16[1536,2048]{1,0:T(8,128)(2,1)} collective-permute-done((bf16[1536,2048]{1,0:T(8,128)(2,1)}, bf16[1536,2048]{1,0:T(8,128)(2,1)}, u32[]{:S(2)}, u32[]{:S(2)}) %collective-permute-start.1) | collective-permute-done | bytes 6291488 | tf_op jit(solution)/shard_map/ppermute | solution.py:505
  591.8 15.6 ln_fwd.3
  607.5 88.7 %add_convert_fusion.3.q_ref.k_ref.v_ref = bf16[1536,6144]{1,0:T(8,128)(2,1)} fusion(bf16[4096,6144]{1,0:T(8,128)(2,1)} %all-gather.8.cloned.1.call-done.w_own, f32[6144]{0:T(1024)S(1)} %bitcast.91, bf16[3072,4096]{1,0:T(8,128)(2,1)} %get-tuple-element.123), kind=kOutput, calls=%fused_computation.4 | convolution fusion | flops 77328285696 | bytes 81813504 | tf_op jit(solution)/shard_map/dot_general | solution.py:27
  696.1 17.4 attn_fwd.4.rest_0_
  713.5 17.4 attn_fwd.5.rest_0_
  734.2 92.9 %add_convert_fusion.2.q_ref.k_ref.v_ref = bf16[3072,3072]{1,0:T(8,128)(2,1)} fusion(f32[3072]{0:T(1024)S(1)} %get-tuple-element.213, bf16[3072,4096]{1,0:T(8,128)(2,1)} %get-tuple-element.123, bf16[4096,3072]{1,0:T(8,128)(2,1)} %all-gather.10.cloned.1.call-done.w_a), kind=kOutput, calls=%fused_computation.3 | convolution fusion | flops 77328285696 | bytes 69218304 | tf_op jit(solution)/shard_map/dot_general | solution.py:27
  827.1 17.4 attn_fwd.6.rest_0_
  844.7 39.8 %all-gather.12.cloned.1.call-done.w_b = bf16[4096,3072]{1,0:T(8,128)(2,1)} async-done(((bf16[1024,3072]{1,0:T(8,128)(2,1)}), bf16[4096,3072]{1,0:T(8,128)(2,1)}) %all-gather.12.cloned.1.call-update) | async-done | bytes 25165840 | tf_op jit(solution)/shard_map/all_gather | solution.py:511
  884.4 90.3 %add_convert_fusion.1.q_ref.k_ref.v_ref = bf16[3072,3072]{1,0:T(8,128)(2,1)} fusion(f32[3072]{0:T(1024)S(1)} %copy-done.17, bf16[3072,4096]{1,0:T(8,128)(2,1)} %get-tuple-element.123, bf16[4096,3072]{1,0:T(8,128)(2,1)} %all-gather.12.cloned.1.call-done.w_b), kind=kOutput, calls=%fused_computation.2 | convolution fusion | flops 77328285696 | bytes 69218304 | tf_op jit(solution)/shard_map/dot_general | solution.py:27
  974.7 17.4 attn_fwd.7.att_ref
  992.2 63.8 %add_convert_fusion.5 = bf16[3072,2048]{1,0:T(8,128)(2,1)} fusion(bf16[1536,2048]{1,0:T(8,128)(2,1)} %collective-permute-done.1.recv_ref.x1_ref, bf16[1536,2048]{1,0:T(8,128)(2,1)} %collective-permute-done.4.recv_ref.x0_ref, f32[2048]{0:T(1024)S(1)} %copy-done.18, bf16[3072,4096]{1,0:T(8,128)(2,1)} %attn_fwd.7.att_ref, ...), kind=kOutput, calls=%fused_computation.6 | convolution fusion | flops 51583647744 | bytes 67117056 | tf_op jit(solution)/shard_map/dot_general | solution.py:27
  1056.0 60.8 %out_rows.1 = bf16[6144,2048]{1,0:T(8,128)(2,1)} custom-call(s32[1]{0:T(128)} %bitcast.2.col_ref, bf16[3072,4096]{1,0:T(8,128)(2,1)} %attn_fwd.7.att_ref, bf16[4096,2048]{1,0:T(8,128)(2,1)} %all-gather.6.cloned.1.call-done.w_ref, bf16[6144,2048]{1,0:T(8,128)(2,1)} %bitcast.69, f32[1,2048]{1,0:T(1,128)} %bitcast.89), custom_call_target="tpu_custom_call" | custom-call | flops 51539607552 | bytes 50331648 | tf_op jit(solution)/shard_map/out_rows/pallas_call | solution.py:409
  1116.7 63.1 %add_convert_fusion.d_ref = bf16[3072,4096]{1,0:T(8,128)(2,1)} fusion(f32[3072,4096]{1,0:T(8,128)} %fusion.5, bf16[3072,2048]{1,0:T(8,128)(2,1)} %collective-permute-done.6.dyr_ref, bf16[4096,2048]{1,0:T(8,128)(2,1)} %all-gather.14.cloned.1.call-done), kind=kOutput, calls=%fused_computation | convolution fusion | flops 51564773376 | bytes 104857600 | tf_op jit(solution)/shard_map/dot_general | solution.py:19
  1179.8 61.3 %convolution_convert_fusion.5 = bf16[4096,2048]{1,0:T(8,128)(2,1)} fusion(bf16[3072,4096]{1,0:T(8,128)(2,1)} %attn_fwd.7.att_ref, bf16[3072,2048]{1,0:T(8,128)(2,1)} %collective-permute-done.6.dyr_ref), kind=kOutput, calls=%fused_computation.16 | convolution fusion | flops 51547996160 | bytes 54525952 | tf_op jit(solution)/shard_map/dot_general | solution.py:23
  1241.1 63.3 %convolution_convert_fusion.4 = bf16[4096,2048]{1,0:T(8,128)(2,1)} fusion(bf16[3072,4096]{1,0:T(8,128)(2,1)} %attn_fwd.7.att_ref, bf16[3072,2048]{1,0:T(8,128)(2,1)} %constant_dynamic-slice_fusion.1), kind=kOutput, calls=%fused_computation.15 | convolution fusion | flops 51547996160 | bytes 54525952 | tf_op jit(solution)/shard_map/dot_general | solution.py:23
  1304.6 28.5 attn_bwd.6
  1333.0 88.0 %convolution_convert_fusion.2 = bf16[4096,3072]{1,0:T(8,128)(2,1)} fusion(bf16[3072,4096]{1,0:T(8,128)(2,1)} %get-tuple-element.123, bf16[3072,3072]{1,0:T(8,128)(2,1)} %get-tuple-element.171.d_a), kind=kOutput, calls=%fused_computation.9 | convolution fusion | flops 77321994240 | bytes 69206016 | tf_op jit(solution)/shard_map/dot_general | solution.py:23
  1421.1 29.8 attn_bwd.7
  1450.9 88.3 %convolution_convert_fusion.3 = bf16[4096,3072]{1,0:T(8,128)(2,1)} fusion(bf16[3072,4096]{1,0:T(8,128)(2,1)} %get-tuple-element.123, bf16[3072,3072]{1,0:T(8,128)(2,1)} %get-tuple-element.134.d_b), kind=kOutput, calls=%fused_computation.10 | convolution fusion | flops 77321994240 | bytes 69206016 | tf_op jit(solution)/shard_map/dot_general | solution.py:23
  1540.2 181.7 %collective-permute-done.7 = bf16[2048,2048]{1,0:T(8,128)(2,1)} collective-permute-done((bf16[2048,2048]{1,0:T(8,128)(2,1)}, bf16[2048,2048]{1,0:T(8,128)(2,1)}, u32[]{:S(2)}, u32[]{:S(2)}) %collective-permute-start.7) | collective-permute-done | bytes 8388640 | tf_op jit(solution)/shard_map/ppermute | solution.py:505
  1721.9 10.6 add_convert_fusion.7
  1732.5 14.4 attn_bwd.8
  1746.9 14.4 attn_bwd.9
  1761.3 88.1 %convolution_convert_fusion.1 = bf16[4096,3072]{1,0:T(8,128)(2,1)} fusion(bf16[3072,4096]{1,0:T(8,128)(2,1)} %get-tuple-element.123, bf16[3072,6144]{1,0:T(8,128)(2,1)} %get-tuple-element.142.rest_0_), kind=kOutput, calls=%fused_computation.8 | convolution fusion | flops 77321994240 | bytes 69206016 | tf_op jit(solution)/shard_map/dot_general | solution.py:23
  1849.5 16.4 attn_bwd.10
  1865.8 15.6 attn_bwd.11
  1881.4 88.5 %convolution_convert_fusion = bf16[4096,3072]{1,0:T(8,128)(2,1)} fusion(bf16[3072,4096]{1,0:T(8,128)(2,1)} %get-tuple-element.123, bf16[3072,6144]{1,0:T(8,128)(2,1)} %get-tuple-element.147.d_own), kind=kOutput, calls=%fused_computation.7 | convolution fusion | flops 77321994240 | bytes 69206016 | tf_op jit(solution)/shard_map/dot_general | solution.py:23
  1973.1 71.1 %dx_part.5 = (bf16[6144,2048]{1,0:T(8,128)(2,1)}, bf16[512,2048]{1,0:T(8,128)(2,1)}, f32[8,4096]{1,0:T(8,128)}, f32[8,4096]{1,0:T(8,128)}) custom-call(s32[1]{0:T(128)} %bitcast.2.col_ref, bf16[3072,6144]{1,0:T(8,128)(2,1)} %get-tuple-element.147.d_own, bf16[3072,3072]{1,0:T(8,128)(2,1)} %get-tuple-element.171.d_a, ...), custom_call_target="tpu_custom_call" | custom-call | flops 51539607552 | bytes 100663296 | tf_op jit(solution)/shard_map/dx_part/pallas_call | solution.py:226
  2049.1 598.9 %collective-permute-done.8 = bf16[1024,3072]{1,0:T(8,128)(2,1)} collective-permute-done((bf16[1024,3072]{1,0:T(8,128)(2,1)}, bf16[1024,3072]{1,0:T(8,128)(2,1)}, u32[]{:S(2)}, u32[]{:S(2)}) %collective-permute-start.8) | collective-permute-done | bytes 6291488 | tf_op jit(solution)/shard_map/ppermute | solution.py:505
  2648.0 10.1 add_convert_fusion.10.own_ref
  2658.0 70.4 %dx_part.6 = (bf16[6144,2048]{1,0:T(8,128)(2,1)}, bf16[512,2048]{1,0:T(8,128)(2,1)}, f32[8,4096]{1,0:T(8,128)}, f32[8,4096]{1,0:T(8,128)}) custom-call(s32[1]{0:T(128)} %bitcast.2.col_ref, bf16[3072,6144]{1,0:T(8,128)(2,1)} %get-tuple-element.147.d_own, bf16[3072,3072]{1,0:T(8,128)(2,1)} %get-tuple-element.171.d_a, ...), custom_call_target="tpu_custom_call", output_to_operand_aliasing={{0}: (14, {})} | custom-call | flops 51539607552 | bytes 100663296 | tf_op jit(solution)/shard_map/dx_part/pallas_call | solution.py:226
  2728.5 9.7 add_convert_fusion.9.half_ref
  2739.1 8.1 add_convert_fusion.8.half_ref
  2747.2 133.9 %dx_part.7 = (bf16[6144,2048]{1,0:T(8,128)(2,1)}, bf16[1024,2048]{1,0:T(8,128)(2,1)}, f32[8,4096]{1,0:T(8,128)}, f32[8,4096]{1,0:T(8,128)}) custom-call(s32[1]{0:T(128)} %bitcast.2.col_ref, bf16[3072,6144]{1,0:T(8,128)(2,1)} %get-tuple-element.147.d_own, bf16[3072,3072]{1,0:T(8,128)(2,1)} %get-tuple-element.171.d_a, ...), custom_call_target="tpu_custom_call", output_to_operand_aliasing={{0}: (14, {})} | custom-call | flops 103079215104 | bytes 201326592 | tf_op jit(solution)/shard_map/dx_part/pallas_call | solution.py:226
  2881.5 70.2 %dx_part.8 = (bf16[6144,2048]{1,0:T(8,128)(2,1)}, bf16[512,2048]{1,0:T(8,128)(2,1)}, f32[8,4096]{1,0:T(8,128)}, f32[8,4096]{1,0:T(8,128)}) custom-call(s32[1]{0:T(128)} %bitcast.2.col_ref, bf16[3072,6144]{1,0:T(8,128)(2,1)} %get-tuple-element.147.d_own, bf16[3072,3072]{1,0:T(8,128)(2,1)} %get-tuple-element.171.d_a, ...), custom_call_target="tpu_custom_call", output_to_operand_aliasing={{0}: (14, {})} | custom-call | flops 51539607552 | bytes 100663296 | tf_op jit(solution)/shard_map/dx_part/pallas_call | solution.py:226
  2951.8 70.4 %dx_part.9 = (bf16[6144,2048]{1,0:T(8,128)(2,1)}, bf16[512,2048]{1,0:T(8,128)(2,1)}, f32[8,4096]{1,0:T(8,128)}, f32[8,4096]{1,0:T(8,128)}) custom-call(s32[1]{0:T(128)} %bitcast.2.col_ref, bf16[3072,6144]{1,0:T(8,128)(2,1)} %get-tuple-element.147.d_own, bf16[3072,3072]{1,0:T(8,128)(2,1)} %get-tuple-element.171.d_a, ...), custom_call_target="tpu_custom_call", output_to_operand_aliasing={{0}: (14, {})} | custom-call | flops 51539607552 | bytes 100663296 | tf_op jit(solution)/shard_map/dx_part/pallas_call | solution.py:226
  3027.1 2.0 collective-permute-start.20
  3029.8 10.7 constant_dynamic-update-slice_fusion.22
  3043.8 46.6 %collective-permute-done.15 = bf16[512,2048]{1,0:T(8,128)(2,1)S(1)} collective-permute-done((bf16[512,2048]{1,0:T(8,128)(2,1)}, bf16[512,2048]{1,0:T(8,128)(2,1)S(1)}, u32[]{:S(2)}, u32[]{:S(2)}) %collective-permute-start.15) | collective-permute-done | bytes 2097184 | tf_op jit(solution)/shard_map/ppermute | solution.py:505
  3092.5 10.4 add_convert_fusion.6
  3102.9 3.2 constant_dynamic-update-slice_fusion.21
  3107.5 4.8 constant_dynamic-update-slice_fusion.19
  3112.3 53.4 %collective-permute-done.18.recv_ref = bf16[1024,3072]{1,0:T(8,128)(2,1)} collective-permute-done((bf16[1024,3072]{1,0:T(8,128)(2,1)}, bf16[1024,3072]{1,0:T(8,128)(2,1)}, u32[]{:S(2)}, u32[]{:S(2)}) %collective-permute-start.18) | collective-permute-done | bytes 6291488 | tf_op jit(solution)/shard_map/ppermute | solution.py:505
  3165.8 134.8 %collective-permute-done.20.rest_ref = bf16[1024,3072]{1,0:T(8,128)(2,1)} collective-permute-done((bf16[1024,3072]{1,0:T(8,128)(2,1)}, bf16[1024,3072]{1,0:T(8,128)(2,1)}, u32[]{:S(2)}, u32[]{:S(2)}) %collective-permute-start.20) | collective-permute-done | bytes 6291488 | tf_op jit(solution)/shard_map/ppermute | solution.py:505
  3300.6 13.2 join.2.rest_0_
  3313.8 116.2 %collective-permute-done.19.rest_ref = bf16[1024,3072]{1,0:T(8,128)(2,1)} collective-permute-done((bf16[1024,3072]{1,0:T(8,128)(2,1)}, bf16[1024,3072]{1,0:T(8,128)(2,1)}, u32[]{:S(2)}, u32[]{:S(2)}) %collective-permute-start.19) | collective-permute-done | bytes 6291488 | tf_op jit(solution)/shard_map/ppermute | solution.py:505
  3430.0 13.2 join.3
  3443.1 3.2 constant_dynamic-update-slice_fusion.18
  3446.3 3.2 constant_dynamic-update-slice_fusion.17
  (161 shorter events, 38.2 us)
Async XLA Ops:
  7.2 105.4 %all-gather.6.cloned.1.call-start = ((), (), s32[]{:S(2)}) async-start(), calls=%async_computation.6 | async-start | bytes 25165824 | tf_op jit(solution)/shard_map/all_gather | solution.py:511
  7.9 356.3 %all-gather.8.cloned.1.call-start = ((), (), s32[]{:S(2)}) async-start(), calls=%async_computation.7 | async-start | bytes 75497472 | tf_op jit(solution)/shard_map/all_gather | solution.py:511
  71.1 3.2 copy-start.15
  71.2 3.2 copy-start.19
  71.2 3.8 copy-start.20
  71.2 4.4 copy-start.21
  71.2 663.0 %all-gather.10.cloned.1.call-start = ((), (), s32[]{:S(2)}) async-start(), calls=%async_computation.8 | async-start | bytes 31457280 | tf_op jit(solution)/shard_map/all_gather | solution.py:511
  71.2 381.8 %collective-permute-start.3 = (bf16[1024,3072]{1,0:T(8,128)(2,1)}, bf16[1024,3072]{1,0:T(8,128)(2,1)}, u32[]{:S(2)}, u32[]{:S(2)}) collective-permute-start(bf16[1024,3072]{1,0:T(8,128)(2,1)} %get-tuple-element.103), channel_id=1, source_target_pairs={{0,2},{2,0},{1,3},{3,1},{4,6},{6,4},{5,7},{7,5}} | collective-permute-start | bytes 18874376 | tf_op jit(solution)/shard_map/ppermute | solution.py:505
  74.3 274.4 %collective-permute-start.4 = (bf16[1536,2048]{1,0:T(8,128)(2,1)}, bf16[1536,2048]{1,0:T(8,128)(2,1)}, u32[]{:S(2)}, u32[]{:S(2)}) collective-permute-start(bf16[1536,2048]{1,0:T(8,128)(2,1)} %constant_dynamic-slice_fusion.5), channel_id=1, source_target_pairs={{0,2},{2,0},{1,3},{3,1},{4,6},{6,4},{5,7},{7,5}} | collective-permute-start | bytes 18874376 | tf_op jit(solution)/shard_map/ppermute | solution.py:505
  78.5 1.2 copy-start.22
  79.7 266.4 %collective-permute-start.2 = (f32[96,128]{1,0:T(8,128)}, f32[96,128]{1,0:T(8,128)}, u32[]{:S(2)}, u32[]{:S(2)}) collective-permute-start(f32[96,128]{1,0:T(8,128)} %constant_dynamic-update-slice_fusion), channel_id=1, source_target_pairs={{0,2},{2,0},{1,3},{3,1},{4,6},{6,4},{5,7},{7,5}} | collective-permute-start | bytes 147464 | tf_op jit(solution)/shard_map/ppermute | solution.py:505
  177.3 186.9 %copy-start.23 = (f32[48,128]{1,0:T(8,128)S(1)}, f32[48,128]{1,0:T(8,128)}, u32[]{:S(2)}) copy-start(f32[48,128]{1,0:T(8,128)} %copy-done.22) | copy-start | bytes 73732
  453.0 431.4 %all-gather.12.cloned.1.call-start = ((), (), s32[]{:S(2)}) async-start(), calls=%async_computation.9 | async-start | bytes 31457280 | tf_op jit(solution)/shard_map/all_gather | solution.py:511
  453.1 138.7 %collective-permute-start.1 = (bf16[1536,2048]{1,0:T(8,128)(2,1)}, bf16[1536,2048]{1,0:T(8,128)(2,1)}, u32[]{:S(2)}, u32[]{:S(2)}) collective-permute-start(bf16[1536,2048]{1,0:T(8,128)(2,1)} %constant_dynamic-slice_fusion.4), channel_id=1, source_target_pairs={{0,2},{2,0},{1,3},{3,1},{4,6},{6,4},{5,7},{7,5}} | collective-permute-start | bytes 18874376 | tf_op jit(solution)/shard_map/ppermute | solution.py:505
  454.9 276.1 %collective-permute-start = (bf16[1024,3072]{1,0:T(8,128)(2,1)}, bf16[1024,3072]{1,0:T(8,128)(2,1)}, u32[]{:S(2)}, u32[]{:S(2)}) collective-permute-start(bf16[1024,3072]{1,0:T(8,128)(2,1)} %get-tuple-element.105), channel_id=1, source_target_pairs={{0,2},{2,0},{1,3},{3,1},{4,6},{6,4},{5,7},{7,5}} | collective-permute-start | bytes 18874376 | tf_op jit(solution)/shard_map/ppermute | solution.py:505
  731.0 261.2 %all-gather.14.cloned.1.call-start = ((), (), s32[]{:S(2)}) async-start(), calls=%async_computation.10 | async-start | bytes 20971520 | tf_op jit(solution)/shard_map/all_gather | solution.py:511
  731.0 113.5 %collective-permute-start.5 = (bf16[1024,2048]{1,0:T(8,128)(2,1)}, bf16[1024,2048]{1,0:T(8,128)(2,1)}, u32[]{:S(2)}, u32[]{:S(2)}) collective-permute-start(bf16[1024,2048]{1,0:T(8,128)(2,1)} %constant_dynamic-slice_fusion.3), channel_id=1, source_target_pairs={{0,2},{2,0},{1,3},{3,1},{4,6},{6,4},{5,7},{7,5}} | collective-permute-start | bytes 12582920 | tf_op jit(solution)/shard_map/ppermute | solution.py:505
  827.1 57.3 %copy-start.17 = (f32[3072]{0:T(1024)S(1)}, f32[3072]{0:T(1024)}, u32[]{:S(2)}) copy-start(f32[3072]{0:T(1024)} %get-tuple-element.212) | copy-start | bytes 36868
  844.6 694.7 %reduce-scatter.13.cloned.1.call-start = ((), (), s32[]{:S(2)}) async-start(), calls=%async_computation.11 | async-start | bytes 25165824 | tf_op jit(solution)/shard_map/reduce_scatter | solution.py:514
  844.6 272.1 %collective-permute-start.6 = (bf16[3072,2048]{1,0:T(8,128)(2,1)}, bf16[3072,2048]{1,0:T(8,128)(2,1)}, u32[]{:S(2)}, u32[]{:S(2)}) collective-permute-start(bf16[3072,2048]{1,0:T(8,128)(2,1)} %constant_dynamic-slice_fusion.2), channel_id=1, source_target_pairs={{0,2},{2,0},{1,3},{3,1},{4,6},{6,4},{5,7},{7,5}} | collective-permute-start | bytes 37748744 | tf_op jit(solution)/shard_map/ppermute | solution.py:505
  974.7 17.4 copy-start.18
  1241.1 299.1 %reduce-scatter.15.cloned.1.call-start = ((), (), s32[]{:S(2)}) async-start(), calls=%async_computation.12 | async-start | bytes 25165824 | tf_op jit(solution)/shard_map/reduce_scatter | solution.py:514
  1304.5 417.4 %reduce-scatter.17.cloned.1.call-start = ((), (), s32[]{:S(2)}) async-start(), calls=%async_computation.13 | async-start | bytes 31457280 | tf_op jit(solution)/shard_map/reduce_scatter | solution.py:514
  1421.1 428.4 %reduce-scatter.21.cloned.1.call-start = ((), (), s32[]{:S(2)}) async-start(), calls=%async_computation.15 | async-start | bytes 37748736
  1539.3 1108.7 %reduce-scatter.19.cloned.1.call-start = ((), (), s32[]{:S(2)}) async-start(), calls=%async_computation.14 | async-start | bytes 31457280 | tf_op jit(solution)/shard_map/reduce_scatter | solution.py:514
  1539.3 182.5 %collective-permute-start.7 = (bf16[2048,2048]{1,0:T(8,128)(2,1)}, bf16[2048,2048]{1,0:T(8,128)(2,1)}, u32[]{:S(2)}, u32[]{:S(2)}) collective-permute-start(bf16[2048,2048]{1,0:T(8,128)(2,1)} %reduce-scatter.13.cloned.1.call-done), channel_id=1, source_target_pairs={{0,2},{2,0},{1,3},{3,1},{4,6},{6,4},{5,7},{7,5}} | collective-permute-start | bytes 25165832 | tf_op jit(solution)/shard_map/ppermute | solution.py:505
  1849.4 879.1 %reduce-scatter.23.cloned.1.call-start = ((), (), s32[]{:S(2)}) async-start(), calls=%async_computation.16 | async-start | bytes 37748736
  1969.9 0.9 copy-start.9
  1969.9 0.9 copy-start.10
  1970.0 1057.1 %collective-permute-start.11 = (bf16[3072,2048]{1,0:T(8,128)(2,1)}, bf16[3072,2048]{1,0:T(8,128)(2,1)}, u32[]{:S(2)}, u32[]{:S(2)}) collective-permute-start(bf16[3072,2048]{1,0:T(8,128)(2,1)} %add_convert_fusion.5), channel_id=1, source_target_pairs={{0,2},{2,0},{1,3},{3,1},{4,6},{6,4},{5,7},{7,5}} | collective-permute-start | bytes 37748744 | tf_op jit(solution)/shard_map/ppermute | solution.py:505
  1971.0 757.5 %collective-permute-start.9 = (bf16[2048,3072]{1,0:T(8,128)(2,1)}, bf16[2048,3072]{1,0:T(8,128)(2,1)}, u32[]{:S(2)}, u32[]{:S(2)}) collective-permute-start(bf16[2048,3072]{1,0:T(8,128)(2,1)} %reduce-scatter.21.cloned.1.call-done), channel_id=1, source_target_pairs={{0,2},{2,0},{1,3},{3,1},{4,6},{6,4},{5,7},{7,5}} | collective-permute-start | bytes 37748744 | tf_op jit(solution)/shard_map/ppermute | solution.py:505
  1972.2 72.0 %copy-start.24 = (f32[10240]{0:T(1024)}, f32[10240]{0:T(1024)S(1)}, u32[]{:S(2)}) copy-start(f32[10240]{0:T(1024)S(1)} %slice_dynamic-update-slice_fusion.5) | copy-start | bytes 122884
  1972.2 1069.1 %collective-permute-start.14 = (bf16[2048,2048]{1,0:T(8,128)(2,1)}, bf16[2048,2048]{1,0:T(8,128)(2,1)}, u32[]{:S(2)}, u32[]{:S(2)}) collective-permute-start(bf16[2048,2048]{1,0:T(8,128)(2,1)} %add_convert_fusion.7), channel_id=1, source_target_pairs={{0,4},{4,0},{1,5},{5,1},{2,6},{6,2},{3,7},{7,3}} | collective-permute-start | bytes 25165832 | tf_op jit(solution)/shard_map/ppermute | solution.py:505
  1972.2 675.8 %collective-permute-start.8 = (bf16[1024,3072]{1,0:T(8,128)(2,1)}, bf16[1024,3072]{1,0:T(8,128)(2,1)}, u32[]{:S(2)}, u32[]{:S(2)}) collective-permute-start(bf16[1024,3072]{1,0:T(8,128)(2,1)} %reduce-scatter.17.cloned.1.call-done), channel_id=1, source_target_pairs={{0,2},{2,0},{1,3},{3,1},{4,6},{6,4},{5,7},{7,5}} | collective-permute-start | bytes 18874376 | tf_op jit(solution)/shard_map/ppermute | solution.py:505
  1973.0 72.4 %copy-start.11 = (f32[8,3072]{1,0:T(8,128)S(1)}, f32[8,3072]{1,0:T(8,128)}, u32[]{:S(2)}) copy-start(f32[8,3072]{1,0:T(8,128)} %get-tuple-element.183) | copy-start | bytes 294916
  1973.1 72.4 %copy-start.12 = (f32[8,3072]{1,0:T(8,128)S(1)}, f32[8,3072]{1,0:T(8,128)}, u32[]{:S(2)}) copy-start(f32[8,3072]{1,0:T(8,128)} %get-tuple-element.184) | copy-start | bytes 294916
  1973.1 72.4 %copy-start.13 = (f32[8,3072]{1,0:T(8,128)S(1)}, f32[8,3072]{1,0:T(8,128)}, u32[]{:S(2)}) copy-start(f32[8,3072]{1,0:T(8,128)} %get-tuple-element.185) | copy-start | bytes 294916
  1973.1 72.4 %copy-start.14 = (f32[8,3072]{1,0:T(8,128)S(1)}, f32[8,3072]{1,0:T(8,128)}, u32[]{:S(2)}) copy-start(f32[8,3072]{1,0:T(8,128)} %get-tuple-element.186) | copy-start | bytes 294916
  2044.2 982.9 %collective-permute-start.12 = (bf16[512,2048]{1,0:T(8,128)(2,1)}, bf16[512,2048]{1,0:T(8,128)(2,1)}, u32[]{:S(2)}, u32[]{:S(2)}) collective-permute-start(bf16[512,2048]{1,0:T(8,128)(2,1)} %get-tuple-element.152), channel_id=1, source_target_pairs={{0,2},{2,0},{1,3},{3,1},{4,6},{6,4},{5,7},{7,5}} | collective-permute-start | bytes 6291464 | tf_op jit(solution)/shard_map/ppermute | solution.py:505
  2728.5 10.6 copy-start
  2881.1 210.7 %collective-permute-start.16 = (bf16[1024,2048]{1,0:T(8,128)(2,1)}, bf16[1024,2048]{1,0:T(8,128)(2,1)}, u32[]{:S(2)}, u32[]{:S(2)}) collective-permute-start(bf16[1024,2048]{1,0:T(8,128)(2,1)} %get-tuple-element.166), channel_id=1, source_target_pairs={{0,2},{2,0},{1,3},{3,1},{4,6},{6,4},{5,7},{7,5}} | collective-permute-start | bytes 12582920 | tf_op jit(solution)/shard_map/ppermute | solution.py:505
  2951.7 70.5 %copy-start.2 = (f32[8,4096]{1,0:T(8,128)S(1)}, f32[8,4096]{1,0:T(8,128)}, u32[]{:S(2)}) copy-start(f32[8,4096]{1,0:T(8,128)} %get-tuple-element.150) | copy-start | bytes 393220
  2951.7 70.5 %copy-start.4 = (f32[8,4096]{1,0:T(8,128)S(1)}, f32[8,4096]{1,0:T(8,128)}, u32[]{:S(2)}) copy-start(f32[8,4096]{1,0:T(8,128)} %get-tuple-element.157) | copy-start | bytes 393220
  2951.7 70.5 %copy-start.7 = (f32[8,4096]{1,0:T(8,128)S(1)}, f32[8,4096]{1,0:T(8,128)}, u32[]{:S(2)}) copy-start(f32[8,4096]{1,0:T(8,128)} %get-tuple-element.165) | copy-start | bytes 393220
  2951.7 70.5 %copy-start.8 = (f32[8,4096]{1,0:T(8,128)S(1)}, f32[8,4096]{1,0:T(8,128)}, u32[]{:S(2)}) copy-start(f32[8,4096]{1,0:T(8,128)} %get-tuple-element.169) | copy-start | bytes 393220
  2951.7 71.5 %copy-start.25 = (f32[10240]{0:T(1024)S(1)}, f32[10240]{0:T(1024)}, u32[]{:S(2)}) copy-start(f32[10240]{0:T(1024)} %copy-done.24) | copy-start | bytes 122884
  2951.7 72.1 %copy-start.1 = (f32[8,4096]{1,0:T(8,128)S(1)}, f32[8,4096]{1,0:T(8,128)}, u32[]{:S(2)}) copy-start(f32[8,4096]{1,0:T(8,128)} %get-tuple-element.174) | copy-start | bytes 393220
  2951.8 72.1 %copy-start.3 = (f32[8,4096]{1,0:T(8,128)S(1)}, f32[8,4096]{1,0:T(8,128)}, u32[]{:S(2)}) copy-start(f32[8,4096]{1,0:T(8,128)} %get-tuple-element.175) | copy-start | bytes 393220
  2951.8 72.1 %copy-start.5 = (f32[8,4096]{1,0:T(8,128)S(1)}, f32[8,4096]{1,0:T(8,128)}, u32[]{:S(2)}) copy-start(f32[8,4096]{1,0:T(8,128)} %get-tuple-element.176) | copy-start | bytes 393220
  2951.8 72.1 %copy-start.6 = (f32[8,4096]{1,0:T(8,128)S(1)}, f32[8,4096]{1,0:T(8,128)}, u32[]{:S(2)}) copy-start(f32[8,4096]{1,0:T(8,128)} %get-tuple-element.177) | copy-start | bytes 393220
  3022.2 19.1 copy-start.16
  3025.4 4.0 collective-permute-start.10
  3027.1 138.7 %collective-permute-start.18 = (bf16[1024,3072]{1,0:T(8,128)(2,1)}, bf16[1024,3072]{1,0:T(8,128)(2,1)}, u32[]{:S(2)}, u32[]{:S(2)}) collective-permute-start(bf16[1024,3072]{1,0:T(8,128)(2,1)} %add_convert_fusion.10.own_ref), channel_id=1, source_target_pairs={{0,4},{4,0},{1,5},{5,1},{2,6},{6,2},{3,7},{7,3}} | collective-permute-start | bytes 18874376 | tf_op jit(solution)/shard_map/ppermute | solution.py:505
  3027.1 273.5 %collective-permute-start.20 = (bf16[1024,3072]{1,0:T(8,128)(2,1)}, bf16[1024,3072]{1,0:T(8,128)(2,1)}, u32[]{:S(2)}, u32[]{:S(2)}) collective-permute-start(bf16[1024,3072]{1,0:T(8,128)(2,1)} %add_convert_fusion.9.half_ref), channel_id=1, source_target_pairs={{0,4},{4,0},{1,5},{5,1},{2,6},{6,2},{3,7},{7,3}} | collective-permute-start | bytes 18874376 | tf_op jit(solution)/shard_map/ppermute | solution.py:505
  3029.4 400.5 %collective-permute-start.19 = (bf16[1024,3072]{1,0:T(8,128)(2,1)}, bf16[1024,3072]{1,0:T(8,128)(2,1)}, u32[]{:S(2)}, u32[]{:S(2)}) collective-permute-start(bf16[1024,3072]{1,0:T(8,128)(2,1)} %add_convert_fusion.8.half_ref), channel_id=1, source_target_pairs={{0,4},{4,0},{1,5},{5,1},{2,6},{6,2},{3,7},{7,3}} | collective-permute-start | bytes 18874376 | tf_op jit(solution)/shard_map/ppermute | solution.py:505
  3041.3 1.3 collective-permute-start.13
  3042.5 47.9 %collective-permute-start.15 = (bf16[512,2048]{1,0:T(8,128)(2,1)}, bf16[512,2048]{1,0:T(8,128)(2,1)S(1)}, u32[]{:S(2)}, u32[]{:S(2)}) collective-permute-start(bf16[512,2048]{1,0:T(8,128)(2,1)} %get-tuple-element.159), channel_id=1, source_target_pairs={{0,2},{2,0},{1,3},{3,1},{4,6},{6,4},{5,7},{7,5}} | collective-permute-start | bytes 6291464 | tf_op jit(solution)/shard_map/ppermute | solution.py:505
  3090.4 352.7 %collective-permute-start.17 = (bf16[512,2048]{1,0:T(8,128)(2,1)}, bf16[512,2048]{1,0:T(8,128)(2,1)}, u32[]{:S(2)}, u32[]{:S(2)}) collective-permute-start(bf16[512,2048]{1,0:T(8,128)(2,1)} %get-tuple-element.170), channel_id=1, source_target_pairs={{0,2},{2,0},{1,3},{3,1},{4,6},{6,4},{5,7},{7,5}} | collective-permute-start | bytes 6291464 | tf_op jit(solution)/shard_map/ppermute | solution.py:505
  3091.8 351.4 %collective-permute-start.21 = (bf16[512,2048]{1,0:T(8,128)(2,1)}, bf16[512,2048]{1,0:T(8,128)(2,1)}, u32[]{:S(2)}, u32[]{:S(2)}) collective-permute-start(bf16[512,2048]{1,0:T(8,128)(2,1)} %get-tuple-element.179), channel_id=1, source_target_pairs={{0,2},{2,0},{1,3},{3,1},{4,6},{6,4},{5,7},{7,5}} | collective-permute-start | bytes 6291464 | tf_op jit(solution)/shard_map/ppermute | solution.py:505
  3165.8 283.7 %collective-permute-start.22 = (f32[96,128]{1,0:T(8,128)S(1)}, f32[96,128]{1,0:T(8,128)S(1)}, u32[]{:S(2)}, u32[]{:S(2)}) collective-permute-start(f32[96,128]{1,0:T(8,128)S(1)} %fusion.4), channel_id=1, source_target_pairs={{0,4},{4,0},{1,5},{5,1},{2,6},{6,2},{3,7},{7,3}} | collective-permute-start | bytes 147464 | tf_op jit(solution)/shard_map/ppermute | solution.py:505
Sparse Core Ops, SparseCore 0:
  9.5 30.0 all-gather.5
  71.3 72.6 all-gather.7
  453.1 153.2 all-gather.9
  731.1 153.2 all-gather.11
  885.8 103.1 all-gather.13
  1241.2 21.9 reduce-scatter.12
  1304.6 21.3 reduce-scatter.14
  1421.2 175.3 reduce-scatter.16
  1598.9 32.6 reduce-scatter.20
  1849.5 225.3 reduce-scatter.18
  2077.1 33.7 reduce-scatter.22

commit v3 on v2

--- a/solution.py
+++ b/solution.py
@@ -126,9 +126,12 @@
             db_ref[:, cols] += sum_b
 
 
-def dx_body(row0, half, col_ref, d_own, d_a, d_b, w_own, w_a, w_b, x_ref, x0_ref, x1_ref, dy_ref, dyr_ref, stat_ref, g_ref, *rest):
+def dx_body(row0, half, steps, with_y, col_ref, d_own, d_a, d_b, w_own, w_a, w_b, x_ref, x0_ref, x1_ref, dy_ref, dyr_ref, stat_ref, g_ref, *rest):
+    if with_y:
+        yr0_ref, yr1_ref, y_ref, y_buf, y_sems = rest[-16], rest[-15], rest[-9], rest[-2], rest[-1]
+        rest = rest[:-9] + rest[-8:-2]
     dx_ref, send_ref, dg_ref, db_ref, acc, w_buf, d_buf, ln_buf, sems, ln_sems = rest[-10:]
-    m, steps = pl.program_id(0), pl.num_programs(0)
+    m = pl.program_id(0)
     blk, wide = d_buf.shape[1:]
     width = x_ref.shape[1]
     col = col_ref[0]
@@ -183,9 +186,38 @@
 
     acc[...] = jnp.zeros_like(acc)
 
+    y_blocks = steps * count // 2
+    y_rows = half // (2 * y_blocks)
+
+    def y_in(t, src, block):
+        place = pl.ds(pl.multiple_of(block * y_rows, y_rows), y_rows)
+        return pltpu.make_async_copy(src.at[place], y_buf.at[lax.rem(t, 2)], y_sems.at[0, lax.rem(t, 2)])
+
+    def y_out(t):
+        place = pl.ds(pl.multiple_of((1 - col) * half + t * y_rows, y_rows), y_rows)
+        return pltpu.make_async_copy(y_buf.at[lax.rem(t, 2)], y_ref.at[place], y_sems.at[1, lax.rem(t, 2)])
+
     @pl.loop(0, count)
     def _(k):
-        slot = lax.rem(m * count + k, 2)
+        t = m * count + k
+        slot = lax.rem(t, 2)
+        if with_y:
+            @pl.when(t >= 2)
+            def _():
+                y_out(t - 2).wait()
+
+            @pl.when(t < y_blocks)
+            def _():
+                y_in(t, yr0_ref, jnp.minimum(t, y_blocks - 1)).start()
+
+            @pl.when(t >= y_blocks)
+            def _():
+                y_in(t, yr1_ref, jnp.maximum(t - y_blocks, 0)).start()
+
+            @pl.when(t >= 1)
+            def _():
+                y_in(t - 1, yr0_ref, 0).wait()
+                y_out(t - 1).start()
 
         @pl.when(k + 1 < count)
         def _():
@@ -201,15 +233,24 @@
 
     for i in range(4):
         ln_copy(i, dyr_ref.at[far_rows]).wait()
+    if with_y:
+        @pl.when(m == steps - 1)
+        def _():
+            last = steps * count - 1
+            y_in(last, yr0_ref, 0).wait()
+            y_out(last).start()
+            y_out(last - 1).wait()
+            y_out(last).wait()
+
     own_cols = pl.ds(pl.multiple_of(col * width, width), width)
     far_cols = pl.ds(pl.multiple_of((1 - col) * width, width), width)
     sides = ((ln_buf.at[0], ln_buf.at[2], dx_ref, own_cols), (ln_buf.at[1], ln_buf.at[3], send_ref, far_cols))
     ln_bwd_rows(acc, sides, stat_ref, g_ref, dg_ref, db_ref)
 
 
-def dx_part(col, dqkv, weights, x_loc, x_recv, dy_loc, dy_recv, stats, g_full, row0, rows, dx_prev):
+def dx_part(col, dqkv, weights, x_loc, x_recv, dy_loc, dy_recv, stats, g_full, row0, rows, dx_prev, y_pair=None):
     total, width = dy_recv.shape
-    blk, wide = 512, 1024
+    blk, wide = 384, 1024
     off = row0 // blk
     nall = total // blk
     own_spec = pl.BlockSpec((blk, width), lambda i, c: (i + off + c[0] * nall, 0))
@@ -222,29 +263,33 @@
         in_specs.append(any_spec)
         args.append(dx_prev)
         aliases = {14: 0}
+    out_shape = [
+        jax.ShapeDtypeStruct((2 * total, width), BF16),
+        jax.ShapeDtypeStruct((rows, width), BF16),
+        jax.ShapeDtypeStruct((8, 2 * width), F32),
+        jax.ShapeDtypeStruct((8, 2 * width), F32),
+    ]
+    out_specs = [own_spec, pl.BlockSpec((blk, width), lambda i, c: (i, 0)), sums_spec, sums_spec]
+    scratch = [
+        pltpu.VMEM((blk, 2 * width), F32),
+        pltpu.VMEM((2, 2 * width, wide), BF16),
+        pltpu.VMEM((2, blk, wide), BF16),
+        pltpu.VMEM((4, blk, width), BF16),
+        pltpu.SemaphoreType.DMA((2, 2)),
+        pltpu.SemaphoreType.DMA((4,)),
+    ]
     depth = sum(d.shape[1] for d in dqkv)
-    return pl.pallas_call(
-        functools.partial(dx_body, row0, total),
-        out_shape=(
-            jax.ShapeDtypeStruct((2 * total, width), BF16),
-            jax.ShapeDtypeStruct((rows, width), BF16),
-            jax.ShapeDtypeStruct((8, 2 * width), F32),
-            jax.ShapeDtypeStruct((8, 2 * width), F32),
-        ),
-        grid_spec=pltpu.PrefetchScalarGridSpec(
-            num_scalar_prefetch=1,
-            grid=(rows // blk,),
-            in_specs=in_specs,
-            out_specs=(own_spec, pl.BlockSpec((blk, width), lambda i, c: (i, 0)), sums_spec, sums_spec),
-            scratch_shapes=[
-                pltpu.VMEM((blk, 2 * width), F32),
-                pltpu.VMEM((2, 2 * width, wide), BF16),
-                pltpu.VMEM((2, blk, wide), BF16),
-                pltpu.VMEM((4, blk, width), BF16),
-                pltpu.SemaphoreType.DMA((2, 2)),
-                pltpu.SemaphoreType.DMA((4,)),
-            ],
-        ),
+    if y_pair is not None:
+        in_specs.extend([any_spec] * 3)
+        args.extend(y_pair)
+        aliases[len(args) - 1] = 4
+        out_shape.append(jax.ShapeDtypeStruct(y_pair[2].shape, BF16))
+        out_specs.append(any_spec)
+        scratch.extend([pltpu.VMEM((2, total * blk * wide // (rows * depth), width), BF16), pltpu.SemaphoreType.DMA((2, 2))])
+    return pl.pallas_call(
+        functools.partial(dx_body, row0, total, rows // blk, y_pair is not None),
+        out_shape=out_shape,
+        grid_spec=pltpu.PrefetchScalarGridSpec(num_scalar_prefetch=1, grid=(rows // blk,), in_specs=in_specs, out_specs=out_specs, scratch_shapes=scratch),
         input_output_aliases=aliases,
         compiler_params=pltpu.CompilerParams(vmem_limit_bytes=60 * 1024 * 1024),
         cost_estimate=pl.CostEstimate(flops=4 * rows * width * depth, bytes_accessed=(rows // blk) * 4 * width * depth, transcendentals=0),
@@ -282,11 +327,10 @@
             out_ref[half:, cols] = nn_dot(p1, v).astype(BF16)
 
 
-def attn_fwd(grp, qkv, groups, width, seq, row0, total, prev):
-    rows = qkv.shape[0]
+def attn_fwd(grp, qkv, groups, width, seq, row0, rows, prev):
     heads = width // 128
     off = row0 // seq
-    in_specs = [pl.BlockSpec((seq, width), lambda g, i, c, j=j: (i, 3 * g + j)) for j in range(3)]
+    in_specs = [pl.BlockSpec((seq, width), lambda g, i, c, j=j: (i + off, 3 * g + j)) for j in range(3)]
     args = [grp, qkv, qkv, qkv]
     aliases = {}
     if prev is not None:
@@ -296,7 +340,7 @@
     nheads = rows // seq * heads * groups
     return pl.pallas_call(
         functools.partial(attn_fwd_body, heads, 128 ** -0.5),
-        out_shape=jax.ShapeDtypeStruct((total, 4096), BF16),
+        out_shape=jax.ShapeDtypeStruct((qkv.shape[0], 4096), BF16),
         grid_spec=pltpu.PrefetchScalarGridSpec(
             num_scalar_prefetch=1,
             grid=(groups, rows // seq),
@@ -396,34 +440,118 @@
     )(*args)
 
 
-def out_body(col_ref, att_ref, w_ref, x_ref, b_ref, out_ref):
-    out_ref[...] = (x_ref[...].astype(F32) + nn_dot(att_ref[...], w_ref[...]) + b_ref[...]).astype(BF16)
-
-
-def out_rows(col, att, w_o, x_loc, bias):
-    tokens, full = att.shape
-    width = w_o.shape[1]
-    blk, wide = 1024, 1024
+def out_early_body(col_ref, a0_ref, a1_ref, a2_ref, w0_ref, w1_ref, w2_ref, out_ref):
+    part = nn_dot(a0_ref[...], w0_ref[...]) + nn_dot(a1_ref[...], w1_ref[...])
+    out_ref[...] = part + nn_dot(a2_ref[...], w2_ref[...])
+
+
+def out_early(col, att, w_o):
+    tokens = att.shape[0]
+    full, width = w_o.shape
+    blk = 1024
+
+    def group(k, c):
+        return 2 * c[0] + k if k < 2 else 2 * (1 - c[0])
+
+    return pl.pallas_call(
+        out_early_body,
+        out_shape=jax.ShapeDtypeStruct((tokens, width), F32),
+        grid_spec=pltpu.PrefetchScalarGridSpec(
+            num_scalar_prefetch=1,
+            grid=(width // blk, tokens // blk),
+            in_specs=[
+                *[pl.BlockSpec((blk, blk), lambda n, m, c, k=k: (m, group(k, c))) for k in range(3)],
+                *[pl.BlockSpec((blk, blk), lambda n, m, c, k=k: (group(k, c), n)) for k in range(3)],
+            ],
+            out_specs=pl.BlockSpec((blk, blk), lambda n, m, c: (m, n)),
+        ),
+        compiler_params=pltpu.CompilerParams(vmem_limit_bytes=56 * 1024 * 1024),
+        cost_estimate=pl.CostEstimate(flops=6 * tokens * blk * width, bytes_accessed=6 * tokens * full, transcendentals=0),
+        name="out_early",
+    )(col, att, att, att, w_o, w_o, w_o)
+
+
+def out_body(col_ref, part_ref, att_ref, w_ref, x_ref, b_ref, out_ref):
+    out_ref[...] = (x_ref[...].astype(F32) + (part_ref[...] + nn_dot(att_ref[...], w_ref[...])) + b_ref[...]).astype(BF16)
+
+
+def out_rows(col, part, att, w_o, x_loc, bias):
+    tokens, width = part.shape
+    blk = 1024
     nblk = tokens // blk
-    place = pl.BlockSpec((blk, wide), lambda n, m, c: (m + c[0] * nblk, n))
+    place = pl.BlockSpec((blk, blk), lambda n, m, c: (m + c[0] * nblk, n))
     return pl.pallas_call(
         out_body,
         out_shape=jax.ShapeDtypeStruct((2 * tokens, width), BF16),
         grid_spec=pltpu.PrefetchScalarGridSpec(
             num_scalar_prefetch=1,
-            grid=(width // wide, nblk),
+            grid=(width // blk, nblk),
             in_specs=[
-                pl.BlockSpec((blk, full), lambda n, m, c: (m, 0)),
-                pl.BlockSpec((full, wide), lambda n, m, c: (0, n)),
+                pl.BlockSpec((blk, blk), lambda n, m, c: (m, n)),
+                pl.BlockSpec((blk, blk), lambda n, m, c: (m, 2 * (1 - c[0]) + 1)),
+                pl.BlockSpec((blk, blk), lambda n, m, c: (2 * (1 - c[0]) + 1, n)),
                 place,
-                pl.BlockSpec((1, wide), lambda n, m, c: (0, n)),
+                pl.BlockSpec((1, blk), lambda n, m, c: (0, n)),
             ],
             out_specs=place,
         ),
         compiler_params=pltpu.CompilerParams(vmem_limit_bytes=56 * 1024 * 1024),
-        cost_estimate=pl.CostEstimate(flops=2 * tokens * full * width, bytes_accessed=4 * tokens * full, transcendentals=0),
+        cost_estimate=pl.CostEstimate(flops=2 * tokens * blk * width, bytes_accessed=12 * tokens * width, transcendentals=0),
         name="out_rows",
-    )(col, att, w_o, x_loc, bias)
+    )(col, part, att, w_o, x_loc, bias)
+
+
+def weight_grad_body(lhs_ref, rhs_ref, out_ref):
+    out_ref[...] = tn_dot(lhs_ref[...], rhs_ref[...]).astype(BF16)
+
+
+def weight_grad_call(lhs, rhs, col0, cols):
+    tokens, full = lhs.shape
+    blk = 1024
+    off = col0 // blk
+    return pl.pallas_call(
+        weight_grad_body,
+        out_shape=jax.ShapeDtypeStruct((full, cols), BF16),
+        grid=(cols // blk, full // blk),
+        in_specs=[pl.BlockSpec((tokens, blk), lambda n, m: (0, m)), pl.BlockSpec((tokens, blk), lambda n, m: (0, n + off))],
+        out_specs=pl.BlockSpec((blk, blk), lambda n, m: (m, n)),
+        compiler_params=pltpu.CompilerParams(vmem_limit_bytes=56 * 1024 * 1024),
+        cost_estimate=pl.CostEstimate(flops=2 * tokens * full * cols, bytes_accessed=4 * tokens * full, transcendentals=0),
+        name="weight_grad",
+    )(lhs, rhs)
+
+
+def project_body(xn_ref, w_ref, b_ref, *rest):
+    rest[-1][...] = (nn_dot(xn_ref[...], w_ref[...]) + b_ref[...]).astype(BF16)
+
+
+def project_rows(xn, w, bias, row0, rows, prev):
+    total, full = xn.shape
+    width = w.shape[1]
+    blk, wide = 768, 1024
+    off = row0 // blk
+    in_specs = [
+        pl.BlockSpec((blk, full), lambda n, m: (m + off, 0)),
+        pl.BlockSpec((full, wide), lambda n, m: (0, n)),
+        pl.BlockSpec((1, wide), lambda n, m: (0, n)),
+    ]
+    args = [xn, w, bias.reshape(1, -1)]
+    aliases = {}
+    if prev is not None:
+        in_specs.append(pl.BlockSpec(memory_space=pl.ANY))
+        args.append(prev)
+        aliases = {3: 0}
+    return pl.pallas_call(
+        project_body,
+        out_shape=jax.ShapeDtypeStruct((total, width), BF16),
+        grid=(width // wide, rows // blk),
+        in_specs=in_specs,
+        out_specs=pl.BlockSpec((blk, wide), lambda n, m: (m + off, n)),
+        input_output_aliases=aliases,
+        compiler_params=pltpu.CompilerParams(vmem_limit_bytes=56 * 1024 * 1024),
+        cost_estimate=pl.CostEstimate(flops=2 * rows * full * width, bytes_accessed=2 * full * width, transcendentals=0),
+        name="project",
+    )(*args)
 
 
 def regroup_body(src_ref, out_ref):
@@ -466,14 +594,15 @@
         out_ref[:, cols(t, 1)] = (half_ref[:, part].astype(F32) + rest_ref[:, part].astype(F32)).astype(BF16)
 
 
-def join(side, pos, own, recv, half, rest, prev):
-    rows, width = own.shape
+def join(row0, rows, pos, own, recv, half, rest, start, prev):
+    piece, width = own.shape
     blk = 128
-    steps = rows // blk
-    own_spec = pl.BlockSpec((blk, width), lambda i, p: (jnp.where(p[0] == side, i, 0), 0))
-    recv_spec = pl.BlockSpec((blk, width), lambda i, p: (jnp.where(p[0] == side, 0, i), 0))
-    full_spec = pl.BlockSpec((blk, width), lambda i, p: (i, 0))
-    in_specs = [own_spec, recv_spec, full_spec, full_spec]
+    side, steps = row0 // piece, rows // blk
+    off, inner, outer = (row0 - side * piece) // blk, (row0 - start) // blk, row0 // blk
+    own_spec = pl.BlockSpec((blk, width), lambda i, p: (jnp.where(p[0] == side, i + off, 0), 0))
+    recv_spec = pl.BlockSpec((blk, width), lambda i, p: (jnp.where(p[0] == side, 0, i + off), 0))
+    part_spec = pl.BlockSpec((blk, width), lambda i, p: (i + inner, 0))
+    in_specs = [own_spec, recv_spec, part_spec, part_spec]
     args = [pos, own, recv, half, rest]
     aliases = {}
     if prev is not None:
@@ -482,12 +611,12 @@
         aliases = {5: 0}
     return pl.pallas_call(
         functools.partial(join_body, side),
-        out_shape=jax.ShapeDtypeStruct((2 * rows, 2 * width), BF16),
+        out_shape=jax.ShapeDtypeStruct((2 * piece, 2 * width), BF16),
         grid_spec=pltpu.PrefetchScalarGridSpec(
             num_scalar_prefetch=1,
             grid=(steps,),
             in_specs=in_specs,
-            out_specs=pl.BlockSpec((blk, 2 * width), lambda i, p: (i + side * steps, 0)),
+            out_specs=pl.BlockSpec((blk, 2 * width), lambda i, p: (i + outer, 0)),
         ),
         input_output_aliases=aliases,
         cost_estimate=pl.CostEstimate(flops=rows * width, bytes_accessed=10 * rows * width, transcendentals=0),
@@ -579,8 +708,8 @@
         def project(j):
             return (nn_dot(xn, wq_oth[j]) + bq_oth[j]).astype(BF16)
 
-        def weight_grad(lhs, rhs):
-            return tn_dot(lhs, rhs).astype(BF16)
+        def weight_grad(lhs, rhs, col0=0, cols=None):
+            return weight_grad_call(lhs, rhs, col0, cols or rhs.shape[1])
 
         dy_own = lax.dynamic_slice_in_dim(tie(dy2, dy_out), col * half, half, 0)
         datt_part = nt_dot(tie(dy_own, w_perm), wo_own)
@@ -599,36 +728,34 @@
         bq_oth = vecs_r[3 * nv:].reshape(2, 3 * hw)
 
         xn, stats = ln_fwd(col_arr, tie(x2, datt_part, db_o), x_recv[0], g_full, b_full, 0, half, None)
-        qkv_own = [(nn_dot(xn[:rows2], w_own) + bq_own).astype(BF16)]
-        wa_in, xn, qkv_own[0] = held(wa_in, xn, qkv_own[0])
+        qkv_own = project_rows(xn, w_own, bq_own, 0, rows2, None)
+        wa_in, qkv_own = held(wa_in, qkv_own)
         wq_oth[0] = gather(wa_in, ("row", "depth"))
-        xn, stats = ln_fwd(col_arr, x2, x_recv[1], g_full, b_full, rows2, half, (xn, stats))
-        qkv_own.append((nn_dot(xn[rows2:], w_own) + bq_own).astype(BF16))
-        att = None
-        for i in range(2):
-            att = attn_fwd(own_grp[0], qkv_own[i] if i else tie(qkv_own[0], qkv_own[1]), 2, hw, seq, i * rows2, half, att)
+        att = attn_fwd(own_grp[0], qkv_own, 2, hw, seq, 0, rows2, None)
+        xn, stats = ln_fwd(col_arr, tie(x2, att), x_recv[1], g_full, b_full, rows2, half, (xn, stats))
+        qkv_own = project_rows(xn, w_own, bq_own, rows2, rows2, qkv_own)
+        att = attn_fwd(own_grp[0], qkv_own, 2, hw, seq, rows2, rows2, att)
         wb_in, xn, att = held(wb_in, xn, att)
         wq_oth[1] = gather(wb_in, ("row", "depth"))
         qkv_oth[0] = project(0)
         att = attn_fwd(oth_grp[0], qkv_oth[0], 1, hw, seq, 0, half, att)
         wo_in, att, xn = held(wo_in, att, xn)
         wo_oth = gather(wo_in, ("row", "depth"))
-        qkv_oth[1] = project(1)
+        y_part = out_early(col_arr, att, wo_own)
+        qkv_oth[1] = (nn_dot(tie(xn, y_part), wq_oth[1]) + bq_oth[1]).astype(BF16)
         att = attn_fwd(oth_grp[1], qkv_oth[1], 1, hw, seq, 0, half, att)
-        x_all = jnp.concatenate(x_recv, axis=0)
-        y_send = (x_all.astype(F32) + nn_dot(att, wo_oth) + bo_oth).astype(BF16)
-        y_recv = send(y_send)
-        y = out_rows(col_arr, tie(att, y_send), wo_own, x2, b_o.reshape(1, -1))
+        y_send, y_recv = [], []
+        for i in range(2):
+            part_att = (att if i == 0 else tie(att, y_send[0]))[i * rows2:(i + 1) * rows2]
+            y_send.append((x_recv[i].astype(F32) + nn_dot(part_att, wo_oth) + bo_oth).astype(BF16))
+            y_recv.append(send(y_send[i]))
+        y = out_rows(col_arr, tie(y_part, y_send[1]), att, wo_own, x2, b_o.reshape(1, -1))
 
         def back_far(j, gate):
             dqkv_oth[j], sum_oth[j] = attn_bwd(oth_grp[j], tie(qkv_oth[j], gate), d_att, 0, 1, hw, seq, 0, half, None)
 
         def back_own(j, gate, prev):
-            total = 0.0
-            for i in range(2):
-                prev, part = attn_bwd(own_grp[j], tie(qkv_own[i], gate), d_att, j, 2, hw, seq, i * rows2, half, prev)
-                total = total + part
-            return prev, total
+            return attn_bwd(own_grp[j], tie(qkv_own, gate), d_att, j, 2, hw, seq, 0, half, prev)
 
         wide = 3 * hw
         sum_own = [None, None]
@@ -636,36 +763,41 @@
         dwo_far = weight_grad(tie(att, d_att), dy_recv)
         red_of = scatter(dwo_far, "row")
         back_far(0, dwo_far)
+        red_of, dqkv_oth[0] = held(red_of, dqkv_oth[0])
+        far_o = send(red_of)
         dw_a = weight_grad(xn, dqkv_oth[0])
         red_a = scatter(dw_a, ("row", "depth"))
-        red_of, dw_a = held(red_of, dw_a)
-        far_o = send(red_of)
         dwo_near = weight_grad(tie(att, dw_a), dy_own)
         red_on = scatter(dwo_near, "row")
         back_far(1, dwo_near)
         dw_b = weight_grad(xn, dqkv_oth[1])
         red_b = scatter(dw_b, "row")
-        far_o, red_on, red_a, dw_b = held(far_o, red_on, red_a, dw_b)
+        red_a, dw_b = held(red_a, dw_b)
         far_a = send(red_a)
+        dqkv_own, sum_own[0] = back_own(0, dw_b, None)
+        far_o, red_on, dqkv_own = held(far_o, red_on, dqkv_own)
         half_o = (red_on.astype(F32) + far_o.astype(F32)).astype(BF16)
         half_r = send(half_o, "depth")
-        dqkv_own, sum_own[0] = back_own(0, half_o, None)
-        dw_oa = weight_grad(xn, dqkv_own[:, :wide])
+        dqkv_own = tie(dqkv_own, half_o)
+        dw_oa = weight_grad(xn, dqkv_own, 0, wide)
         red_oa = scatter(dw_oa, ("row", "depth"))
         red_b, dw_oa = held(red_b, dw_oa)
         far_b = send(red_b)
         dqkv_own, sum_own[1] = back_own(1, dw_oa, dqkv_own)
-        dw_ob = weight_grad(xn, dqkv_own[:, wide:])
+        dw_ob = weight_grad(xn, dqkv_own, wide, wide)
         red_ob = scatter(dw_ob, "row")
 
-        unit = half // 6
-        parts = (unit, unit, 2 * unit, unit, unit)
+        unit = half // 8
+        parts = (2 * unit, 2 * unit, 2 * unit, unit, unit)
+        cut = piece + piece // 2
         dx, gate, lo = None, dw_ob, 0
         dx_recv, sums_n = [], []
         grads = [dqkv_own, *dqkv_oth]
         for part, rows in enumerate(parts):
             grads[1] = tie(grads[1], gate)
-            dx, dx_send, dg8, db8 = dx_part(col_arr, grads, (w_own, *wq_oth), x2, x_recv, dy2, dy_recv, stats, g_full, lo, rows, dx)
+            y_pair = (*y_recv, y) if part == 2 else None
+            dx, dx_send, dg8, db8, *rest = dx_part(col_arr, grads, (w_own, *wq_oth), x2, x_recv, dy2, dy_recv, stats, g_full, lo, rows, dx, y_pair)
+            y = rest[0] if rest else y
             lo += rows
             sums_n.append((dg8, db8))
             dx_recv.append(send(dx_send))
@@ -679,7 +811,7 @@
                 far_b, red_ob, gate = held(far_b, red_ob, gate)
                 half_b, rest_b = [], []
                 for i in range(2):
-                    part_rows = slice(i * piece, (i + 1) * piece)
+                    part_rows = slice(0, cut) if i == 0 else slice(cut, None)
                     half_b.append((tie(red_ob, gate)[part_rows].astype(F32) + far_b[part_rows].astype(F32)).astype(BF16))
                     rest_b.append(send(half_b[i], "depth"))
                     gate = half_b[i]
@@ -694,19 +826,21 @@
         near = jnp.concatenate([natural(sum_own), lax.dynamic_slice_in_dim(dg, col * width, width), lax.dynamic_slice_in_dim(dbn, col * width, width)])
         near = near.reshape(-1, 128)
         far = send(far.reshape(-1, 128))
-        y = lax.dynamic_update_slice(y, tie(y_recv, gate), (other * half, 0))
-        far, y = held(far, y)
+        far, gate = held(far, gate)
         total = jnp.concatenate([near + far, db_o.reshape(-1, 128)], axis=0)
         row_in = send(total, "row")
-        dw_o = (tie(half_o, y, total).astype(F32) + half_r.astype(F32)).astype(BF16)
+        dw_o = (tie(half_o, total).astype(F32) + half_r.astype(F32)).astype(BF16)
         row_in, dw_o = held(row_in, dw_o)
         total = total + row_in
         dep_in = send(total, "depth")
         place, lo = dw_o, 0
         for part, rows in enumerate(parts):
             if part == 3:
-                dw_qkv = join(0, dep_arr, half_a, tie(rest_a, dx), half_b[0], rest_b[0], None)
-                dw_qkv = join(1, dep_arr, half_a, rest_a, half_b[1], rest_b[1], dw_qkv)
+                dw_qkv = join(0, piece, dep_arr, half_a, tie(rest_a, dx), half_b[0], rest_b[0], 0, None)
+                dw_qkv = join(piece, cut - piece, dep_arr, half_a, rest_a, half_b[0], rest_b[0], 0, dw_qkv)
+                place = dw_qkv
+            if part == 4:
+                dw_qkv = join(cut, 2 * piece - cut, dep_arr, half_a, tie(rest_a, dx), half_b[1], rest_b[1], cut, dw_qkv)
                 place = dw_qkv
             dx = lax.dynamic_update_slice(dx, tie(dx_recv[part], place), (other * half + lo, 0))
             lo += rows

time: 3470 us -> 3050 us (0.88)
  Pallas kernels: 741 us -> 1410 us
  matrix products: 1030 us -> 383 us
  waiting for transfers between devices: 1480 us -> 1050 us
    pallas_call x5 -> x14, Pallas kernels: 416 us -> 1120 us  [the longest x6 469 us: weight_grad_call(): pl.pallas_call(weight_grad_body, out_shape=jax.ShapeDtypeStruct((full, co...]
    dot_general x6 -> x0, matrix products: 477 us -> none  [tn_dot(): lax.dot_general(lhs, rhs, (((0,), (0,)), ((), ())), preferred_element_typ...]
    ppermute x23 -> x24, waiting for transfers between devices: 1440 us -> 1050 us  [swap(): return lax.ppermute(val, axis, SWAP)]
    dot_general x5 -> x4, matrix products: 425 us -> 255 us  [nn_dot(): lax.dot_general(lhs, rhs, (((1,), (0,)), ((), ())), preferred_element_typ...]
    all_gather x5, waiting for transfers between devices: 39.8 us -> 0.01 us  [gather(): return lax.all_gather(val, axes, axis=0, tiled=True)]
    pallas_call x1, Pallas kernels: 60.8 us -> 25.2 us  [out_rows(): pl.pallas_call(out_body, out_shape=jax.ShapeDtypeStruct((2 * tokens, widt...]
    pallas_call x6 -> x4, Pallas kernels: 119 us -> 113 us  [attn_bwd(): pl.pallas_call(functools.partial(attn_bwd_body, heads, 128 ** (-0.5)), ou...]
  transfers between devices with their start and end apart: 34 -> 35, of which waited for: 11 -> 12; matrix products, arithmetic and copies ran while one was open for 31% -> 16% of each run, Pallas kernels for 21% -> 40%
where the time goes in v3:
time: 3050 us; the launch traced here: 3040 us
  Pallas kernels  1410 us (46%)
  waiting for transfers between devices  1050 us (34%)
  matrix products  383 us (13%)
  local copies, waits for them, and re-layouts  79.1 us (3%)
  other arithmetic  78.2 us (3%)
    ppermute x24, waiting for transfers between devices, swap(): return lax.ppermute(val, axis, SWAP)  1050 us
    pallas_call x6, Pallas kernels, weight_grad_call(): pl.pallas_call(weight_grad_body, out_shape=jax.ShapeDtypeStruct((full, co...  469 us
    pallas_call x5, Pallas kernels, dx_part(): pl.pallas_call(functools.partial(dx_body, row0, total, rows // blk, y_pai...  433 us
    dot_general x4, matrix products, nn_dot(): lax.dot_general(lhs, rhs, (((1,), (0,)), ((), ())), preferred_element_typ...  255 us
    pallas_call x2, Pallas kernels, project_rows(): pl.pallas_call(project_body, out_shape=jax.ShapeDtypeStruct((total, width...  173 us
    dot_general x2, matrix products, nt_dot(): lax.dot_general(lhs, rhs, (((1,), (1,)), ((), ())), preferred_element_typ...  128 us
    pallas_call x4, Pallas kernels, attn_bwd(): pl.pallas_call(functools.partial(attn_bwd_body, heads, 128 ** (-0.5)), ou...  113 us
    pallas_call x4, Pallas kernels, attn_fwd(): pl.pallas_call(functools.partial(attn_fwd_body, heads, 128 ** (-0.5)), ou...  72.2 us
  transfers between devices with their start and end apart: 35, of which 12 were waited for; matrix products, arithmetic and copies ran while one was open for 16% of the time, Pallas kernels for 40%

profile of v3, /device:TPU:0, one launch (start us, length us, event | category | flops | bytes accessed | tf_op | source)
XLA Modules:
  0.0 3040.5 jit_solution(13257901872299683727)
XLA Ops:
  8.0 5.4 fusion.5
  13.4 8.9 constant_dynamic-slice_fusion.5
  22.3 6.7 pad_maximum_fusion
  29.0 8.4 constant_dynamic-slice_fusion.4
  37.4 4.7 constant_dynamic-slice_fusion.3
  42.1 10.7 constant_dynamic-slice_fusion.2
  52.8 18.3 regroup.1
  71.2 3.1 collective-permute-start.1
  81.7 14.4 constant_dynamic-slice_fusion.1.rhs_ref
  96.0 16.8 convert_reduce_fusion
  112.8 64.8 %fusion.6 = f32[3072,4096]{1,0:T(8,128)} fusion(bf16[3072,2048]{1,0:T(8,128)(2,1)} %constant_dynamic-slice_fusion.1.rhs_ref, bf16[4096,2048]{1,0:T(8,128)(2,1)} %all-gather.6.cloned.1.call-done.w0_ref.w1_ref.w2_ref.w_ref), kind=kOutput, calls=%fused_computation.77 | convolution fusion | flops 51539607552 | bytes 79691776 | tf_op jit(solution)/shard_map/dot_general | solution.py:19
  177.6 168.5 %collective-permute-done.2 = f32[96,128]{1,0:T(8,128)} collective-permute-done((f32[96,128]{1,0:T(8,128)}, f32[96,128]{1,0:T(8,128)}, u32[]{:S(2)}, u32[]{:S(2)}) %collective-permute-start.2) | collective-permute-done | bytes 49184 | tf_op jit(solution)/shard_map/ppermute | solution.py:634
  348.7 15.5 ln_fwd.2
  364.2 86.5 %project.2.q_ref.k_ref.v_ref.rest_0_ = bf16[3072,6144]{1,0:T(8,128)(2,1)} custom-call(bf16[3072,4096]{1,0:T(8,128)(2,1)} %get-tuple-element.110.xn_ref.rest_0_, bf16[4096,6144]{1,0:T(8,128)(2,1)} %all-gather.8.cloned.1.call-done.w_ref.w_own, f32[1,6144]{1,0:T(1,128)} %bitcast.74), custom_call_target="tpu_custom_call" | custom-call | flops 77309411328 | bytes 50331648 | tf_op jit(solution)/shard_map/project/pallas_call | solution.py:544
  452.8 19.9 attn_fwd.4.rest_0_
  472.7 116.8 %collective-permute-done.3.recv_ref.x1_ref = bf16[1536,2048]{1,0:T(8,128)(2,1)} collective-permute-done((bf16[1536,2048]{1,0:T(8,128)(2,1)}, bf16[1536,2048]{1,0:T(8,128)(2,1)}, u32[]{:S(2)}, u32[]{:S(2)}) %collective-permute-start.3) | collective-permute-done | bytes 6291488 | tf_op jit(solution)/shard_map/ppermute | solution.py:634
  589.5 15.5 ln_fwd.3
  605.0 86.6 %project.3.q_ref.k_ref.v_ref = bf16[3072,6144]{1,0:T(8,128)(2,1)} custom-call(bf16[3072,4096]{1,0:T(8,128)(2,1)} %get-tuple-element.120.xn_ref.lhs_ref, bf16[4096,6144]{1,0:T(8,128)(2,1)} %all-gather.8.cloned.1.call-done.w_ref.w_own, f32[1,6144]{1,0:T(1,128)} %bitcast.75, ...), custom_call_target="tpu_custom_call", output_to_operand_aliasing={{}: (3, {})} | custom-call | flops 77309411328 | bytes 50331648 | tf_op jit(solution)/shard_map/project/pallas_call | solution.py:544
  691.6 17.4 attn_fwd.5.rest_0_
  709.0 13.7 collective-permute-done.6
  725.6 92.5 %add_convert_fusion.2.q_ref.k_ref.v_ref = bf16[3072,3072]{1,0:T(8,128)(2,1)} fusion(f32[3072]{0:T(1024)S(1)} %get-tuple-element.205, bf16[3072,4096]{1,0:T(8,128)(2,1)} %get-tuple-element.120.xn_ref.lhs_ref, bf16[4096,3072]{1,0:T(8,128)(2,1)} %all-gather.10.cloned.1.call-done.w_a), kind=kOutput, calls=%fused_computation.3 | convolution fusion | flops 77328285696 | bytes 69218304 | tf_op jit(solution)/shard_map/dot_general | solution.py:27
  818.2 17.5 attn_fwd.6.a0_ref.a1_ref.a2_ref.rest_0_
  835.7 47.6 %out_early.1.part_ref = f32[3072,2048]{1,0:T(8,128)} custom-call(s32[1]{0:T(128)} %bitcast.col_ref, bf16[3072,4096]{1,0:T(8,128)(2,1)} %attn_fwd.6.a0_ref.a1_ref.a2_ref.rest_0_, bf16[3072,4096]{1,0:T(8,128)(2,1)} %attn_fwd.6.a0_ref.a1_ref.a2_ref.rest_0_, bf16[3072,4096]{1,0:T(8,128)(2,1)} %attn_fwd.6.a0_ref.a1_ref.a2_ref.rest_0_, ...), custom_call_target="tpu_custom_call" | custom-call | flops 38654705664 | bytes 75497472 | tf_op jit(solution)/shard_map/out_early/pallas_call | solution.py:456
  883.3 92.4 %add_convert_fusion.1.q_ref.k_ref.v_ref = bf16[3072,3072]{1,0:T(8,128)(2,1)} fusion(f32[3072]{0:T(1024)S(1)} %copy-done.16, bf16[3072,4096]{1,0:T(8,128)(2,1)} %get-tuple-element.120.xn_ref.lhs_ref, bf16[4096,3072]{1,0:T(8,128)(2,1)} %all-gather.12.cloned.1.call-done.w_b), kind=kOutput, calls=%fused_computation.2 | convolution fusion | flops 77328285696 | bytes 69218304 | tf_op jit(solution)/shard_map/dot_general | solution.py:27
  975.7 17.5 attn_fwd.7.att_ref.lhs_ref
  993.2 35.3 %add_convert_fusion.8 = bf16[1536,2048]{1,0:T(8,128)(2,1)} fusion(bf16[1536,2048]{1,0:T(8,128)(2,1)} %collective-permute-done.1.recv_ref.x0_ref, f32[2048]{0:T(1024)S(1)} %copy-done.17, bf16[4096,2048]{1,0:T(8,128)(2,1)} %all-gather.14.cloned.1.call-done, bf16[3072,4096]{1,0:T(8,128)(2,1)} %attn_fwd.7.att_ref.lhs_ref), kind=kOutput, calls=%fused_computation.13 | convolution fusion | flops 25782386688 | bytes 41951232 | tf_op jit(solution)/shard_map/dot_general | solution.py:27
  1028.5 34.9 %add_convert_fusion.7 = bf16[1536,2048]{1,0:T(8,128)(2,1)} fusion(bf16[1536,2048]{1,0:T(8,128)(2,1)} %collective-permute-done.3.recv_ref.x1_ref, f32[2048]{0:T(1024)S(1)} %copy-done.17, bf16[4096,2048]{1,0:T(8,128)(2,1)} %all-gather.14.cloned.1.call-done, bf16[3072,4096]{1,0:T(8,128)(2,1)} %attn_fwd.7.att_ref.lhs_ref), kind=kOutput, calls=%fused_computation.10 | convolution fusion | flops 25782386688 | bytes 41951232 | tf_op jit(solution)/shard_map/dot_general | solution.py:27
  1063.3 25.2 out_rows.1.rest_3_
  1088.5 16.3 collective-permute-done.4.rhs_ref.dyr_ref
  1104.8 63.0 %add_convert_fusion.d_ref = bf16[3072,4096]{1,0:T(8,128)(2,1)} fusion(f32[3072,4096]{1,0:T(8,128)} %fusion.6, bf16[3072,2048]{1,0:T(8,128)(2,1)} %collective-permute-done.4.rhs_ref.dyr_ref, bf16[4096,2048]{1,0:T(8,128)(2,1)} %all-gather.14.cloned.1.call-done), kind=kOutput, calls=%fused_computation | convolution fusion | flops 51564773376 | bytes 104857600 | tf_op jit(solution)/shard_map/dot_general | solution.py:19
  1167.8 59.6 %weight_grad.6 = bf16[4096,2048]{1,0:T(8,128)(2,1)} custom-call(bf16[3072,4096]{1,0:T(8,128)(2,1)} %attn_fwd.7.att_ref.lhs_ref, bf16[3072,2048]{1,0:T(8,128)(2,1)} %collective-permute-done.4.rhs_ref.dyr_ref), custom_call_target="tpu_custom_call" | custom-call | flops 51539607552 | bytes 50331648 | tf_op jit(solution)/shard_map/weight_grad/pallas_call | solution.py:512
  1227.5 28.4 attn_bwd.4
  1255.9 86.6 %weight_grad.7 = bf16[4096,3072]{1,0:T(8,128)(2,1)} custom-call(bf16[3072,4096]{1,0:T(8,128)(2,1)} %get-tuple-element.120.xn_ref.lhs_ref, bf16[3072,3072]{1,0:T(8,128)(2,1)} %get-tuple-element.160.rhs_ref.d_a), custom_call_target="tpu_custom_call" | custom-call | flops 77309411328 | bytes 50331648 | tf_op jit(solution)/shard_map/weight_grad/pallas_call | solution.py:512
  1342.4 59.8 %weight_grad.8 = bf16[4096,2048]{1,0:T(8,128)(2,1)} custom-call(bf16[3072,4096]{1,0:T(8,128)(2,1)} %attn_fwd.7.att_ref.lhs_ref, bf16[3072,2048]{1,0:T(8,128)(2,1)} %constant_dynamic-slice_fusion.1.rhs_ref), custom_call_target="tpu_custom_call" | custom-call | flops 51539607552 | bytes 50331648 | tf_op jit(solution)/shard_map/weight_grad/pallas_call | solution.py:512
  1403.0 28.7 attn_bwd.7
  1431.8 89.3 %weight_grad.10 = bf16[4096,3072]{1,0:T(8,128)(2,1)} custom-call(bf16[3072,4096]{1,0:T(8,128)(2,1)} %get-tuple-element.120.xn_ref.lhs_ref, bf16[3072,3072]{1,0:T(8,128)(2,1)} %get-tuple-element.140.rhs_ref.d_b), custom_call_target="tpu_custom_call" | custom-call | flops 77309411328 | bytes 50331648 | tf_op jit(solution)/shard_map/weight_grad/pallas_call | solution.py:512
  1521.1 26.5 attn_bwd.5
  1547.6 151.0 %collective-permute-done.7 = bf16[2048,2048]{1,0:T(8,128)(2,1)} collective-permute-done((bf16[2048,2048]{1,0:T(8,128)(2,1)}, bf16[2048,2048]{1,0:T(8,128)(2,1)}, u32[]{:S(2)}, u32[]{:S(2)}) %collective-permute-start.7) | collective-permute-done | bytes 8388640 | tf_op jit(solution)/shard_map/ppermute | solution.py:634
  1698.7 10.5 add_convert_fusion.5
  1709.1 86.5 %weight_grad.11 = bf16[4096,3072]{1,0:T(8,128)(2,1)} custom-call(bf16[3072,4096]{1,0:T(8,128)(2,1)} %get-tuple-element.120.xn_ref.lhs_ref, bf16[3072,6144]{1,0:T(8,128)(2,1)} %get-tuple-element.136.rest_0_.rhs_ref), custom_call_target="tpu_custom_call" | custom-call | flops 77309411328 | bytes 50331648 | tf_op jit(solution)/shard_map/weight_grad/pallas_call | solution.py:512
  1795.7 29.5 attn_bwd.6
  1825.2 86.8 %weight_grad.9 = bf16[4096,3072]{1,0:T(8,128)(2,1)} custom-call(bf16[3072,4096]{1,0:T(8,128)(2,1)} %get-tuple-element.120.xn_ref.lhs_ref, bf16[3072,6144]{1,0:T(8,128)(2,1)} %get-tuple-element.137.rhs_ref.d_own), custom_call_target="tpu_custom_call" | custom-call | flops 77309411328 | bytes 50331648 | tf_op jit(solution)/shard_map/weight_grad/pallas_call | solution.py:512
  1917.7 106.4 %dx_part.5 = (bf16[6144,2048]{1,0:T(8,128)(2,1)}, bf16[768,2048]{1,0:T(8,128)(2,1)}, f32[8,4096]{1,0:T(8,128)}, f32[8,4096]{1,0:T(8,128)}) custom-call(s32[1]{0:T(128)} %bitcast.col_ref, bf16[3072,6144]{1,0:T(8,128)(2,1)} %get-tuple-element.137.rhs_ref.d_own, bf16[3072,3072]{1,0:T(8,128)(2,1)} %get-tuple-element.160.rhs_ref.d_a, ...), custom_call_target="tpu_custom_call" | custom-call | flops 77309411328 | bytes 201326592 | tf_op jit(solution)/shard_map/dx_part/pallas_call | solution.py:289
  2024.1 296.3 %collective-permute-done.8 = bf16[1024,3072]{1,0:T(8,128)(2,1)} collective-permute-done((bf16[1024,3072]{1,0:T(8,128)(2,1)}, bf16[1024,3072]{1,0:T(8,128)(2,1)}, u32[]{:S(2)}, u32[]{:S(2)}) %collective-permute-start.8) | collective-permute-done | bytes 6291488 | tf_op jit(solution)/shard_map/ppermute | solution.py:634
  2321.3 10.0 add_convert_fusion.6.own_ref
  2331.3 105.2 %dx_part.6 = (bf16[6144,2048]{1,0:T(8,128)(2,1)}, bf16[768,2048]{1,0:T(8,128)(2,1)}, f32[8,4096]{1,0:T(8,128)}, f32[8,4096]{1,0:T(8,128)}) custom-call(s32[1]{0:T(128)} %bitcast.col_ref, bf16[3072,6144]{1,0:T(8,128)(2,1)} %get-tuple-element.137.rhs_ref.d_own, bf16[3072,3072]{1,0:T(8,128)(2,1)} %get-tuple-element.160.rhs_ref.d_a, ...), custom_call_target="tpu_custom_call", output_to_operand_aliasing={{0}: (14, {})} | custom-call | flops 77309411328 | bytes 201326592 | tf_op jit(solution)/shard_map/dx_part/pallas_call | solution.py:289
  2436.6 153.5 %collective-permute-done.9 = bf16[2048,3072]{1,0:T(8,128)(2,1)} collective-permute-done((bf16[2048,3072]{1,0:T(8,128)(2,1)}, bf16[2048,3072]{1,0:T(8,128)(2,1)}, u32[]{:S(2)}, u32[]{:S(2)}) %collective-permute-start.9) | collective-permute-done | bytes 12582944 | tf_op jit(solution)/shard_map/ppermute | solution.py:634
  2591.3 12.6 add_convert_fusion.3.half_ref
  2603.9 5.6 add_convert_fusion.9.half_ref
  2610.4 110.5 %dx_part.7 = (bf16[6144,2048]{1,0:T(8,128)(2,1)}, bf16[768,2048]{1,0:T(8,128)(2,1)}, f32[8,4096]{1,0:T(8,128)}, f32[8,4096]{1,0:T(8,128)}, bf16[6144,2048]{1,0:T(8,128)(2,1)}) custom-call(s32[1]{0:T(128)} %bitcast.col_ref, bf16[3072,6144]{1,0:T(8,128)(2,1)} %get-tuple-element.137.rhs_ref.d_own, ...), custom_call_target="tpu_custom_call", output_to_operand_aliasing={{0}: (14, {}), {4}: (17, {})} | custom-call | flops 77309411328 | bytes 201326592 | tf_op jit(solution)/shard_map/dx_part/pallas_call | solution.py:289
  2720.8 55.0 %dx_part.8 = (bf16[6144,2048]{1,0:T(8,128)(2,1)}, bf16[384,2048]{1,0:T(8,128)(2,1)}, f32[8,4096]{1,0:T(8,128)}, f32[8,4096]{1,0:T(8,128)}) custom-call(s32[1]{0:T(128)} %bitcast.col_ref, bf16[3072,6144]{1,0:T(8,128)(2,1)} %get-tuple-element.137.rhs_ref.d_own, bf16[3072,3072]{1,0:T(8,128)(2,1)} %get-tuple-element.160.rhs_ref.d_a, ...), custom_call_target="tpu_custom_call", output_to_operand_aliasing={{0}: (14, {})} | custom-call | flops 38654705664 | bytes 100663296 | tf_op jit(solution)/shard_map/dx_part/pallas_call | solution.py:289
  2776.0 55.8 %dx_part.9 = (bf16[6144,2048]{1,0:T(8,128)(2,1)}, bf16[384,2048]{1,0:T(8,128)(2,1)}, f32[8,4096]{1,0:T(8,128)}, f32[8,4096]{1,0:T(8,128)}) custom-call(s32[1]{0:T(128)} %bitcast.col_ref, bf16[3072,6144]{1,0:T(8,128)(2,1)} %get-tuple-element.137.rhs_ref.d_own, bf16[3072,3072]{1,0:T(8,128)(2,1)} %get-tuple-element.160.rhs_ref.d_a, ...), custom_call_target="tpu_custom_call", output_to_operand_aliasing={{0}: (14, {})} | custom-call | flops 38654705664 | bytes 100663296 | tf_op jit(solution)/shard_map/dx_part/pallas_call | solution.py:289
  2837.0 2.6 collective-permute-done.13
  2843.8 63.5 %collective-permute-done.17 = bf16[768,2048]{1,0:T(8,128)(2,1)} collective-permute-done((bf16[768,2048]{1,0:T(8,128)(2,1)}, bf16[768,2048]{1,0:T(8,128)(2,1)}, u32[]{:S(2)}, u32[]{:S(2)}) %collective-permute-start.17) | collective-permute-done | bytes 3145760 | tf_op jit(solution)/shard_map/ppermute | solution.py:634
  2908.3 66.4 %collective-permute-done.16 = bf16[768,2048]{1,0:T(8,128)(2,1)} collective-permute-done((bf16[768,2048]{1,0:T(8,128)(2,1)}, bf16[768,2048]{1,0:T(8,128)(2,1)}, u32[]{:S(2)}, u32[]{:S(2)}) %collective-permute-start.16) | collective-permute-done | bytes 3145760 | tf_op jit(solution)/shard_map/ppermute | solution.py:634
  2975.7 10.4 add_convert_fusion.4
  2986.2 4.0 constant_dynamic-update-slice_fusion.21
  2990.2 4.0 constant_dynamic-update-slice_fusion.20
  2994.1 4.0 constant_dynamic-update-slice_fusion.19
  2999.3 13.2 join.3.rest_0_
  3012.5 7.0 join.4.rest_0_
  3019.5 2.7 constant_dynamic-update-slice_fusion.18
  3022.2 7.0 join.5
  3029.9 2.7 constant_dynamic-update-slice_fusion.17
  (155 shorter events, 39.9 us)
Async XLA Ops:
  7.2 105.7 %all-gather.6.cloned.1.call-start = ((), (), s32[]{:S(2)}) async-start(), calls=%async_computation.6 | async-start | bytes 25165824 | tf_op jit(solution)/shard_map/all_gather | solution.py:640
  7.9 356.3 %all-gather.8.cloned.1.call-start = ((), (), s32[]{:S(2)}) async-start(), calls=%async_computation.7 | async-start | bytes 75497472 | tf_op jit(solution)/shard_map/all_gather | solution.py:640
  71.1 3.2 copy-start.12
  71.1 3.2 copy-start.18
  71.1 3.8 copy-start.19
  71.1 4.4 copy-start.15
  71.2 654.5 %all-gather.10.cloned.1.call-start = ((), (), s32[]{:S(2)}) async-start(), calls=%async_computation.8 | async-start | bytes 31457280 | tf_op jit(solution)/shard_map/all_gather | solution.py:640
  71.2 277.5 %collective-permute-start.1 = (bf16[1536,2048]{1,0:T(8,128)(2,1)}, bf16[1536,2048]{1,0:T(8,128)(2,1)}, u32[]{:S(2)}, u32[]{:S(2)}) collective-permute-start(bf16[1536,2048]{1,0:T(8,128)(2,1)} %constant_dynamic-slice_fusion.5), channel_id=1, source_target_pairs={{0,2},{2,0},{1,3},{3,1},{4,6},{6,4},{5,7},{7,5}} | collective-permute-start | bytes 18874376 | tf_op jit(solution)/shard_map/ppermute | solution.py:634
  74.3 376.4 %collective-permute-start = (bf16[1024,3072]{1,0:T(8,128)(2,1)}, bf16[1024,3072]{1,0:T(8,128)(2,1)}, u32[]{:S(2)}, u32[]{:S(2)}) collective-permute-start(bf16[1024,3072]{1,0:T(8,128)(2,1)} %get-tuple-element.99), channel_id=1, source_target_pairs={{0,2},{2,0},{1,3},{3,1},{4,6},{6,4},{5,7},{7,5}} | collective-permute-start | bytes 18874376 | tf_op jit(solution)/shard_map/ppermute | solution.py:634
  78.5 1.2 copy-start.20
  79.7 266.4 %collective-permute-start.2 = (f32[96,128]{1,0:T(8,128)}, f32[96,128]{1,0:T(8,128)}, u32[]{:S(2)}, u32[]{:S(2)}) collective-permute-start(f32[96,128]{1,0:T(8,128)} %constant_dynamic-update-slice_fusion), channel_id=1, source_target_pairs={{0,2},{2,0},{1,3},{3,1},{4,6},{6,4},{5,7},{7,5}} | collective-permute-start | bytes 147464 | tf_op jit(solution)/shard_map/ppermute | solution.py:634
  450.7 432.6 %all-gather.12.cloned.1.call-start = ((), (), s32[]{:S(2)}) async-start(), calls=%async_computation.9 | async-start | bytes 31457280 | tf_op jit(solution)/shard_map/all_gather | solution.py:640
  450.8 138.7 %collective-permute-start.3 = (bf16[1536,2048]{1,0:T(8,128)(2,1)}, bf16[1536,2048]{1,0:T(8,128)(2,1)}, u32[]{:S(2)}, u32[]{:S(2)}) collective-permute-start(bf16[1536,2048]{1,0:T(8,128)(2,1)} %constant_dynamic-slice_fusion.4), channel_id=1, source_target_pairs={{0,2},{2,0},{1,3},{3,1},{4,6},{6,4},{5,7},{7,5}} | collective-permute-start | bytes 18874376 | tf_op jit(solution)/shard_map/ppermute | solution.py:634
  452.6 270.2 %collective-permute-start.6 = (bf16[1024,3072]{1,0:T(8,128)(2,1)}, bf16[1024,3072]{1,0:T(8,128)(2,1)}, u32[]{:S(2)}, u32[]{:S(2)}) collective-permute-start(bf16[1024,3072]{1,0:T(8,128)(2,1)} %get-tuple-element.101), channel_id=1, source_target_pairs={{0,2},{2,0},{1,3},{3,1},{4,6},{6,4},{5,7},{7,5}} | collective-permute-start | bytes 18874376 | tf_op jit(solution)/shard_map/ppermute | solution.py:634
  722.8 270.4 %all-gather.14.cloned.1.call-start = ((), (), s32[]{:S(2)}) async-start(), calls=%async_computation.10 | async-start | bytes 20971520 | tf_op jit(solution)/shard_map/all_gather | solution.py:640
  722.8 112.8 %collective-permute-start.5 = (bf16[1024,2048]{1,0:T(8,128)(2,1)}, bf16[1024,2048]{1,0:T(8,128)(2,1)}, u32[]{:S(2)}, u32[]{:S(2)}) collective-permute-start(bf16[1024,2048]{1,0:T(8,128)(2,1)} %constant_dynamic-slice_fusion.3), channel_id=1, source_target_pairs={{0,2},{2,0},{1,3},{3,1},{4,6},{6,4},{5,7},{7,5}} | collective-permute-start | bytes 12582920 | tf_op jit(solution)/shard_map/ppermute | solution.py:634
  835.6 420.2 %reduce-scatter.13.cloned.1.call-start = ((), (), s32[]{:S(2)}) async-start(), calls=%async_computation.11 | async-start | bytes 25165824 | tf_op jit(solution)/shard_map/reduce_scatter | solution.py:643
  835.7 269.1 %collective-permute-start.4 = (bf16[3072,2048]{1,0:T(8,128)(2,1)}, bf16[3072,2048]{1,0:T(8,128)(2,1)}, u32[]{:S(2)}, u32[]{:S(2)}) collective-permute-start(bf16[3072,2048]{1,0:T(8,128)(2,1)} %constant_dynamic-slice_fusion.2), channel_id=1, source_target_pairs={{0,2},{2,0},{1,3},{3,1},{4,6},{6,4},{5,7},{7,5}} | collective-permute-start | bytes 37748744 | tf_op jit(solution)/shard_map/ppermute | solution.py:634
  835.7 47.6 %copy-start.16 = (f32[3072]{0:T(1024)S(1)}, f32[3072]{0:T(1024)}, u32[]{:S(2)}) copy-start(f32[3072]{0:T(1024)} %get-tuple-element.204) | copy-start | bytes 36868
  975.7 17.5 copy-start.17
  1227.4 471.2 %reduce-scatter.15.cloned.1.call-start = ((), (), s32[]{:S(2)}) async-start(), calls=%async_computation.12 | async-start | bytes 25165824 | tf_op jit(solution)/shard_map/reduce_scatter | solution.py:643
  1402.2 513.4 %reduce-scatter.17.cloned.1.call-start = ((), (), s32[]{:S(2)}) async-start(), calls=%async_computation.13 | async-start | bytes 31457280 | tf_op jit(solution)/shard_map/reduce_scatter | solution.py:643
  1403.0 513.4 %reduce-scatter.21.cloned.1.call-start = ((), (), s32[]{:S(2)}) async-start(), calls=%async_computation.15 | async-start | bytes 37748736
  1521.0 800.2 %reduce-scatter.19.cloned.1.call-start = ((), (), s32[]{:S(2)}) async-start(), calls=%async_computation.14 | async-start | bytes 31457280 | tf_op jit(solution)/shard_map/reduce_scatter | solution.py:643
  1521.1 177.6 %collective-permute-start.7 = (bf16[2048,2048]{1,0:T(8,128)(2,1)}, bf16[2048,2048]{1,0:T(8,128)(2,1)}, u32[]{:S(2)}, u32[]{:S(2)}) collective-permute-start(bf16[2048,2048]{1,0:T(8,128)(2,1)} %reduce-scatter.13.cloned.1.call-done), channel_id=1, source_target_pairs={{0,2},{2,0},{1,3},{3,1},{4,6},{6,4},{5,7},{7,5}} | collective-permute-start | bytes 25165832 | tf_op jit(solution)/shard_map/ppermute | solution.py:634
  1795.7 795.6 %reduce-scatter.23.cloned.1.call-start = ((), (), s32[]{:S(2)}) async-start(), calls=%async_computation.16 | async-start | bytes 37748736
  1912.0 2.1 copy-start.8
  1912.0 2.1 copy-start.10
  1912.0 2.2 copy-start.9
  1912.0 3.5 copy-start.11
  1912.0 697.5 %collective-permute-start.11 = (bf16[1536,2048]{1,0:T(8,128)(2,1)}, bf16[1536,2048]{1,0:T(8,128)(2,1)}, u32[]{:S(2)}, u32[]{:S(2)}) collective-permute-start(bf16[1536,2048]{1,0:T(8,128)(2,1)} %add_convert_fusion.7), channel_id=1, source_target_pairs={{0,2},{2,0},{1,3},{3,1},{4,6},{6,4},{5,7},{7,5}} | collective-permute-start | bytes 18874376 | tf_op jit(solution)/shard_map/ppermute | solution.py:634
  1912.9 697.4 %collective-permute-start.10 = (bf16[1536,2048]{1,0:T(8,128)(2,1)}, bf16[1536,2048]{1,0:T(8,128)(2,1)}, u32[]{:S(2)}, u32[]{:S(2)}) collective-permute-start(bf16[1536,2048]{1,0:T(8,128)(2,1)} %add_convert_fusion.8), channel_id=1, source_target_pairs={{0,2},{2,0},{1,3},{3,1},{4,6},{6,4},{5,7},{7,5}} | collective-permute-start | bytes 18874376 | tf_op jit(solution)/shard_map/ppermute | solution.py:634
  1914.3 109.8 %copy-start.21 = (f32[10240]{0:T(1024)}, f32[10240]{0:T(1024)S(1)}, u32[]{:S(2)}) copy-start(f32[10240]{0:T(1024)S(1)} %slice_dynamic-update-slice_fusion) | copy-start | bytes 122884
  1914.3 927.2 %collective-permute-start.15 = (bf16[2048,2048]{1,0:T(8,128)(2,1)}, bf16[2048,2048]{1,0:T(8,128)(2,1)}, u32[]{:S(2)}, u32[]{:S(2)}) collective-permute-start(bf16[2048,2048]{1,0:T(8,128)(2,1)} %add_convert_fusion.5), channel_id=1, source_target_pairs={{0,4},{4,0},{1,5},{5,1},{2,6},{6,2},{3,7},{7,3}} | collective-permute-start | bytes 25165832 | tf_op jit(solution)/shard_map/ppermute | solution.py:634
  1915.6 108.5 %copy-start.14 = (f32[10240]{0:T(1024)}, f32[10240]{0:T(1024)S(1)}, u32[]{:S(2)}) copy-start(f32[10240]{0:T(1024)S(1)} %slice_dynamic-update-slice_fusion.5) | copy-start | bytes 122884
  1915.7 404.7 %collective-permute-start.8 = (bf16[1024,3072]{1,0:T(8,128)(2,1)}, bf16[1024,3072]{1,0:T(8,128)(2,1)}, u32[]{:S(2)}, u32[]{:S(2)}) collective-permute-start(bf16[1024,3072]{1,0:T(8,128)(2,1)} %reduce-scatter.17.cloned.1.call-done), channel_id=1, source_target_pairs={{0,2},{2,0},{1,3},{3,1},{4,6},{6,4},{5,7},{7,5}} | collective-permute-start | bytes 18874376 | tf_op jit(solution)/shard_map/ppermute | solution.py:634
  1916.4 673.6 %collective-permute-start.9 = (bf16[2048,3072]{1,0:T(8,128)(2,1)}, bf16[2048,3072]{1,0:T(8,128)(2,1)}, u32[]{:S(2)}, u32[]{:S(2)}) collective-permute-start(bf16[2048,3072]{1,0:T(8,128)(2,1)} %reduce-scatter.21.cloned.1.call-done), channel_id=1, source_target_pairs={{0,2},{2,0},{1,3},{3,1},{4,6},{6,4},{5,7},{7,5}} | collective-permute-start | bytes 37748744 | tf_op jit(solution)/shard_map/ppermute | solution.py:634
  2320.4 515.6 %collective-permute-start.12 = (bf16[768,2048]{1,0:T(8,128)(2,1)}, bf16[768,2048]{1,0:T(8,128)(2,1)}, u32[]{:S(2)}, u32[]{:S(2)}) collective-permute-start(bf16[768,2048]{1,0:T(8,128)(2,1)} %get-tuple-element.143), channel_id=1, source_target_pairs={{0,2},{2,0},{1,3},{3,1},{4,6},{6,4},{5,7},{7,5}} | collective-permute-start | bytes 9437192 | tf_op jit(solution)/shard_map/ppermute | solution.py:634
  2590.1 408.0 %collective-permute-start.19 = (bf16[1024,3072]{1,0:T(8,128)(2,1)}, bf16[1024,3072]{1,0:T(8,128)(2,1)}, u32[]{:S(2)}, u32[]{:S(2)}) collective-permute-start(bf16[1024,3072]{1,0:T(8,128)(2,1)} %add_convert_fusion.6.own_ref), channel_id=1, source_target_pairs={{0,4},{4,0},{1,5},{5,1},{2,6},{6,2},{3,7},{7,3}} | collective-permute-start | bytes 18874376 | tf_op jit(solution)/shard_map/ppermute | solution.py:634
  2609.5 389.8 %collective-permute-start.20 = (bf16[1536,3072]{1,0:T(8,128)(2,1)}, bf16[1536,3072]{1,0:T(8,128)(2,1)}, u32[]{:S(2)}, u32[]{:S(2)}) collective-permute-start(bf16[1536,3072]{1,0:T(8,128)(2,1)} %add_convert_fusion.3.half_ref), channel_id=1, source_target_pairs={{0,4},{4,0},{1,5},{5,1},{2,6},{6,2},{3,7},{7,3}} | collective-permute-start | bytes 28311560 | tf_op jit(solution)/shard_map/ppermute | solution.py:634
  2775.9 55.9 %copy-start.2 = (f32[8,4096]{1,0:T(8,128)S(1)}, f32[8,4096]{1,0:T(8,128)}, u32[]{:S(2)}) copy-start(f32[8,4096]{1,0:T(8,128)} %get-tuple-element.165) | copy-start | bytes 393220
  2775.9 55.9 %copy-start.4 = (f32[8,4096]{1,0:T(8,128)S(1)}, f32[8,4096]{1,0:T(8,128)}, u32[]{:S(2)}) copy-start(f32[8,4096]{1,0:T(8,128)} %get-tuple-element.166) | copy-start | bytes 393220
  2775.9 55.9 %copy-start.7 = (f32[8,4096]{1,0:T(8,128)S(1)}, f32[8,4096]{1,0:T(8,128)}, u32[]{:S(2)}) copy-start(f32[8,4096]{1,0:T(8,128)} %get-tuple-element.167) | copy-start | bytes 393220
  2775.9 57.5 %copy-start.1 = (f32[8,4096]{1,0:T(8,128)S(1)}, f32[8,4096]{1,0:T(8,128)}, u32[]{:S(2)}) copy-start(f32[8,4096]{1,0:T(8,128)} %get-tuple-element.170) | copy-start | bytes 393220
  2775.9 57.5 %copy-start.3 = (f32[8,4096]{1,0:T(8,128)S(1)}, f32[8,4096]{1,0:T(8,128)}, u32[]{:S(2)}) copy-start(f32[8,4096]{1,0:T(8,128)} %get-tuple-element.171) | copy-start | bytes 393220
  2775.9 57.5 %copy-start.5 = (f32[8,4096]{1,0:T(8,128)S(1)}, f32[8,4096]{1,0:T(8,128)}, u32[]{:S(2)}) copy-start(f32[8,4096]{1,0:T(8,128)} %get-tuple-element.172) | copy-start | bytes 393220
  2775.9 57.5 %copy-start.6 = (f32[8,4096]{1,0:T(8,128)S(1)}, f32[8,4096]{1,0:T(8,128)}, u32[]{:S(2)}) copy-start(f32[8,4096]{1,0:T(8,128)} %get-tuple-element.173) | copy-start | bytes 393220
  2775.9 65.5 %copy-start.13 = (f32[2048]{0:T(1024)S(1)}, f32[2048]{0:T(1024)}, u32[]{:S(2)}) copy-start(f32[2048]{0:T(1024)} %convert_reduce_fusion) | copy-start | bytes 24580
  2775.9 66.8 %copy-start = (bf16[512,3072]{1,0:T(8,128)(2,1)S(1)}, bf16[512,3072]{1,0:T(8,128)(2,1)}, u32[]{:S(2)}) copy-start(bf16[512,3072]{1,0:T(8,128)(2,1)} %add_convert_fusion.9.half_ref) | copy-start | bytes 9437188
  2835.0 4.6 collective-permute-start.13
  2836.0 71.3 %collective-permute-start.17 = (bf16[768,2048]{1,0:T(8,128)(2,1)}, bf16[768,2048]{1,0:T(8,128)(2,1)}, u32[]{:S(2)}, u32[]{:S(2)}) collective-permute-start(bf16[768,2048]{1,0:T(8,128)(2,1)} %get-tuple-element.156), channel_id=1, source_target_pairs={{0,2},{2,0},{1,3},{3,1},{4,6},{6,4},{5,7},{7,5}} | collective-permute-start | bytes 9437192 | tf_op jit(solution)/shard_map/ppermute | solution.py:634
  2839.6 135.1 %collective-permute-start.16 = (bf16[768,2048]{1,0:T(8,128)(2,1)}, bf16[768,2048]{1,0:T(8,128)(2,1)}, u32[]{:S(2)}, u32[]{:S(2)}) collective-permute-start(bf16[768,2048]{1,0:T(8,128)(2,1)} %get-tuple-element.149), channel_id=1, source_target_pairs={{0,2},{2,0},{1,3},{3,1},{4,6},{6,4},{5,7},{7,5}} | collective-permute-start | bytes 9437192 | tf_op jit(solution)/shard_map/ppermute | solution.py:634
  2841.5 1.3 collective-permute-start.14
  2842.7 179.5 %collective-permute-start.22 = (bf16[512,3072]{1,0:T(8,128)(2,1)S(1)}, bf16[512,3072]{1,0:T(8,128)(2,1)}, u32[]{:S(2)}, u32[]{:S(2)}) collective-permute-start(bf16[512,3072]{1,0:T(8,128)(2,1)S(1)} %copy-done), channel_id=1, source_target_pairs={{0,4},{4,0},{1,5},{5,1},{2,6},{6,2},{3,7},{7,3}} | collective-permute-start | bytes 9437192 | tf_op jit(solution)/shard_map/ppermute | solution.py:634
  2907.3 112.2 %collective-permute-start.18 = (bf16[384,2048]{1,0:T(8,128)(2,1)}, bf16[384,2048]{1,0:T(8,128)(2,1)}, u32[]{:S(2)}, u32[]{:S(2)}) collective-permute-start(bf16[384,2048]{1,0:T(8,128)(2,1)} %get-tuple-element.159), channel_id=1, source_target_pairs={{0,2},{2,0},{1,3},{3,1},{4,6},{6,4},{5,7},{7,5}} | collective-permute-start | bytes 4718600 | tf_op jit(solution)/shard_map/ppermute | solution.py:634
  2974.7 55.2 %collective-permute-start.21 = (bf16[384,2048]{1,0:T(8,128)(2,1)}, bf16[384,2048]{1,0:T(8,128)(2,1)}, u32[]{:S(2)}, u32[]{:S(2)}) collective-permute-start(bf16[384,2048]{1,0:T(8,128)(2,1)} %get-tuple-element.177), channel_id=1, source_target_pairs={{0,2},{2,0},{1,3},{3,1},{4,6},{6,4},{5,7},{7,5}} | collective-permute-start | bytes 4718600 | tf_op jit(solution)/shard_map/ppermute | solution.py:634
  2998.1 34.5 %collective-permute-start.23 = (f32[96,128]{1,0:T(8,128)S(1)}, f32[96,128]{1,0:T(8,128)S(1)}, u32[]{:S(2)}, u32[]{:S(2)}) collective-permute-start(f32[96,128]{1,0:T(8,128)S(1)} %fusion.4), channel_id=1, source_target_pairs={{0,4},{4,0},{1,5},{5,1},{2,6},{6,2},{3,7},{7,3}} | collective-permute-start | bytes 147464 | tf_op jit(solution)/shard_map/ppermute | solution.py:634
Sparse Core Ops, SparseCore 0:
  9.5 30.0 all-gather.5
  71.3 72.6 all-gather.7
  450.9 153.2 all-gather.9
  722.9 152.9 all-gather.11
  877.2 103.1 all-gather.13
  1227.5 22.0 reduce-scatter.12
  1402.3 22.1 reduce-scatter.14
  1427.1 177.6 reduce-scatter.16
  1607.1 32.8 reduce-scatter.20
  1795.8 231.6 reduce-scatter.18
  2029.7 33.2 reduce-scatter.22

commit v4 on v3

--- a/solution.py
+++ b/solution.py
@@ -353,12 +353,12 @@
     )(*args)
 
 
-def attn_bwd_body(heads, scale, grp_ref, q_ref, k_ref, v_ref, d_ref, *rest):
+def attn_bwd_body(heads, seq, scale, grp_ref, q_ref, k_ref, v_ref, d_ref, *rest):
     dq_ref, sum_ref = rest[-2:]
-    seq, width = q_ref.shape
+    width = q_ref.shape[1]
     half = seq // 2
+    lanes = heads * (q_ref.shape[0] // seq)
     causal = lax.broadcasted_iota(jnp.int32, (half, half), 1) >= lax.broadcasted_iota(jnp.int32, (half, half), 0)
-    unroll = 8
     coef = scale * LOG2E
 
     @pl.when(pl.program_id(0) == 0)
@@ -368,50 +368,50 @@
     def col_sum(val):
         return jnp.sum(val, 0, keepdims=True)
 
-    def emit(top, bottom, start):
-        cols = pl.ds(pl.multiple_of(start, 128), 128)
-        dq_ref[:half, cols] = top.astype(BF16)
-        dq_ref[half:, cols] = bottom.astype(BF16)
+    def emit(top, bottom, start, row):
+        cols = pl.ds(start, 128)
+        dq_ref[row:row + half, cols] = top.astype(BF16)
+        dq_ref[row + half:row + seq, cols] = bottom.astype(BF16)
         sum_ref[:, cols] += jnp.sum((top + bottom).reshape(half // 8, 8, 128), axis=0)
 
-    @pl.loop(0, heads // unroll)
-    def _(i):
-        first = []
-        for j in range(unroll):
-            h = (i * unroll + j) * 128
-            cols = pl.ds(pl.multiple_of(h, 128), 128)
-            q, k, v, d = q_ref[:, cols], k_ref[:, cols], v_ref[:, cols], d_ref[:, cols]
-            first.append((h, cols, nt_dot(k[:half], q), nt_dot(k[half:], q[half:]), nt_dot(v[:half], d), nt_dot(v[half:], d[half:])))
-        second = []
-        for h, cols, s0, s1, dp0, dpc in first:
-            sa = jnp.where(causal, s0[:, :half], -1e30)
-            ea = jnp.exp2((sa - jnp.max(sa, 0, keepdims=True)) * coef)
-            pa = ea * (1.0 / col_sum(ea))
-            dpa, dpb = dp0[:, :half], dp0[:, half:]
-            dsa = (pa * (dpa - col_sum(dpa * pa)) * scale).astype(BF16)
-            sb, sc = s0[:, half:], jnp.where(causal, s1, -1e30)
-            top = jnp.max(jnp.maximum(sb, sc), 0, keepdims=True)
-            eb, ec = jnp.exp2((sb - top) * coef), jnp.exp2((sc - top) * coef)
-            inv = 1.0 / col_sum(eb + ec)
-            pb, pc = eb * inv, ec * inv
-            dot = col_sum(dpb * pb + dpc * pc)
-            dsb = (pb * (dpb - dot) * scale).astype(BF16)
-            dsc = (pc * (dpc - dot) * scale).astype(BF16)
-            p0 = jnp.concatenate([pa.astype(BF16), pb.astype(BF16)], axis=1)
-            second.append((h, cols, p0, pc.astype(BF16), dsa, dsb, dsc))
-        for h, cols, p0, p1, dsa, dsb, dsc in second:
-            q, k, d = q_ref[:, cols], k_ref[:, cols], d_ref[:, cols]
-            emit(nn_dot(p0, d), nn_dot(p1, d[half:]), h + 2 * width)
-            emit(nn_dot(jnp.concatenate([dsa, dsb], axis=1), q), nn_dot(dsc, q[half:]), h + width)
-            emit(tn_dot(dsa, k[:half]), tn_dot(jnp.concatenate([dsb, dsc], axis=0), k), h)
+    first = []
+    for lane in range(lanes):
+        h, row = lane % heads * 128, lane // heads * seq
+        rows, cols = pl.ds(row, seq), pl.ds(h, 128)
+        q, k, v, d = q_ref[rows, cols], k_ref[rows, cols], v_ref[rows, cols], d_ref[rows, cols]
+        first.append((h, row, nt_dot(k[:half], q), nt_dot(k[half:], q[half:]), nt_dot(v[:half], d), nt_dot(v[half:], d[half:])))
+    second = []
+    for h, row, s0, s1, dp0, dpc in first:
+        sa = jnp.where(causal, s0[:, :half], -1e30)
+        ea = jnp.exp2((sa - jnp.max(sa, 0, keepdims=True)) * coef)
+        pa = ea * (1.0 / col_sum(ea))
+        dpa, dpb = dp0[:, :half], dp0[:, half:]
+        dsa = (pa * (dpa - col_sum(dpa * pa)) * scale).astype(BF16)
+        sb, sc = s0[:, half:], jnp.where(causal, s1, -1e30)
+        top = jnp.max(jnp.maximum(sb, sc), 0, keepdims=True)
+        eb, ec = jnp.exp2((sb - top) * coef), jnp.exp2((sc - top) * coef)
+        inv = 1.0 / col_sum(eb + ec)
+        pb, pc = eb * inv, ec * inv
+        dot = col_sum(dpb * pb + dpc * pc)
+        dsb = (pb * (dpb - dot) * scale).astype(BF16)
+        dsc = (pc * (dpc - dot) * scale).astype(BF16)
+        p0 = jnp.concatenate([pa.astype(BF16), pb.astype(BF16)], axis=1)
+        second.append((h, row, p0, pc.astype(BF16), dsa, dsb, dsc))
+    for h, row, p0, p1, dsa, dsb, dsc in second:
+        rows, cols = pl.ds(row, seq), pl.ds(h, 128)
+        q, k, d = q_ref[rows, cols], k_ref[rows, cols], d_ref[rows, cols]
+        emit(nn_dot(p0, d), nn_dot(p1, d[half:]), h + 2 * width, row)
+        emit(nn_dot(jnp.concatenate([dsa, dsb], axis=1), q), nn_dot(dsc, q[half:]), h + width, row)
+        emit(tn_dot(dsa, k[:half]), tn_dot(jnp.concatenate([dsb, dsc], axis=0), k), h, row)
 
 
 def attn_bwd(grp, qkv, d_att, group, out_groups, width, seq, row0, total, prev):
     rows = qkv.shape[0]
+    blk = 2 * seq
     heads = width // 128
-    off = row0 // seq
-    in_specs = [pl.BlockSpec((seq, width), lambda i, c, j=j: (i, 3 * group + j)) for j in range(3)]
-    in_specs.append(pl.BlockSpec((seq, width), lambda i, c: (i + off, c[0])))
+    off = row0 // blk
+    in_specs = [pl.BlockSpec((blk, width), lambda i, c, j=j: (i, 3 * group + j)) for j in range(3)]
+    in_specs.append(pl.BlockSpec((blk, width), lambda i, c: (i + off, c[0])))
     args = [grp, qkv, qkv, qkv, d_att]
     aliases = {}
     if prev is not None:
@@ -420,17 +420,17 @@
         aliases = {5: 0}
     nheads = rows // seq * heads
     return pl.pallas_call(
-        functools.partial(attn_bwd_body, heads, 128 ** -0.5),
+        functools.partial(attn_bwd_body, heads, seq, 128 ** -0.5),
         out_shape=(
             jax.ShapeDtypeStruct((total, 3 * width * out_groups), BF16),
             jax.ShapeDtypeStruct((8, 3 * width), F32),
         ),
         grid_spec=pltpu.PrefetchScalarGridSpec(
             num_scalar_prefetch=1,
-            grid=(rows // seq,),
+            grid=(rows // blk,),
             in_specs=in_specs,
             out_specs=(
-                pl.BlockSpec((seq, 3 * width), lambda i, c: (i + off, group)),
+                pl.BlockSpec((blk, 3 * width), lambda i, c: (i + off, group)),
                 pl.BlockSpec((8, 3 * width), lambda i, c: (0, 0)),
             ),
         ),
@@ -789,7 +789,7 @@
 
         unit = half // 8
         parts = (2 * unit, 2 * unit, 2 * unit, unit, unit)
-        cut = piece + piece // 2
+        cut = piece + 3 * piece // 4
         dx, gate, lo = None, dw_ob, 0
         dx_recv, sums_n = [], []
         grads = [dqkv_own, *dqkv_oth]
@@ -839,11 +839,9 @@
                 dw_qkv = join(0, piece, dep_arr, half_a, tie(rest_a, dx), half_b[0], rest_b[0], 0, None)
                 dw_qkv = join(piece, cut - piece, dep_arr, half_a, rest_a, half_b[0], rest_b[0], 0, dw_qkv)
                 place = dw_qkv
-            if part == 4:
-                dw_qkv = join(cut, 2 * piece - cut, dep_arr, half_a, tie(rest_a, dx), half_b[1], rest_b[1], cut, dw_qkv)
-                place = dw_qkv
             dx = lax.dynamic_update_slice(dx, tie(dx_recv[part], place), (other * half + lo, 0))
             lo += rows
+        dw_qkv = join(cut, 2 * piece - cut, dep_arr, half_a, tie(rest_a, dx), half_b[1], rest_b[1], cut, dw_qkv)
         total = total + tie(dep_in, dx)
         db_o = total[-nv:]
         nq = 3 * nv

time: 3050 us -> 3140 us (1.030)
  waiting for transfers between devices: 1050 us -> 1150 us
    ppermute x24, waiting for transfers between devices: 1050 us -> 1150 us  [swap(): return lax.ppermute(val, axis, SWAP)]
  transfers between devices with their start and end apart: 35 -> 35, of which waited for: 12 -> 11; matrix products, arithmetic and copies ran while one was open for 16% -> 15% of each run, Pallas kernels for 40% -> 38%
where the time goes in v4:
time: 3140 us; the launch traced here: 3130 us
  Pallas kernels  1400 us (45%)
  waiting for transfers between devices  1150 us (37%)
  matrix products  383 us (12%)
  other arithmetic  76.9 us (2%)
  local copies, waits for them, and re-layouts  76.7 us (2%)
    ppermute x24, waiting for transfers between devices, swap(): return lax.ppermute(val, axis, SWAP)  1150 us
    pallas_call x6, Pallas kernels, weight_grad_call(): pl.pallas_call(weight_grad_body, out_shape=jax.ShapeDtypeStruct((full, co...  469 us
    pallas_call x5, Pallas kernels, dx_part(): pl.pallas_call(functools.partial(dx_body, row0, total, rows // blk, y_pai...  431 us
    dot_general x4, matrix products, nn_dot(): lax.dot_general(lhs, rhs, (((1,), (0,)), ((), ())), preferred_element_typ...  255 us
    pallas_call x2, Pallas kernels, project_rows(): pl.pallas_call(project_body, out_shape=jax.ShapeDtypeStruct((total, width...  173 us
    dot_general x2, matrix products, nt_dot(): lax.dot_general(lhs, rhs, (((1,), (1,)), ((), ())), preferred_element_typ...  128 us
    pallas_call x4, Pallas kernels, attn_bwd(): pl.pallas_call(functools.partial(attn_bwd_body, heads, seq, 128 ** (-0.5)...  107 us
    pallas_call x4, Pallas kernels, attn_fwd(): pl.pallas_call(functools.partial(attn_fwd_body, heads, 128 ** (-0.5)), ou...  71.8 us
  transfers between devices with their start and end apart: 35, of which 11 were waited for; matrix products, arithmetic and copies ran while one was open for 15% of the time, Pallas kernels for 38%

profile of v4, /device:TPU:0, one launch (start us, length us, event | category | flops | bytes accessed | tf_op | source)
XLA Modules:
  0.0 3129.5 jit_solution(1215372050731844777)
XLA Ops:
  8.0 5.4 fusion.5
  13.4 8.9 constant_dynamic-slice_fusion.5
  22.3 6.7 pad_maximum_fusion
  29.0 8.4 constant_dynamic-slice_fusion.4
  37.4 4.7 constant_dynamic-slice_fusion.3
  42.1 10.7 constant_dynamic-slice_fusion.2
  52.8 18.3 regroup.1
  71.2 3.1 collective-permute-start.1
  79.7 2.0 collective-permute-start.2
  81.6 14.6 constant_dynamic-slice_fusion.1.rhs_ref
  96.3 16.8 convert_reduce_fusion
  113.1 64.8 %fusion.6 = f32[3072,4096]{1,0:T(8,128)} fusion(bf16[3072,2048]{1,0:T(8,128)(2,1)} %constant_dynamic-slice_fusion.1.rhs_ref, bf16[4096,2048]{1,0:T(8,128)(2,1)} %all-gather.6.cloned.1.call-done.w0_ref.w1_ref.w2_ref.w_ref), kind=kOutput, calls=%fused_computation.77 | convolution fusion | flops 51539607552 | bytes 79691776 | tf_op jit(solution)/shard_map/dot_general | solution.py:19
  177.9 168.2 %collective-permute-done.2 = f32[96,128]{1,0:T(8,128)} collective-permute-done((f32[96,128]{1,0:T(8,128)}, f32[96,128]{1,0:T(8,128)}, u32[]{:S(2)}, u32[]{:S(2)}) %collective-permute-start.2) | collective-permute-done | bytes 49184 | tf_op jit(solution)/shard_map/ppermute | solution.py:634
  348.7 15.5 ln_fwd.2
  364.2 86.5 %project.2.q_ref.k_ref.v_ref.rest_0_ = bf16[3072,6144]{1,0:T(8,128)(2,1)} custom-call(bf16[3072,4096]{1,0:T(8,128)(2,1)} %get-tuple-element.110.xn_ref.rest_0_, bf16[4096,6144]{1,0:T(8,128)(2,1)} %all-gather.8.cloned.1.call-done.w_ref.w_own, f32[1,6144]{1,0:T(1,128)} %bitcast.74), custom_call_target="tpu_custom_call" | custom-call | flops 77309411328 | bytes 50331648 | tf_op jit(solution)/shard_map/project/pallas_call | solution.py:544
  452.8 19.5 attn_fwd.4.rest_0_
  472.4 117.1 %collective-permute-done.3.recv_ref.x1_ref = bf16[1536,2048]{1,0:T(8,128)(2,1)} collective-permute-done((bf16[1536,2048]{1,0:T(8,128)(2,1)}, bf16[1536,2048]{1,0:T(8,128)(2,1)}, u32[]{:S(2)}, u32[]{:S(2)}) %collective-permute-start.3) | collective-permute-done | bytes 6291488 | tf_op jit(solution)/shard_map/ppermute | solution.py:634
  589.5 15.5 ln_fwd.3
  605.0 86.6 %project.3.q_ref.k_ref.v_ref = bf16[3072,6144]{1,0:T(8,128)(2,1)} custom-call(bf16[3072,4096]{1,0:T(8,128)(2,1)} %get-tuple-element.120.xn_ref.lhs_ref, bf16[4096,6144]{1,0:T(8,128)(2,1)} %all-gather.8.cloned.1.call-done.w_ref.w_own, f32[1,6144]{1,0:T(1,128)} %bitcast.75, ...), custom_call_target="tpu_custom_call", output_to_operand_aliasing={{}: (3, {})} | custom-call | flops 77309411328 | bytes 50331648 | tf_op jit(solution)/shard_map/project/pallas_call | solution.py:544
  691.5 17.4 attn_fwd.5.rest_0_
  708.9 13.8 collective-permute-done.6
  725.6 92.5 %add_convert_fusion.2.q_ref.k_ref.v_ref = bf16[3072,3072]{1,0:T(8,128)(2,1)} fusion(f32[3072]{0:T(1024)S(1)} %get-tuple-element.205, bf16[3072,4096]{1,0:T(8,128)(2,1)} %get-tuple-element.120.xn_ref.lhs_ref, bf16[4096,3072]{1,0:T(8,128)(2,1)} %all-gather.10.cloned.1.call-done.w_a), kind=kOutput, calls=%fused_computation.3 | convolution fusion | flops 77328285696 | bytes 69218304 | tf_op jit(solution)/shard_map/dot_general | solution.py:27
  818.2 17.4 attn_fwd.6.a0_ref.a1_ref.a2_ref.rest_0_
  835.7 47.8 %out_early.1.part_ref = f32[3072,2048]{1,0:T(8,128)} custom-call(s32[1]{0:T(128)} %bitcast.col_ref, bf16[3072,4096]{1,0:T(8,128)(2,1)} %attn_fwd.6.a0_ref.a1_ref.a2_ref.rest_0_, bf16[3072,4096]{1,0:T(8,128)(2,1)} %attn_fwd.6.a0_ref.a1_ref.a2_ref.rest_0_, bf16[3072,4096]{1,0:T(8,128)(2,1)} %attn_fwd.6.a0_ref.a1_ref.a2_ref.rest_0_, ...), custom_call_target="tpu_custom_call" | custom-call | flops 38654705664 | bytes 75497472 | tf_op jit(solution)/shard_map/out_early/pallas_call | solution.py:456
  883.5 92.3 %add_convert_fusion.1.q_ref.k_ref.v_ref = bf16[3072,3072]{1,0:T(8,128)(2,1)} fusion(f32[3072]{0:T(1024)S(1)} %copy-done.18, bf16[3072,4096]{1,0:T(8,128)(2,1)} %get-tuple-element.120.xn_ref.lhs_ref, bf16[4096,3072]{1,0:T(8,128)(2,1)} %all-gather.12.cloned.1.call-done.w_b), kind=kOutput, calls=%fused_computation.2 | convolution fusion | flops 77328285696 | bytes 69218304 | tf_op jit(solution)/shard_map/dot_general | solution.py:27
  975.9 17.4 attn_fwd.7.att_ref.lhs_ref
  993.3 35.0 %add_convert_fusion.8 = bf16[1536,2048]{1,0:T(8,128)(2,1)} fusion(bf16[1536,2048]{1,0:T(8,128)(2,1)} %collective-permute-done.1.recv_ref.x0_ref, f32[2048]{0:T(1024)S(1)} %copy-done.19, bf16[4096,2048]{1,0:T(8,128)(2,1)} %all-gather.14.cloned.1.call-done, bf16[3072,4096]{1,0:T(8,128)(2,1)} %attn_fwd.7.att_ref.lhs_ref), kind=kOutput, calls=%fused_computation.13 | convolution fusion | flops 25782386688 | bytes 41951232 | tf_op jit(solution)/shard_map/dot_general | solution.py:27
  1028.4 34.9 %add_convert_fusion.7 = bf16[1536,2048]{1,0:T(8,128)(2,1)} fusion(bf16[1536,2048]{1,0:T(8,128)(2,1)} %collective-permute-done.3.recv_ref.x1_ref, f32[2048]{0:T(1024)S(1)} %copy-done.19, bf16[4096,2048]{1,0:T(8,128)(2,1)} %all-gather.14.cloned.1.call-done, bf16[3072,4096]{1,0:T(8,128)(2,1)} %attn_fwd.7.att_ref.lhs_ref), kind=kOutput, calls=%fused_computation.10 | convolution fusion | flops 25782386688 | bytes 41951232 | tf_op jit(solution)/shard_map/dot_general | solution.py:27
  1063.2 25.1 out_rows.1.rest_3_
  1088.4 16.4 collective-permute-done.4.rhs_ref.dyr_ref
  1104.8 63.0 %add_convert_fusion.d_ref = bf16[3072,4096]{1,0:T(8,128)(2,1)} fusion(f32[3072,4096]{1,0:T(8,128)} %fusion.6, bf16[3072,2048]{1,0:T(8,128)(2,1)} %collective-permute-done.4.rhs_ref.dyr_ref, bf16[4096,2048]{1,0:T(8,128)(2,1)} %all-gather.14.cloned.1.call-done), kind=kOutput, calls=%fused_computation | convolution fusion | flops 51564773376 | bytes 104857600 | tf_op jit(solution)/shard_map/dot_general | solution.py:19
  1167.8 59.7 %weight_grad.6 = bf16[4096,2048]{1,0:T(8,128)(2,1)} custom-call(bf16[3072,4096]{1,0:T(8,128)(2,1)} %attn_fwd.7.att_ref.lhs_ref, bf16[3072,2048]{1,0:T(8,128)(2,1)} %collective-permute-done.4.rhs_ref.dyr_ref), custom_call_target="tpu_custom_call" | custom-call | flops 51539607552 | bytes 50331648 | tf_op jit(solution)/shard_map/weight_grad/pallas_call | solution.py:512
  1227.5 26.9 attn_bwd.4
  1254.4 86.6 %weight_grad.7 = bf16[4096,3072]{1,0:T(8,128)(2,1)} custom-call(bf16[3072,4096]{1,0:T(8,128)(2,1)} %get-tuple-element.120.xn_ref.lhs_ref, bf16[3072,3072]{1,0:T(8,128)(2,1)} %get-tuple-element.160.rhs_ref.d_a), custom_call_target="tpu_custom_call" | custom-call | flops 77309411328 | bytes 50331648 | tf_op jit(solution)/shard_map/weight_grad/pallas_call | solution.py:512
  1341.0 59.7 %weight_grad.8 = bf16[4096,2048]{1,0:T(8,128)(2,1)} custom-call(bf16[3072,4096]{1,0:T(8,128)(2,1)} %attn_fwd.7.att_ref.lhs_ref, bf16[3072,2048]{1,0:T(8,128)(2,1)} %constant_dynamic-slice_fusion.1.rhs_ref), custom_call_target="tpu_custom_call" | custom-call | flops 51539607552 | bytes 50331648 | tf_op jit(solution)/shard_map/weight_grad/pallas_call | solution.py:512
  1401.5 26.9 attn_bwd.7
  1428.4 89.1 %weight_grad.10 = bf16[4096,3072]{1,0:T(8,128)(2,1)} custom-call(bf16[3072,4096]{1,0:T(8,128)(2,1)} %get-tuple-element.120.xn_ref.lhs_ref, bf16[3072,3072]{1,0:T(8,128)(2,1)} %get-tuple-element.140.rhs_ref.d_b), custom_call_target="tpu_custom_call" | custom-call | flops 77309411328 | bytes 50331648 | tf_op jit(solution)/shard_map/weight_grad/pallas_call | solution.py:512
  1517.6 25.3 attn_bwd.5
  1542.9 152.2 %collective-permute-done.7 = bf16[2048,2048]{1,0:T(8,128)(2,1)} collective-permute-done((bf16[2048,2048]{1,0:T(8,128)(2,1)}, bf16[2048,2048]{1,0:T(8,128)(2,1)}, u32[]{:S(2)}, u32[]{:S(2)}) %collective-permute-start.7) | collective-permute-done | bytes 8388640 | tf_op jit(solution)/shard_map/ppermute | solution.py:634
  1695.1 10.5 add_convert_fusion.5
  1705.6 86.6 %weight_grad.11 = bf16[4096,3072]{1,0:T(8,128)(2,1)} custom-call(bf16[3072,4096]{1,0:T(8,128)(2,1)} %get-tuple-element.120.xn_ref.lhs_ref, bf16[3072,6144]{1,0:T(8,128)(2,1)} %get-tuple-element.136.rest_0_.rhs_ref), custom_call_target="tpu_custom_call" | custom-call | flops 77309411328 | bytes 50331648 | tf_op jit(solution)/shard_map/weight_grad/pallas_call | solution.py:512
  1792.2 27.6 attn_bwd.6
  1819.8 87.8 %weight_grad.9 = bf16[4096,3072]{1,0:T(8,128)(2,1)} custom-call(bf16[3072,4096]{1,0:T(8,128)(2,1)} %get-tuple-element.120.xn_ref.lhs_ref, bf16[3072,6144]{1,0:T(8,128)(2,1)} %get-tuple-element.137.rhs_ref.d_own), custom_call_target="tpu_custom_call" | custom-call | flops 77309411328 | bytes 50331648 | tf_op jit(solution)/shard_map/weight_grad/pallas_call | solution.py:512
  1913.9 106.0 %dx_part.5 = (bf16[6144,2048]{1,0:T(8,128)(2,1)}, bf16[768,2048]{1,0:T(8,128)(2,1)}, f32[8,4096]{1,0:T(8,128)}, f32[8,4096]{1,0:T(8,128)}) custom-call(s32[1]{0:T(128)} %bitcast.col_ref, bf16[3072,6144]{1,0:T(8,128)(2,1)} %get-tuple-element.137.rhs_ref.d_own, bf16[3072,3072]{1,0:T(8,128)(2,1)} %get-tuple-element.160.rhs_ref.d_a, ...), custom_call_target="tpu_custom_call" | custom-call | flops 77309411328 | bytes 201326592 | tf_op jit(solution)/shard_map/dx_part/pallas_call | solution.py:289
  2019.9 296.2 %collective-permute-done.8 = bf16[1024,3072]{1,0:T(8,128)(2,1)} collective-permute-done((bf16[1024,3072]{1,0:T(8,128)(2,1)}, bf16[1024,3072]{1,0:T(8,128)(2,1)}, u32[]{:S(2)}, u32[]{:S(2)}) %collective-permute-start.8) | collective-permute-done | bytes 6291488 | tf_op jit(solution)/shard_map/ppermute | solution.py:634
  2317.9 10.0 add_convert_fusion.6.own_ref
  2327.9 105.1 %dx_part.6 = (bf16[6144,2048]{1,0:T(8,128)(2,1)}, bf16[768,2048]{1,0:T(8,128)(2,1)}, f32[8,4096]{1,0:T(8,128)}, f32[8,4096]{1,0:T(8,128)}) custom-call(s32[1]{0:T(128)} %bitcast.col_ref, bf16[3072,6144]{1,0:T(8,128)(2,1)} %get-tuple-element.137.rhs_ref.d_own, bf16[3072,3072]{1,0:T(8,128)(2,1)} %get-tuple-element.160.rhs_ref.d_a, ...), custom_call_target="tpu_custom_call", output_to_operand_aliasing={{0}: (14, {})} | custom-call | flops 77309411328 | bytes 201326592 | tf_op jit(solution)/shard_map/dx_part/pallas_call | solution.py:289
  2433.0 152.6 %collective-permute-done.9 = bf16[2048,3072]{1,0:T(8,128)(2,1)} collective-permute-done((bf16[2048,3072]{1,0:T(8,128)(2,1)}, bf16[2048,3072]{1,0:T(8,128)(2,1)}, u32[]{:S(2)}, u32[]{:S(2)}) %collective-permute-start.9) | collective-permute-done | bytes 12582944 | tf_op jit(solution)/shard_map/ppermute | solution.py:634
  2585.7 14.2 add_convert_fusion.3.half_ref
  2599.9 3.6 add_convert_fusion.9.half_ref
  2603.5 110.2 %dx_part.7 = (bf16[6144,2048]{1,0:T(8,128)(2,1)}, bf16[768,2048]{1,0:T(8,128)(2,1)}, f32[8,4096]{1,0:T(8,128)}, f32[8,4096]{1,0:T(8,128)}, bf16[6144,2048]{1,0:T(8,128)(2,1)}) custom-call(s32[1]{0:T(128)} %bitcast.col_ref, bf16[3072,6144]{1,0:T(8,128)(2,1)} %get-tuple-element.137.rhs_ref.d_own, ...), custom_call_target="tpu_custom_call", output_to_operand_aliasing={{0}: (14, {}), {4}: (17, {})} | custom-call | flops 77309411328 | bytes 201326592 | tf_op jit(solution)/shard_map/dx_part/pallas_call | solution.py:289
  2717.7 54.9 %dx_part.8 = (bf16[6144,2048]{1,0:T(8,128)(2,1)}, bf16[384,2048]{1,0:T(8,128)(2,1)}, f32[8,4096]{1,0:T(8,128)}, f32[8,4096]{1,0:T(8,128)}) custom-call(s32[1]{0:T(128)} %bitcast.col_ref, bf16[3072,6144]{1,0:T(8,128)(2,1)} %get-tuple-element.137.rhs_ref.d_own, bf16[3072,3072]{1,0:T(8,128)(2,1)} %get-tuple-element.160.rhs_ref.d_a, ...), custom_call_target="tpu_custom_call", output_to_operand_aliasing={{0}: (14, {})} | custom-call | flops 38654705664 | bytes 100663296 | tf_op jit(solution)/shard_map/dx_part/pallas_call | solution.py:289
  2772.7 55.1 %dx_part.9 = (bf16[6144,2048]{1,0:T(8,128)(2,1)}, bf16[384,2048]{1,0:T(8,128)(2,1)}, f32[8,4096]{1,0:T(8,128)}, f32[8,4096]{1,0:T(8,128)}) custom-call(s32[1]{0:T(128)} %bitcast.col_ref, bf16[3072,6144]{1,0:T(8,128)(2,1)} %get-tuple-element.137.rhs_ref.d_own, bf16[3072,3072]{1,0:T(8,128)(2,1)} %get-tuple-element.160.rhs_ref.d_a, ...), custom_call_target="tpu_custom_call", output_to_operand_aliasing={{0}: (14, {})} | custom-call | flops 38654705664 | bytes 100663296 | tf_op jit(solution)/shard_map/dx_part/pallas_call | solution.py:289
  2830.1 4.3 collective-permute-done.13
  2837.8 10.4 add_convert_fusion.4
  2848.3 4.0 constant_dynamic-update-slice_fusion.21
  2852.2 53.4 %collective-permute-done.16 = bf16[768,2048]{1,0:T(8,128)(2,1)} collective-permute-done((bf16[768,2048]{1,0:T(8,128)(2,1)}, bf16[768,2048]{1,0:T(8,128)(2,1)}, u32[]{:S(2)}, u32[]{:S(2)}) %collective-permute-start.16) | collective-permute-done | bytes 3145760 | tf_op jit(solution)/shard_map/ppermute | solution.py:634
  2907.1 4.0 constant_dynamic-update-slice_fusion.20
  2911.1 4.0 constant_dynamic-update-slice_fusion.19
  2915.6 174.7 %collective-permute-done.20.rest_ref = bf16[1792,3072]{1,0:T(8,128)(2,1)} collective-permute-done((bf16[1792,3072]{1,0:T(8,128)(2,1)}, bf16[1792,3072]{1,0:T(8,128)(2,1)}, u32[]{:S(2)}, u32[]{:S(2)}) %collective-permute-start.20) | collective-permute-done | bytes 11010080 | tf_op jit(solution)/shard_map/ppermute | solution.py:634
  3090.3 13.2 join.3.rest_0_
  3103.5 10.1 join.4.rest_0_
  3113.6 2.7 constant_dynamic-update-slice_fusion.18
  3118.8 4.0 join.5
  (161 shorter events, 37.0 us)
Async XLA Ops:
  7.2 105.9 %all-gather.6.cloned.1.call-start = ((), (), s32[]{:S(2)}) async-start(), calls=%async_computation.6 | async-start | bytes 25165824 | tf_op jit(solution)/shard_map/all_gather | solution.py:640
  7.9 356.3 %all-gather.8.cloned.1.call-start = ((), (), s32[]{:S(2)}) async-start(), calls=%async_computation.7 | async-start | bytes 75497472 | tf_op jit(solution)/shard_map/all_gather | solution.py:640
  71.1 3.2 copy-start.13
  71.1 3.2 copy-start.20
  71.1 3.8 copy-start.21
  71.1 4.4 copy-start.17
  71.1 654.5 %all-gather.10.cloned.1.call-start = ((), (), s32[]{:S(2)}) async-start(), calls=%async_computation.8 | async-start | bytes 31457280 | tf_op jit(solution)/shard_map/all_gather | solution.py:640
  71.2 277.5 %collective-permute-start.1 = (bf16[1536,2048]{1,0:T(8,128)(2,1)}, bf16[1536,2048]{1,0:T(8,128)(2,1)}, u32[]{:S(2)}, u32[]{:S(2)}) collective-permute-start(bf16[1536,2048]{1,0:T(8,128)(2,1)} %constant_dynamic-slice_fusion.5), channel_id=1, source_target_pairs={{0,2},{2,0},{1,3},{3,1},{4,6},{6,4},{5,7},{7,5}} | collective-permute-start | bytes 18874376 | tf_op jit(solution)/shard_map/ppermute | solution.py:634
  74.2 376.5 %collective-permute-start = (bf16[1024,3072]{1,0:T(8,128)(2,1)}, bf16[1024,3072]{1,0:T(8,128)(2,1)}, u32[]{:S(2)}, u32[]{:S(2)}) collective-permute-start(bf16[1024,3072]{1,0:T(8,128)(2,1)} %get-tuple-element.99), channel_id=1, source_target_pairs={{0,2},{2,0},{1,3},{3,1},{4,6},{6,4},{5,7},{7,5}} | collective-permute-start | bytes 18874376 | tf_op jit(solution)/shard_map/ppermute | solution.py:634
  78.5 1.2 copy-start.22
  79.7 266.4 %collective-permute-start.2 = (f32[96,128]{1,0:T(8,128)}, f32[96,128]{1,0:T(8,128)}, u32[]{:S(2)}, u32[]{:S(2)}) collective-permute-start(f32[96,128]{1,0:T(8,128)} %constant_dynamic-update-slice_fusion), channel_id=1, source_target_pairs={{0,2},{2,0},{1,3},{3,1},{4,6},{6,4},{5,7},{7,5}} | collective-permute-start | bytes 147464 | tf_op jit(solution)/shard_map/ppermute | solution.py:634
  450.7 432.8 %all-gather.12.cloned.1.call-start = ((), (), s32[]{:S(2)}) async-start(), calls=%async_computation.9 | async-start | bytes 31457280 | tf_op jit(solution)/shard_map/all_gather | solution.py:640
  450.8 138.7 %collective-permute-start.3 = (bf16[1536,2048]{1,0:T(8,128)(2,1)}, bf16[1536,2048]{1,0:T(8,128)(2,1)}, u32[]{:S(2)}, u32[]{:S(2)}) collective-permute-start(bf16[1536,2048]{1,0:T(8,128)(2,1)} %constant_dynamic-slice_fusion.4), channel_id=1, source_target_pairs={{0,2},{2,0},{1,3},{3,1},{4,6},{6,4},{5,7},{7,5}} | collective-permute-start | bytes 18874376 | tf_op jit(solution)/shard_map/ppermute | solution.py:634
  452.6 270.2 %collective-permute-start.6 = (bf16[1024,3072]{1,0:T(8,128)(2,1)}, bf16[1024,3072]{1,0:T(8,128)(2,1)}, u32[]{:S(2)}, u32[]{:S(2)}) collective-permute-start(bf16[1024,3072]{1,0:T(8,128)(2,1)} %get-tuple-element.101), channel_id=1, source_target_pairs={{0,2},{2,0},{1,3},{3,1},{4,6},{6,4},{5,7},{7,5}} | collective-permute-start | bytes 18874376 | tf_op jit(solution)/shard_map/ppermute | solution.py:634
  722.8 270.5 %all-gather.14.cloned.1.call-start = ((), (), s32[]{:S(2)}) async-start(), calls=%async_computation.10 | async-start | bytes 20971520 | tf_op jit(solution)/shard_map/all_gather | solution.py:640
  722.8 112.8 %collective-permute-start.5 = (bf16[1024,2048]{1,0:T(8,128)(2,1)}, bf16[1024,2048]{1,0:T(8,128)(2,1)}, u32[]{:S(2)}, u32[]{:S(2)}) collective-permute-start(bf16[1024,2048]{1,0:T(8,128)(2,1)} %constant_dynamic-slice_fusion.3), channel_id=1, source_target_pairs={{0,2},{2,0},{1,3},{3,1},{4,6},{6,4},{5,7},{7,5}} | collective-permute-start | bytes 12582920 | tf_op jit(solution)/shard_map/ppermute | solution.py:634
  835.6 418.8 %reduce-scatter.13.cloned.1.call-start = ((), (), s32[]{:S(2)}) async-start(), calls=%async_computation.11 | async-start | bytes 25165824 | tf_op jit(solution)/shard_map/reduce_scatter | solution.py:643
  835.7 269.1 %collective-permute-start.4 = (bf16[3072,2048]{1,0:T(8,128)(2,1)}, bf16[3072,2048]{1,0:T(8,128)(2,1)}, u32[]{:S(2)}, u32[]{:S(2)}) collective-permute-start(bf16[3072,2048]{1,0:T(8,128)(2,1)} %constant_dynamic-slice_fusion.2), channel_id=1, source_target_pairs={{0,2},{2,0},{1,3},{3,1},{4,6},{6,4},{5,7},{7,5}} | collective-permute-start | bytes 37748744 | tf_op jit(solution)/shard_map/ppermute | solution.py:634
  835.7 47.8 %copy-start.18 = (f32[3072]{0:T(1024)S(1)}, f32[3072]{0:T(1024)}, u32[]{:S(2)}) copy-start(f32[3072]{0:T(1024)} %get-tuple-element.204) | copy-start | bytes 36868
  975.9 17.5 copy-start.19
  1227.5 467.6 %reduce-scatter.15.cloned.1.call-start = ((), (), s32[]{:S(2)}) async-start(), calls=%async_computation.12 | async-start | bytes 25165824 | tf_op jit(solution)/shard_map/reduce_scatter | solution.py:643
  1400.7 511.1 %reduce-scatter.17.cloned.1.call-start = ((), (), s32[]{:S(2)}) async-start(), calls=%async_computation.13 | async-start | bytes 31457280 | tf_op jit(solution)/shard_map/reduce_scatter | solution.py:643
  1401.5 512.0 %reduce-scatter.21.cloned.1.call-start = ((), (), s32[]{:S(2)}) async-start(), calls=%async_computation.15 | async-start | bytes 37748736
  1517.5 800.4 %reduce-scatter.19.cloned.1.call-start = ((), (), s32[]{:S(2)}) async-start(), calls=%async_computation.14 | async-start | bytes 31457280 | tf_op jit(solution)/shard_map/reduce_scatter | solution.py:643
  1517.5 177.6 %collective-permute-start.7 = (bf16[2048,2048]{1,0:T(8,128)(2,1)}, bf16[2048,2048]{1,0:T(8,128)(2,1)}, u32[]{:S(2)}, u32[]{:S(2)}) collective-permute-start(bf16[2048,2048]{1,0:T(8,128)(2,1)} %reduce-scatter.13.cloned.1.call-done), channel_id=1, source_target_pairs={{0,2},{2,0},{1,3},{3,1},{4,6},{6,4},{5,7},{7,5}} | collective-permute-start | bytes 25165832 | tf_op jit(solution)/shard_map/ppermute | solution.py:634
  1792.2 793.5 %reduce-scatter.23.cloned.1.call-start = ((), (), s32[]{:S(2)}) async-start(), calls=%async_computation.16 | async-start | bytes 37748736
  1907.6 2.1 copy-start.9
  1907.6 2.1 copy-start.11
  1907.6 2.2 copy-start.10
  1907.6 4.1 copy-start.12
  1907.7 695.8 %collective-permute-start.11 = (bf16[1536,2048]{1,0:T(8,128)(2,1)}, bf16[1536,2048]{1,0:T(8,128)(2,1)}, u32[]{:S(2)}, u32[]{:S(2)}) collective-permute-start(bf16[1536,2048]{1,0:T(8,128)(2,1)} %add_convert_fusion.7), channel_id=1, source_target_pairs={{0,2},{2,0},{1,3},{3,1},{4,6},{6,4},{5,7},{7,5}} | collective-permute-start | bytes 18874376 | tf_op jit(solution)/shard_map/ppermute | solution.py:634
  1909.6 693.9 %collective-permute-start.10 = (bf16[1536,2048]{1,0:T(8,128)(2,1)}, bf16[1536,2048]{1,0:T(8,128)(2,1)}, u32[]{:S(2)}, u32[]{:S(2)}) collective-permute-start(bf16[1536,2048]{1,0:T(8,128)(2,1)} %add_convert_fusion.8), channel_id=1, source_target_pairs={{0,2},{2,0},{1,3},{3,1},{4,6},{6,4},{5,7},{7,5}} | collective-permute-start | bytes 18874376 | tf_op jit(solution)/shard_map/ppermute | solution.py:634
  1909.9 109.9 %copy-start.23 = (f32[10240]{0:T(1024)}, f32[10240]{0:T(1024)S(1)}, u32[]{:S(2)}) copy-start(f32[10240]{0:T(1024)S(1)} %slice_dynamic-update-slice_fusion) | copy-start | bytes 122884
  1909.9 924.6 %collective-permute-start.15 = (bf16[2048,2048]{1,0:T(8,128)(2,1)}, bf16[2048,2048]{1,0:T(8,128)(2,1)}, u32[]{:S(2)}, u32[]{:S(2)}) collective-permute-start(bf16[2048,2048]{1,0:T(8,128)(2,1)} %add_convert_fusion.5), channel_id=1, source_target_pairs={{0,4},{4,0},{1,5},{5,1},{2,6},{6,2},{3,7},{7,3}} | collective-permute-start | bytes 25165832 | tf_op jit(solution)/shard_map/ppermute | solution.py:634
  1911.8 108.1 %copy-start.15 = (f32[10240]{0:T(1024)}, f32[10240]{0:T(1024)S(1)}, u32[]{:S(2)}) copy-start(f32[10240]{0:T(1024)S(1)} %slice_dynamic-update-slice_fusion.5) | copy-start | bytes 122884
  1911.8 404.2 %collective-permute-start.8 = (bf16[1024,3072]{1,0:T(8,128)(2,1)}, bf16[1024,3072]{1,0:T(8,128)(2,1)}, u32[]{:S(2)}, u32[]{:S(2)}) collective-permute-start(bf16[1024,3072]{1,0:T(8,128)(2,1)} %reduce-scatter.17.cloned.1.call-done), channel_id=1, source_target_pairs={{0,2},{2,0},{1,3},{3,1},{4,6},{6,4},{5,7},{7,5}} | collective-permute-start | bytes 18874376 | tf_op jit(solution)/shard_map/ppermute | solution.py:634
  1913.5 672.2 %collective-permute-start.9 = (bf16[2048,3072]{1,0:T(8,128)(2,1)}, bf16[2048,3072]{1,0:T(8,128)(2,1)}, u32[]{:S(2)}, u32[]{:S(2)}) collective-permute-start(bf16[2048,3072]{1,0:T(8,128)(2,1)} %reduce-scatter.21.cloned.1.call-done), channel_id=1, source_target_pairs={{0,2},{2,0},{1,3},{3,1},{4,6},{6,4},{5,7},{7,5}} | collective-permute-start | bytes 37748744 | tf_op jit(solution)/shard_map/ppermute | solution.py:634
  2316.0 513.8 %collective-permute-start.12 = (bf16[768,2048]{1,0:T(8,128)(2,1)}, bf16[768,2048]{1,0:T(8,128)(2,1)}, u32[]{:S(2)}, u32[]{:S(2)}) collective-permute-start(bf16[768,2048]{1,0:T(8,128)(2,1)} %get-tuple-element.143), channel_id=1, source_target_pairs={{0,2},{2,0},{1,3},{3,1},{4,6},{6,4},{5,7},{7,5}} | collective-permute-start | bytes 9437192 | tf_op jit(solution)/shard_map/ppermute | solution.py:634
  2713.7 123.9 %collective-permute-start.17 = (bf16[768,2048]{1,0:T(8,128)(2,1)}, bf16[768,2048]{1,0:T(8,128)(2,1)}, u32[]{:S(2)}, u32[]{:S(2)}) collective-permute-start(bf16[768,2048]{1,0:T(8,128)(2,1)} %get-tuple-element.156), channel_id=1, source_target_pairs={{0,2},{2,0},{1,3},{3,1},{4,6},{6,4},{5,7},{7,5}} | collective-permute-start | bytes 9437192 | tf_op jit(solution)/shard_map/ppermute | solution.py:634
  2715.6 199.4 %collective-permute-start.19 = (bf16[1024,3072]{1,0:T(8,128)(2,1)}, bf16[1024,3072]{1,0:T(8,128)(2,1)}, u32[]{:S(2)}, u32[]{:S(2)}) collective-permute-start(bf16[1024,3072]{1,0:T(8,128)(2,1)} %add_convert_fusion.6.own_ref), channel_id=1, source_target_pairs={{0,4},{4,0},{1,5},{5,1},{2,6},{6,2},{3,7},{7,3}} | collective-permute-start | bytes 18874376 | tf_op jit(solution)/shard_map/ppermute | solution.py:634
  2717.1 373.2 %collective-permute-start.20 = (bf16[1792,3072]{1,0:T(8,128)(2,1)}, bf16[1792,3072]{1,0:T(8,128)(2,1)}, u32[]{:S(2)}, u32[]{:S(2)}) collective-permute-start(bf16[1792,3072]{1,0:T(8,128)(2,1)} %add_convert_fusion.3.half_ref), channel_id=1, source_target_pairs={{0,4},{4,0},{1,5},{5,1},{2,6},{6,2},{3,7},{7,3}} | collective-permute-start | bytes 33030152 | tf_op jit(solution)/shard_map/ppermute | solution.py:634
  2772.6 55.2 %copy-start.2 = (f32[8,4096]{1,0:T(8,128)S(1)}, f32[8,4096]{1,0:T(8,128)}, u32[]{:S(2)}) copy-start(f32[8,4096]{1,0:T(8,128)} %get-tuple-element.165) | copy-start | bytes 393220
  2772.6 55.2 %copy-start.4 = (f32[8,4096]{1,0:T(8,128)S(1)}, f32[8,4096]{1,0:T(8,128)}, u32[]{:S(2)}) copy-start(f32[8,4096]{1,0:T(8,128)} %get-tuple-element.166) | copy-start | bytes 393220
  2772.6 55.2 %copy-start.6 = (f32[8,4096]{1,0:T(8,128)S(1)}, f32[8,4096]{1,0:T(8,128)}, u32[]{:S(2)}) copy-start(f32[8,4096]{1,0:T(8,128)} %get-tuple-element.167) | copy-start | bytes 393220
  2772.6 55.2 %copy-start.8 = (f32[8,4096]{1,0:T(8,128)S(1)}, f32[8,4096]{1,0:T(8,128)}, u32[]{:S(2)}) copy-start(f32[8,4096]{1,0:T(8,128)} %get-tuple-element.168) | copy-start | bytes 393220
  2772.6 56.2 %copy-start.16 = (f32[10240]{0:T(1024)S(1)}, f32[10240]{0:T(1024)}, u32[]{:S(2)}) copy-start(f32[10240]{0:T(1024)} %copy-done.15) | copy-start | bytes 122884
  2772.6 56.2 %copy-start.24 = (f32[10240]{0:T(1024)S(1)}, f32[10240]{0:T(1024)}, u32[]{:S(2)}) copy-start(f32[10240]{0:T(1024)} %copy-done.23) | copy-start | bytes 122884
  2772.6 56.2 %copy-start.1 = (f32[8,4096]{1,0:T(8,128)S(1)}, f32[8,4096]{1,0:T(8,128)}, u32[]{:S(2)}) copy-start(f32[8,4096]{1,0:T(8,128)} %get-tuple-element.170) | copy-start | bytes 393220
  2772.6 56.2 %copy-start.3 = (f32[8,4096]{1,0:T(8,128)S(1)}, f32[8,4096]{1,0:T(8,128)}, u32[]{:S(2)}) copy-start(f32[8,4096]{1,0:T(8,128)} %get-tuple-element.171) | copy-start | bytes 393220
  2772.7 56.2 %copy-start.5 = (f32[8,4096]{1,0:T(8,128)S(1)}, f32[8,4096]{1,0:T(8,128)}, u32[]{:S(2)}) copy-start(f32[8,4096]{1,0:T(8,128)} %get-tuple-element.172) | copy-start | bytes 393220
  2772.7 56.2 %copy-start.7 = (f32[8,4096]{1,0:T(8,128)S(1)}, f32[8,4096]{1,0:T(8,128)}, u32[]{:S(2)}) copy-start(f32[8,4096]{1,0:T(8,128)} %get-tuple-element.173) | copy-start | bytes 393220
  2772.7 61.8 %copy-start.14 = (f32[2048]{0:T(1024)S(1)}, f32[2048]{0:T(1024)}, u32[]{:S(2)}) copy-start(f32[2048]{0:T(1024)} %convert_reduce_fusion) | copy-start | bytes 24580
  2829.9 4.5 collective-permute-start.13
  2834.3 71.3 %collective-permute-start.16 = (bf16[768,2048]{1,0:T(8,128)(2,1)}, bf16[768,2048]{1,0:T(8,128)(2,1)}, u32[]{:S(2)}, u32[]{:S(2)}) collective-permute-start(bf16[768,2048]{1,0:T(8,128)(2,1)} %get-tuple-element.149), channel_id=1, source_target_pairs={{0,2},{2,0},{1,3},{3,1},{4,6},{6,4},{5,7},{7,5}} | collective-permute-start | bytes 9437192 | tf_op jit(solution)/shard_map/ppermute | solution.py:634
  2834.5 1.3 collective-permute-start.14
  2834.6 71.1 %copy-start = (bf16[256,3072]{1,0:T(8,128)(2,1)S(1)}, bf16[256,3072]{1,0:T(8,128)(2,1)}, u32[]{:S(2)}) copy-start(bf16[256,3072]{1,0:T(8,128)(2,1)} %add_convert_fusion.9.half_ref) | copy-start | bytes 4718596
  2835.8 277.8 %collective-permute-start.21 = (bf16[384,2048]{1,0:T(8,128)(2,1)}, bf16[384,2048]{1,0:T(8,128)(2,1)S(1)}, u32[]{:S(2)}, u32[]{:S(2)}) collective-permute-start(bf16[384,2048]{1,0:T(8,128)(2,1)} %get-tuple-element.177), channel_id=1, source_target_pairs={{0,2},{2,0},{1,3},{3,1},{4,6},{6,4},{5,7},{7,5}} | collective-permute-start | bytes 4718600 | tf_op jit(solution)/shard_map/ppermute | solution.py:634
  2837.7 275.9 %collective-permute-start.18 = (bf16[384,2048]{1,0:T(8,128)(2,1)}, bf16[384,2048]{1,0:T(8,128)(2,1)}, u32[]{:S(2)}, u32[]{:S(2)}) collective-permute-start(bf16[384,2048]{1,0:T(8,128)(2,1)} %get-tuple-element.159), channel_id=1, source_target_pairs={{0,2},{2,0},{1,3},{3,1},{4,6},{6,4},{5,7},{7,5}} | collective-permute-start | bytes 4718600 | tf_op jit(solution)/shard_map/ppermute | solution.py:634
  2905.6 213.1 %collective-permute-start.22 = (bf16[256,3072]{1,0:T(8,128)(2,1)S(1)}, bf16[256,3072]{1,0:T(8,128)(2,1)}, u32[]{:S(2)}, u32[]{:S(2)}) collective-permute-start(bf16[256,3072]{1,0:T(8,128)(2,1)S(1)} %copy-done), channel_id=1, source_target_pairs={{0,4},{4,0},{1,5},{5,1},{2,6},{6,2},{3,7},{7,3}} | collective-permute-start | bytes 4718600 | tf_op jit(solution)/shard_map/ppermute | solution.py:634
  2915.1 202.5 %collective-permute-start.23 = (f32[96,128]{1,0:T(8,128)S(1)}, f32[96,128]{1,0:T(8,128)S(1)}, u32[]{:S(2)}, u32[]{:S(2)}) collective-permute-start(f32[96,128]{1,0:T(8,128)S(1)} %fusion.4), channel_id=1, source_target_pairs={{0,4},{4,0},{1,5},{5,1},{2,6},{6,2},{3,7},{7,3}} | collective-permute-start | bytes 147464 | tf_op jit(solution)/shard_map/ppermute | solution.py:634
Sparse Core Ops, SparseCore 0:
  9.5 30.0 all-gather.5
  71.3 72.6 all-gather.7
  450.9 153.2 all-gather.9
  722.9 152.9 all-gather.11
  877.2 103.1 all-gather.13
  1227.6 22.0 reduce-scatter.12
  1400.8 22.0 reduce-scatter.14
  1425.5 177.6 reduce-scatter.16
  1605.5 32.6 reduce-scatter.20
  1792.3 234.8 reduce-scatter.18
  2029.5 32.5 reduce-scatter.22
